TPU v7x, 256 devices: a whole 4x4x8 slice. The times are simulated.
256 devices in a mesh: gz: 32 (over y_lo, z, core), xy: 8 (over x, y_hi).
Axes of the slice: x: 4, y: 4 (y_hi: 2, y_lo: 2; y = y_hi * 2 + y_lo), z: 8, core: 2. Of those that a mesh axis runs over, the one named last changes fastest.
Arguments:
- fields: float32 [2, 2048, 256, 256], P(None, 'gz', 'xy'), may hold values from -64 to 64, as said below
- threshold: float32 [2], replicated, may hold values from 0.1 to 0.6
Outputs:
- detail_one: float32 [2, 1024, 256, 256], P(None, 'gz', 'xy')
- detail_two: float32 [2, 512, 256, 256], P(None, 'gz', 'xy')
- detail_three: float32 [2, 256, 256, 256], P(None, 'gz', 'xy')
- detail_four: float32 [2, 128, 256, 256], P(None, 'gz', 'xy')
- detail_five: float32 [2, 64, 256, 256], P(None, 'gz', 'xy')
- coarse: float32 [2, 64, 256, 256], P(None, 'gz', 'xy')
- band_energy: float32 [2, 6], replicated
Inputs may be any that keep to these rules, and one draw needn't show every extreme that they name: Finite values; the spread of the fields varies over the grid.
All inputs are finite; a program needn't handle non-finite values.
Results may differ from a plain program's by a relative error of at most 0.00002.
Values sent between devices are 32-bit elements; how exact they have to be, the bound alone decides.
No kernel may reach another device: no remote copies, remote signals or barrier semaphores. Data moves between devices by JAX's collectives and lax.ppermute only.
A program may use at most 64 MiB of HBM per device.

v0:
```python
import jax
import jax.numpy as jnp
from jax import lax
from jax.sharding import Mesh
from jax.sharding import PartitionSpec as P

GZ = ("gz_0", "gz_1", "gz_2")
GZ_XY = ("gz_0", "gz_1", "gz_2", "xy_0", "xy_1")
XY = ("xy_0", "xy_1")


ALPHA = -1.586134342059924
BETA = -0.052980118572961
GAMMA = 0.882911075530934
DELTA = 0.443506852043971
KAPPA = 1.230174104914001
SQRT_TWO = 1.4142135623730951


def extended_2(block, sides, width):
    for axis, dim in sides:
        count = lax.axis_size(axis)
        forward = [(i, i + 1) for i in range(count - 1)]
        backward = [(target, source) for source, target in forward]
        low = lax.ppermute(
            lax.slice_in_dim(block, block.shape[dim] - width, None, axis=dim), axis, forward
        )
        high = lax.ppermute(lax.slice_in_dim(block, 0, width, axis=dim), axis, backward)
        block = jnp.concatenate([low, block, high], axis=dim)
    return block


def by_axis(value, axes):
    for axis in axes:
        value = lax.psum(value, axis)
    return value


def right_of(evens):
    return jnp.concatenate([evens[:, 1:], evens[:, -1:]], axis=1)


def left_of(odds):
    return jnp.concatenate([odds[:, :1], odds[:, :-1]], axis=1)


def one_level(values):
    half = values.shape[1] // 2
    paired = values.reshape(values.shape[0], half, 2, values.shape[2], values.shape[3])
    evens = paired[:, :, 0]
    odds = paired[:, :, 1]
    odds = odds + ALPHA * (evens + right_of(evens))
    evens = evens + BETA * (left_of(odds) + odds)
    odds = odds + GAMMA * (evens + right_of(evens))
    evens = evens + DELTA * (left_of(odds) + odds)
    return (evens * (SQRT_TWO / KAPPA), odds * (KAPPA / SQRT_TWO))


def shrink(band, limit):
    return band - jnp.clip(band, -limit, limit)


def rim_level(values):
    length = values.shape[1]
    extended = extended_2(values, ((GZ, 1),), 4)
    position = lax.axis_index(GZ)
    count = lax.axis_size(GZ)
    lower = jnp.where(position == 0, extended[:, 8:4:-1], extended[:, 0:4])
    upper = jnp.where(
        position == count - 1,
        extended[:, length + 2 : length - 2 : -1],
        extended[:, length + 4 : length + 8],
    )
    extended = jnp.concatenate([lower, extended[:, 4 : length + 4], upper], axis=1)
    approx, detail = one_level(extended)
    pairs = length // 2
    return (approx[:, 2 : 2 + pairs], detail[:, 2 : 2 + pairs])


def local(fields, threshold):
    limit = threshold.reshape(2, 1, 1, 1)
    bands = []
    approx = fields
    for level in range(5):
        approx, detail = rim_level(approx)
        bands.append(shrink(detail, limit))
    bands.append(shrink(approx, limit))
    partial_sums = jnp.stack([jnp.sum(band * band, axis=(1, 2, 3)) for band in bands], axis=1)
    totals = by_axis(partial_sums, GZ_XY)
    devices_all = lax.axis_size(GZ) * lax.axis_size(XY)
    cells = jnp.array(
        [band.shape[1] * band.shape[2] * band.shape[3] * devices_all for band in bands], jnp.float32
    )
    energy = totals / cells[None, :]
    return (bands[0], bands[1], bands[2], bands[3], bands[4], bands[5], energy)


def solution(mesh):
    torus = Mesh(mesh.devices.reshape(2, 8, 2, 4, 2), ("gz_0", "gz_1", "gz_2", "xy_0", "xy_1"))
    in_specs = (P(None, GZ, XY, None), P())
    out_specs = (
        P(None, GZ, XY, None),
        P(None, GZ, XY, None),
        P(None, GZ, XY, None),
        P(None, GZ, XY, None),
        P(None, GZ, XY, None),
        P(None, GZ, XY, None),
        P(),
    )
    return jax.shard_map(local, mesh=torus, in_specs=in_specs, out_specs=out_specs, check_vma=False)
```

profile of v0, /device:TPU:56, one launch (start us, length us, event | category | flops | bytes accessed | tf_op | source)
XLA Modules:
  0.0 124.1 jit_solution(10196596703482064531)
XLA Ops:
  0.6 1.3 %fusion.45 = (f32[2,4,32,256]{3,2,1,0:T(8,128)S(1)}, f32[2,4,32,256]{3,2,1,0:T(8,128)S(1)}, f32[2,4,32,256]{3,2,1,0:T(8,128)S(1)}, f32[2,4,32,256]{3,2,1,0:T(8,128)S(1)}) fusion(f32[2,64,32,256]{3,2,1,0:T(8,128)} %param.3), kind=kLoop, calls=%fused_computation.110 | loop fusion | bytes 2097152 | tf_op jit(solution)/shard_map/slice | solution.py:68
  1.9 1.9 %collective-permute-start = (f32[2,4,32,256]{3,2,1,0:T(8,128)S(1)}, f32[2,4,32,256]{3,2,1,0:T(8,128)S(1)}, u32[]{:S(2)}, u32[]{:S(2)}) collective-permute-start(f32[2,4,32,256]{3,2,1,0:T(8,128)S(1)} %get-tuple-element.42), channel_id=1, source_target_pairs={{0,8},{8,16},{16,24},{24,32},{32,40},{40,48},{48,56},{56,64},{64,7... | collective-permute-start | bytes 786440 | tf_op jit(solution)/shard_map/ppermute | solution.py:25
  3.8 3.6 %collective-permute-start.1 = (f32[2,4,32,256]{3,2,1,0:T(8,128)S(1)}, f32[2,4,32,256]{3,2,1,0:T(8,128)S(1)}, u32[]{:S(2)}, u32[]{:S(2)}) collective-permute-start(f32[2,4,32,256]{3,2,1,0:T(8,128)S(1)} %get-tuple-element.43), channel_id=1, source_target_pairs={{8,0},{16,8},{24,16},{32,24},{40,32},{48,40},{56,48},{64,56},{72,6... | collective-permute-start | bytes 786440 | tf_op jit(solution)/shard_map/ppermute | solution.py:28
  7.5 2.1 %collective-permute-done = f32[2,4,32,256]{3,2,1,0:T(8,128)S(1)} collective-permute-done((f32[2,4,32,256]{3,2,1,0:T(8,128)S(1)}, f32[2,4,32,256]{3,2,1,0:T(8,128)S(1)}, u32[]{:S(2)}, u32[]{:S(2)}) %collective-permute-start) | collective-permute-done | bytes 262176 | tf_op jit(solution)/shard_map/ppermute | solution.py:25
  9.6 1.7 %collective-permute-done.1 = f32[2,4,32,256]{3,2,1,0:T(8,128)S(1)} collective-permute-done((f32[2,4,32,256]{3,2,1,0:T(8,128)S(1)}, f32[2,4,32,256]{3,2,1,0:T(8,128)S(1)}, u32[]{:S(2)}, u32[]{:S(2)}) %collective-permute-start.1) | collective-permute-done | bytes 262176 | tf_op jit(solution)/shard_map/ppermute | solution.py:28
  11.4 2.6 %pad_maximum_fusion = f32[2,72,32,256]{3,2,1,0:T(8,128)S(1)} fusion(f32[2,4,32,256]{3,2,1,0:T(8,128)S(1)} %reverse_select_fusion.8, f32[2,64,32,256]{3,2,1,0:T(8,128)} %param.3, f32[2,4,32,256]{3,2,1,0:T(8,128)S(1)} %reverse_select_fusion.9), kind=kLoop, calls=%fused_computation | loop fusion | flops 2359296 | bytes 9437184 | tf_op jit(solution)/shard_map/concatenate | solution.py:74
  14.0 0.3 slice_bitcast_fusion
  14.3 0.2 slice.328
  14.5 0.8 fusion
  15.3 0.3 slice.331
  15.6 0.8 fusion.3
  16.4 0.3 slice.332
  16.6 1.0 fusion.5
  17.7 0.3 slice.336
  18.0 1.1 fusion.8
  19.0 0.1 fusion.46
  19.1 4.1 %collective-permute-start.2 = (f32[2,4,32,256]{3,2,1,0:T(8,128)S(1)}, f32[2,4,32,256]{3,2,1,0:T(8,128)S(1)}, u32[]{:S(2)}, u32[]{:S(2)}) collective-permute-start(f32[2,4,32,256]{3,2,1,0:T(8,128)S(1)} %get-tuple-element.47), channel_id=1, source_target_pairs={{0,8},{8,16},{16,24},{24,32},{32,40},{40,48},{48,56},{56,64},{64,7... | collective-permute-start | bytes 786440 | tf_op jit(solution)/shard_map/ppermute | solution.py:25
  23.3 1.9 %collective-permute-start.3 = (f32[2,4,32,256]{3,2,1,0:T(8,128)S(1)}, f32[2,4,32,256]{3,2,1,0:T(8,128)S(1)}, u32[]{:S(2)}, u32[]{:S(2)}) collective-permute-start(f32[2,4,32,256]{3,2,1,0:T(8,128)S(1)} %get-tuple-element.45), channel_id=1, source_target_pairs={{8,0},{16,8},{24,16},{32,24},{40,32},{48,40},{56,48},{64,56},{72,6... | collective-permute-start | bytes 786440 | tf_op jit(solution)/shard_map/ppermute | solution.py:28
  25.2 0.1 slice.339
  25.3 1.7 %collective-permute-done.2 = f32[2,4,32,256]{3,2,1,0:T(8,128)S(1)} collective-permute-done((f32[2,4,32,256]{3,2,1,0:T(8,128)S(1)}, f32[2,4,32,256]{3,2,1,0:T(8,128)S(1)}, u32[]{:S(2)}, u32[]{:S(2)}) %collective-permute-start.2) | collective-permute-done | bytes 262176 | tf_op jit(solution)/shard_map/ppermute | solution.py:25
  27.1 2.0 %collective-permute-done.3 = f32[2,4,32,256]{3,2,1,0:T(8,128)S(1)} collective-permute-done((f32[2,4,32,256]{3,2,1,0:T(8,128)S(1)}, f32[2,4,32,256]{3,2,1,0:T(8,128)S(1)}, u32[]{:S(2)}, u32[]{:S(2)}) %collective-permute-start.3) | collective-permute-done | bytes 262176 | tf_op jit(solution)/shard_map/ppermute | solution.py:28
  29.1 0.3 pad_maximum_fusion.1
  29.4 0.1 slice_bitcast_fusion.2
  29.7 0.4 fusion.9
  30.1 0.1 slice.347
  30.2 0.4 fusion.12
  30.6 0.1 slice.348
  30.8 0.4 fusion.14
  31.2 0.1 slice.352
  31.3 0.5 fusion.17
  31.8 0.1 fusion.47
  31.9 4.1 %collective-permute-start.4 = (f32[2,4,32,256]{3,2,1,0:T(8,128)S(1)}, f32[2,4,32,256]{3,2,1,0:T(8,128)S(1)}, u32[]{:S(2)}, u32[]{:S(2)}) collective-permute-start(f32[2,4,32,256]{3,2,1,0:T(8,128)S(1)} %get-tuple-element.51), channel_id=1, source_target_pairs={{0,8},{8,16},{16,24},{24,32},{32,40},{40,48},{48,56},{56,64},{64,7... | collective-permute-start | bytes 786440 | tf_op jit(solution)/shard_map/ppermute | solution.py:25
  36.0 1.9 %collective-permute-start.5 = (f32[2,4,32,256]{3,2,1,0:T(8,128)S(1)}, f32[2,4,32,256]{3,2,1,0:T(8,128)S(1)}, u32[]{:S(2)}, u32[]{:S(2)}) collective-permute-start(f32[2,4,32,256]{3,2,1,0:T(8,128)S(1)} %get-tuple-element.49), channel_id=1, source_target_pairs={{8,0},{16,8},{24,16},{32,24},{40,32},{48,40},{56,48},{64,56},{72,6... | collective-permute-start | bytes 786440 | tf_op jit(solution)/shard_map/ppermute | solution.py:28
  38.1 2.0 %collective-permute-done.4 = f32[2,4,32,256]{3,2,1,0:T(8,128)S(1)} collective-permute-done((f32[2,4,32,256]{3,2,1,0:T(8,128)S(1)}, f32[2,4,32,256]{3,2,1,0:T(8,128)S(1)}, u32[]{:S(2)}, u32[]{:S(2)}) %collective-permute-start.4) | collective-permute-done | bytes 262176 | tf_op jit(solution)/shard_map/ppermute | solution.py:25
  40.1 1.7 %collective-permute-done.5 = f32[2,4,32,256]{3,2,1,0:T(8,128)S(1)} collective-permute-done((f32[2,4,32,256]{3,2,1,0:T(8,128)S(1)}, f32[2,4,32,256]{3,2,1,0:T(8,128)S(1)}, u32[]{:S(2)}, u32[]{:S(2)}) %collective-permute-start.5) | collective-permute-done | bytes 262176 | tf_op jit(solution)/shard_map/ppermute | solution.py:28
  41.9 0.2 pad_maximum_fusion.2
  42.2 0.2 fusion.18
  42.5 0.2 fusion.21
  42.7 0.2 fusion.23
  43.0 0.2 fusion.26
  43.2 0.9 fusion.48
  44.1 6.5 %collective-permute-start.6 = (f32[2,4,32,256]{3,2,1,0:T(8,128)}, f32[2,4,32,256]{3,2,1,0:T(8,128)}, u32[]{:S(2)}, u32[]{:S(2)}) collective-permute-start(f32[2,4,32,256]{3,2,1,0:T(8,128)} %get-tuple-element.55), channel_id=1, source_target_pairs={{0,8},{8,16},{16,24},{24,32},{32,40},{40,48},{48,56},{56,64},{64,7... | collective-permute-start | bytes 786440 | tf_op jit(solution)/shard_map/ppermute | solution.py:25
  50.6 1.9 %collective-permute-start.7 = (f32[2,4,32,256]{3,2,1,0:T(8,128)}, f32[2,4,32,256]{3,2,1,0:T(8,128)}, u32[]{:S(2)}, u32[]{:S(2)}) collective-permute-start(f32[2,4,32,256]{3,2,1,0:T(8,128)} %get-tuple-element.53), channel_id=1, source_target_pairs={{8,0},{16,8},{24,16},{32,24},{40,32},{48,40},{56,48},{64,56},{72,6... | collective-permute-start | bytes 786440 | tf_op jit(solution)/shard_map/ppermute | solution.py:28
  52.6 1.8 %multiply_reduce_fusion = (f32[2]{0:T(128)S(1)}, f32[2,32,32,256]{3,2,1,0:T(8,128)}) fusion(f32[2]{0:T(128)S(1)} %neg.3, f32[2]{0:T(128)S(1)} %copy-done, f32[2,36,32,256]{3,2,1,0:T(8,128)S(1)} %fusion.5), kind=kLoop, calls=%fused_computation.18 | loop fusion | flops 3145726 | bytes 4194328 | tf_op jit(solution)/shard_map/reduce_sum | solution.py:88
  54.5 1.0 reverse_select_fusion.3
  55.5 1.2 collective-permute-done.7
  56.8 1.0 reverse_select_fusion.2
  57.8 0.1 pad_maximum_fusion.3
  58.0 0.1 fusion.27
  58.1 0.1 fusion.30
  58.3 0.1 fusion.32
  58.5 0.9 multiply_reduce_fusion.3
  59.4 4.1 %collective-permute-start.8 = (f32[2,4,32,256]{3,2,1,0:T(8,128)S(1)}, f32[2,4,32,256]{3,2,1,0:T(8,128)S(1)}, u32[]{:S(2)}, u32[]{:S(2)}) collective-permute-start(f32[2,4,32,256]{3,2,1,0:T(8,128)S(1)} %get-tuple-element.56), channel_id=1, source_target_pairs={{8,0},{16,8},{24,16},{32,24},{40,32},{48,40},{56,48},{64,56},{72,6... | collective-permute-start | bytes 786440 | tf_op jit(solution)/shard_map/ppermute | solution.py:28
  63.5 1.3 %multiply_reduce_fusion.1 = (f32[2]{0:T(128)S(1)}, f32[2,16,32,256]{3,2,1,0:T(8,128)}) fusion(f32[2]{0:T(128)S(1)} %neg.3, f32[2]{0:T(128)S(1)} %copy-done, f32[2,20,32,256]{3,2,1,0:T(8,128)S(1)} %fusion.14), kind=kLoop, calls=%fused_computation.38 | loop fusion | flops 1572862 | bytes 2097176 | tf_op jit(solution)/shard_map/reduce_sum | solution.py:88
  64.8 2.8 %collective-permute-start.9 = (f32[2,4,32,256]{3,2,1,0:T(8,128)S(1)}, f32[2,4,32,256]{3,2,1,0:T(8,128)S(1)}, u32[]{:S(2)}, u32[]{:S(2)}) collective-permute-start(f32[2,4,32,256]{3,2,1,0:T(8,128)S(1)} %get-tuple-element.56), channel_id=1, source_target_pairs={{0,8},{8,16},{16,24},{24,32},{32,40},{40,48},{48,56},{56,64},{64,7... | collective-permute-start | bytes 786440 | tf_op jit(solution)/shard_map/ppermute | solution.py:25
  67.7 1.0 multiply_reduce_fusion.2
  68.8 6.7 %collective-permute-done.9 = f32[2,4,32,256]{3,2,1,0:T(8,128)S(1)} collective-permute-done((f32[2,4,32,256]{3,2,1,0:T(8,128)S(1)}, f32[2,4,32,256]{3,2,1,0:T(8,128)S(1)}, u32[]{:S(2)}, u32[]{:S(2)}) %collective-permute-start.9) | collective-permute-done | bytes 262176 | tf_op jit(solution)/shard_map/ppermute | solution.py:25
  76.3 0.8 multiply_reduce_fusion.4
  77.4 4.9 %psum.35 = f32[2,6]{1,0:T(2,128)S(1)} all-reduce(f32[2,6]{1,0:T(2,128)S(1)} %stack.27), channel_id=1, replica_groups=mesh['gz_0'=2,'gz_1'=8,'gz_2'=2,'xy_0'=4,'xy_1'=2] {'gz_0'}, use_global_device_ids=true, to_apply=%region_6.7 | all-reduce | flops 12 | bytes 96 | tf_op jit(solution)/shard_map/psum | solution.py:35
  82.3 21.9 %psum.36 = f32[2,6]{1,0:T(2,128)S(1)} all-reduce(f32[2,6]{1,0:T(2,128)S(1)} %psum.35), channel_id=1, replica_groups=mesh['gz_0'=2,'gz_1'=8,'gz_2'=2,'xy_0'=4,'xy_1'=2] {'gz_1'}, use_global_device_ids=true, to_apply=%region_7.8 | all-reduce | flops 12 | bytes 96 | tf_op jit(solution)/shard_map/psum | solution.py:35
  104.2 2.5 %psum.37 = f32[2,6]{1,0:T(2,128)S(1)} all-reduce(f32[2,6]{1,0:T(2,128)S(1)} %psum.36), channel_id=1, replica_groups=mesh['gz_0'=2,'gz_1'=8,'gz_2'=2,'xy_0'=4,'xy_1'=2] {'gz_2'}, use_global_device_ids=true, to_apply=%region_8.9 | all-reduce | flops 12 | bytes 96 | tf_op jit(solution)/shard_map/psum | solution.py:35
  106.6 10.5 %psum.38 = f32[2,6]{1,0:T(2,128)S(1)} all-reduce(f32[2,6]{1,0:T(2,128)S(1)} %psum.37), channel_id=1, replica_groups=mesh['gz_0'=2,'gz_1'=8,'gz_2'=2,'xy_0'=4,'xy_1'=2] {'xy_0'}, use_global_device_ids=true, to_apply=%region_9.10 | all-reduce | flops 12 | bytes 96 | tf_op jit(solution)/shard_map/psum | solution.py:35
  117.1 6.4 %psum.39 = f32[2,6]{1,0:T(2,128)S(1)} all-reduce(f32[2,6]{1,0:T(2,128)S(1)} %psum.38), channel_id=1, replica_groups=mesh['gz_0'=2,'gz_1'=8,'gz_2'=2,'xy_0'=4,'xy_1'=2] {'xy_1'}, use_global_device_ids=true, to_apply=%region_10.11 | all-reduce | flops 12 | bytes 96 | tf_op jit(solution)/shard_map/psum | solution.py:35
  123.5 0.6 broadcast_multiply_fusion
  (65 shorter events, 2.2 us)
Async XLA Ops:
  1.9 7.7 %collective-permute-start = (f32[2,4,32,256]{3,2,1,0:T(8,128)S(1)}, f32[2,4,32,256]{3,2,1,0:T(8,128)S(1)}, u32[]{:S(2)}, u32[]{:S(2)}) collective-permute-start(f32[2,4,32,256]{3,2,1,0:T(8,128)S(1)} %get-tuple-element.42), channel_id=1, source_target_pairs={{0,8},{8,16},{16,24},{24,32},{32,40},{40,48},{48,56},{56,64},{64,7... | collective-permute-start | bytes 786440 | tf_op jit(solution)/shard_map/ppermute | solution.py:25
  3.8 7.5 %collective-permute-start.1 = (f32[2,4,32,256]{3,2,1,0:T(8,128)S(1)}, f32[2,4,32,256]{3,2,1,0:T(8,128)S(1)}, u32[]{:S(2)}, u32[]{:S(2)}) collective-permute-start(f32[2,4,32,256]{3,2,1,0:T(8,128)S(1)} %get-tuple-element.43), channel_id=1, source_target_pairs={{8,0},{16,8},{24,16},{32,24},{40,32},{48,40},{56,48},{64,56},{72,6... | collective-permute-start | bytes 786440 | tf_op jit(solution)/shard_map/ppermute | solution.py:28
  19.1 7.9 %collective-permute-start.2 = (f32[2,4,32,256]{3,2,1,0:T(8,128)S(1)}, f32[2,4,32,256]{3,2,1,0:T(8,128)S(1)}, u32[]{:S(2)}, u32[]{:S(2)}) collective-permute-start(f32[2,4,32,256]{3,2,1,0:T(8,128)S(1)} %get-tuple-element.47), channel_id=1, source_target_pairs={{0,8},{8,16},{16,24},{24,32},{32,40},{40,48},{48,56},{56,64},{64,7... | collective-permute-start | bytes 786440 | tf_op jit(solution)/shard_map/ppermute | solution.py:25
  23.3 5.8 %collective-permute-start.3 = (f32[2,4,32,256]{3,2,1,0:T(8,128)S(1)}, f32[2,4,32,256]{3,2,1,0:T(8,128)S(1)}, u32[]{:S(2)}, u32[]{:S(2)}) collective-permute-start(f32[2,4,32,256]{3,2,1,0:T(8,128)S(1)} %get-tuple-element.45), channel_id=1, source_target_pairs={{8,0},{16,8},{24,16},{32,24},{40,32},{48,40},{56,48},{64,56},{72,6... | collective-permute-start | bytes 786440 | tf_op jit(solution)/shard_map/ppermute | solution.py:28
  31.3 6.6 %copy-start = (f32[2]{0:T(128)S(1)}, f32[2]{0:T(128)}, u32[]{:S(2)}) copy-start(f32[2]{0:T(128)} %param.4) | copy-start | bytes 28
  31.9 8.2 %collective-permute-start.4 = (f32[2,4,32,256]{3,2,1,0:T(8,128)S(1)}, f32[2,4,32,256]{3,2,1,0:T(8,128)S(1)}, u32[]{:S(2)}, u32[]{:S(2)}) collective-permute-start(f32[2,4,32,256]{3,2,1,0:T(8,128)S(1)} %get-tuple-element.51), channel_id=1, source_target_pairs={{0,8},{8,16},{16,24},{24,32},{32,40},{40,48},{48,56},{56,64},{64,7... | collective-permute-start | bytes 786440 | tf_op jit(solution)/shard_map/ppermute | solution.py:25
  36.0 5.8 %collective-permute-start.5 = (f32[2,4,32,256]{3,2,1,0:T(8,128)S(1)}, f32[2,4,32,256]{3,2,1,0:T(8,128)S(1)}, u32[]{:S(2)}, u32[]{:S(2)}) collective-permute-start(f32[2,4,32,256]{3,2,1,0:T(8,128)S(1)} %get-tuple-element.49), channel_id=1, source_target_pairs={{8,0},{16,8},{24,16},{32,24},{40,32},{48,40},{56,48},{64,56},{72,6... | collective-permute-start | bytes 786440 | tf_op jit(solution)/shard_map/ppermute | solution.py:28
  44.1 10.4 %collective-permute-start.6 = (f32[2,4,32,256]{3,2,1,0:T(8,128)}, f32[2,4,32,256]{3,2,1,0:T(8,128)}, u32[]{:S(2)}, u32[]{:S(2)}) collective-permute-start(f32[2,4,32,256]{3,2,1,0:T(8,128)} %get-tuple-element.55), channel_id=1, source_target_pairs={{0,8},{8,16},{16,24},{24,32},{32,40},{40,48},{48,56},{56,64},{64,7... | collective-permute-start | bytes 786440 | tf_op jit(solution)/shard_map/ppermute | solution.py:25
  50.6 6.1 %collective-permute-start.7 = (f32[2,4,32,256]{3,2,1,0:T(8,128)}, f32[2,4,32,256]{3,2,1,0:T(8,128)}, u32[]{:S(2)}, u32[]{:S(2)}) collective-permute-start(f32[2,4,32,256]{3,2,1,0:T(8,128)} %get-tuple-element.53), channel_id=1, source_target_pairs={{8,0},{16,8},{24,16},{32,24},{40,32},{48,40},{56,48},{64,56},{72,6... | collective-permute-start | bytes 786440 | tf_op jit(solution)/shard_map/ppermute | solution.py:28
  59.4 9.5 %collective-permute-start.8 = (f32[2,4,32,256]{3,2,1,0:T(8,128)S(1)}, f32[2,4,32,256]{3,2,1,0:T(8,128)S(1)}, u32[]{:S(2)}, u32[]{:S(2)}) collective-permute-start(f32[2,4,32,256]{3,2,1,0:T(8,128)S(1)} %get-tuple-element.56), channel_id=1, source_target_pairs={{8,0},{16,8},{24,16},{32,24},{40,32},{48,40},{56,48},{64,56},{72,6... | collective-permute-start | bytes 786440 | tf_op jit(solution)/shard_map/ppermute | solution.py:28
  64.8 10.8 %collective-permute-start.9 = (f32[2,4,32,256]{3,2,1,0:T(8,128)S(1)}, f32[2,4,32,256]{3,2,1,0:T(8,128)S(1)}, u32[]{:S(2)}, u32[]{:S(2)}) collective-permute-start(f32[2,4,32,256]{3,2,1,0:T(8,128)S(1)} %get-tuple-element.56), channel_id=1, source_target_pairs={{0,8},{8,16},{16,24},{24,32},{32,40},{40,48},{48,56},{56,64},{64,7... | collective-permute-start | bytes 786440 | tf_op jit(solution)/shard_map/ppermute | solution.py:25
  76.1 47.5 %copy-start.1 = (f32[6]{0:T(128)S(1)}, f32[6]{0:T(128)}, u32[]{:S(2)}) copy-start(f32[6]{0:T(128)} %constant.7) | copy-start | bytes 76
where the time goes:
time: 125 us; the launch traced here: 124 us
  blocking collectives  46.2 us (37%)
  starting transfers between devices  33 us (26%)
  waiting for transfers between devices  19.2 us (15%)
  other arithmetic  18.6 us (15%)
  local copies, waits for them, and re-layouts  5.83 us (5%)
  between operations  1.35 us (1%)
    psum x5, blocking collectives, by_axis(): value = lax.psum(value, axis)  46.2 us
    ppermute x5, starting transfers between devices, extended_2(): lax.ppermute(lax.slice_in_dim(block, block.shape[dim] - width, None, axis...  19.5 us
    ppermute x5, starting transfers between devices, extended_2(): lax.ppermute(lax.slice_in_dim(block, 0, width, axis=dim), axis, backward)  13.5 us
    ppermute x5, waiting for transfers between devices, extended_2(): lax.ppermute(lax.slice_in_dim(block, block.shape[dim] - width, None, axis...  12.5 us
    ppermute x5, waiting for transfers between devices, extended_2(): lax.ppermute(lax.slice_in_dim(block, 0, width, axis=dim), axis, backward)  6.66 us
    reduce_sum x5, other arithmetic, local(): jnp.sum(band * band, axis=(1, 2, 3))  5.73 us
    concatenate x5, other arithmetic, rim_level(): jnp.concatenate([lower, extended[:, 4:length + 4], upper], axis=1)  3.26 us
  transfers between devices with their start and end apart: 10, of which 8 were waited for; matrix products, arithmetic and copies ran while one was open for 5% of the time, Pallas kernels for 0%

commit v1 on v0

v1 whole, which is shorter than its diff:
```python
import functools

import jax
import jax.numpy as jnp
import numpy as np
from jax import lax
from jax.experimental import pallas as pl
from jax.experimental.pallas import tpu as pltpu
from jax.sharding import PartitionSpec as P

ALPHA = -1.586134342059924
BETA = -0.052980118572961
GAMMA = 0.882911075530934
DELTA = 0.443506852043971
KAPPA = 1.230174104914001
SQRT_TWO = 1.4142135623730951
LOW = SQRT_TWO / KAPPA
HIGH = KAPPA / SQRT_TWO
FAR = 4
EDGE_LO = (1, 2, 3, 3)
EDGE_HI = (2, 3, 3, 3)


class Level:
    def __init__(self, n, left, right, emit_d, emit_s):
        self.n, self.left, self.right, self.emit_d, self.emit_s = n, left, right, emit_d, emit_s
        self.s, self.d, self.d1, self.s2, self.d3 = [], [], [], [], []

    def push(self, x):
        if len(self.s) == len(self.d):
            self.s.append(x)
            i = len(self.s) - 2
            if i >= 0:
                self.add(self.d[i] + ALPHA * (self.s[i] + self.s[i + 1]))
        else:
            self.d.append(x)
            if len(self.d) == self.n:
                self.finish()

    def add(self, v):
        self.d1.append(v)
        i = len(self.d1) - 1
        if i == 0:
            self.p = ALPHA * self.s[0]
            self.c = self.s[0] + BETA * v
            return
        if i == 1:
            a, b = self.left(self)
            below = a + self.p
            self.s2.append(self.c + BETA * below)
            self.d3m = below + GAMMA * ((b + BETA * below) + self.s2[0])
        if i == self.n - 1:
            self.s2.append(self.b + BETA * v)
        else:
            self.s2.append(self.s[i] + BETA * (self.d1[i - 1] + v))
        self.third(i - 1, self.s2[i])

    def third(self, j, above):
        self.d3.append(self.d1[j] + GAMMA * (self.s2[j] + above))
        self.emit_d(j, self.d3[j])
        before = self.d3[j - 1] if j else self.d3m
        self.emit_s(j, self.s2[j] + DELTA * (before + self.d3[j]))

    def finish(self):
        n = self.n
        self.a = self.d[n - 1] + ALPHA * self.s[n - 1]
        self.b = self.s[n - 1] + BETA * self.d1[n - 2]
        p, c = self.right(self)
        v = self.a + p
        self.add(v)
        self.third(n - 1, c + BETA * v)


def low_end(level):
    return level.d[0] + ALPHA * level.s[1], level.s[1] + BETA * level.d1[1]


def high_end(level):
    return ALPHA * level.s[-1], level.b


@functools.cache
def response(side):
    width = 2 * FAR
    zero, unit = np.zeros(width), np.eye(width)
    back, details, u = [], [], [zero] * 512
    for l in range(FAR):
        n = len(u) // 2
        state, none = (unit[2 * l], unit[2 * l + 1]), (zero, zero)
        d, s = [None] * n, [None] * n
        level = Level(
            n,
            lambda _: state if side == "lo" else none,
            lambda _: state if side == "hi" else none,
            d.__setitem__,
            s.__setitem__,
        )
        for x in u:
            level.push(x)
        back.append((level.p, level.c) if side == "lo" else (level.a, level.b))
        details.append(d[:6] if side == "lo" else d[::-1][:6])
        last = s[:6] if side == "lo" else s[::-1][:6]
        u = s
    return back, details, last


def combine(row, states):
    total = None
    for k, x in zip(row, states):
        if k != 0.0:
            term = float(k) * x
            total = term if total is None else total + term
    return total


def where_am_i():
    z = lax.axis_index("gz")
    return lax.rem(z, 2) == 1, z == 0, z == lax.axis_size("gz") - 1


def cell(i):
    return i // 8, pl.ds(pl.multiple_of(lax.rem(i // 2, 4) * 8, 8), 8), pl.ds(pl.multiple_of(lax.rem(i, 2) * 128, 128), 128)


def transform(x_hbm, outer, inner, d1, d2, d3, d4, s4, x_vmem, sem):
    upper, lowest, highest = where_am_i()

    def fetch(j):
        rows = pl.ds(pl.multiple_of(lax.rem(j, 4) * 8, 8), 8)
        at = (j // 4, slice(None), rows)
        return pltpu.make_async_copy(x_hbm.at[at], x_vmem.at[at], sem.at[j])

    for j in range(8):
        fetch(j).start()
    from_above, from_below = response("hi")[0], response("lo")[0]
    bands = (d1, d2, d3, d4)

    def tile(i, _):
        @pl.when(lax.rem(i, 2) == 0)
        def _():
            fetch(i // 2).wait()

        f, rows, cols = cell(i)
        down, up, levels = [], [], []

        def left(l):
            def state(level):
                down.extend((level.p, level.c))
                end = low_end(level)
                if l == 0:
                    return tuple(jnp.where(lowest, e, 0.0) for e in end)
                return tuple(jnp.where(lowest, e, combine(r, down)) for e, r in zip(end, from_above[l]))

            return state

        def right(l):
            def state(level):
                up.extend((level.a, level.b))
                end = high_end(level)
                if l == 0:
                    return tuple(jnp.where(highest, e, 0.0) for e in end)
                return tuple(jnp.where(highest, e, combine(r, up)) for e, r in zip(end, from_below[l]))

            return state

        def keep(l):
            def store(j, v):
                bands[l][f, j, rows, cols] = v

            return store

        def pass_on(l):
            def store(j, v):
                if l == FAR - 1:
                    s4[f, j, rows, cols] = v
                else:
                    levels[l + 1].push(v)

            return store

        for l in range(FAR):
            levels.append(Level(32 >> l, left(l), right(l), keep(l), pass_on(l)))
        for z in range(64):
            levels[0].push(x_vmem[f, z, rows, cols])
        for k in range(2 * FAR):
            outer[f, k, rows, cols] = jnp.where(upper, up[k], down[k])
            inner[f, k, rows, cols] = jnp.where(upper, down[k], up[k])
        return 0

    lax.fori_loop(0, 16, tile, 0)


def shrink(v, scale, limit):
    v = v * scale
    return v - jnp.clip(v, -limit, limit)


def interiors(limits, d1, d2, d3, o1, o2, o3, sums, b1, b2, b3, sem):
    copies = []
    for f in range(2):
        limit = limits[f]
        for l, (raw, buf, out) in enumerate(((d1, b1, o1), (d2, b2, o2), (d3, b3, o3))):
            n = 32 >> l
            lo, hi = EDGE_LO[l], n - EDGE_HI[l]

            def layer(z, acc, raw=raw, buf=buf, l=l):
                v = shrink(raw[f, z], LOW**l * HIGH, limit)
                buf[f, z] = v
                return acc + v * v

            acc = lax.fori_loop(lo, hi, layer, jnp.zeros((32, 256), jnp.float32), unroll=True)
            acc = acc.reshape(4, 8, 256).sum(axis=0)
            sums[f, l] = acc[:, :128] + acc[:, 128:]
            at = (f, pl.ds(lo, hi - lo))
            copy = pltpu.make_async_copy(buf.at[at], out.at[at], sem.at[3 * f + l])
            copy.start()
            copies.append(copy)
    for copy in copies:
        copy.wait()


def arrived(outer, inner, f, rows, cols, upper, lowest, highest, width):
    below, above = [], []
    for k in range(width):
        o, i = outer[f, k, rows, cols], inner[f, k, rows, cols]
        below.append(jnp.where(lowest, 0.0, jnp.where(upper, i, o)))
        above.append(jnp.where(highest, 0.0, jnp.where(upper, o, i)))
    return below, above


def corrected(v, row_lo, below, row_hi, above):
    for term in (combine(row_lo, below), combine(row_hi, above)):
        if term is not None:
            v = v + term
    return v


def approximation(outer, inner, s4, outer5, inner5, full):
    upper, lowest, highest = where_am_i()
    last_lo, last_hi = response("lo")[2], response("hi")[2]

    def tile(i, _):
        f, rows, cols = cell(i)
        below, above = arrived(outer, inner, f, rows, cols, upper, lowest, highest, 2 * FAR)
        u = [corrected(s4[f, j, rows, cols], last_lo[j], below, last_hi[3 - j], above) for j in range(4)]
        for j in range(4):
            full[f, j, rows, cols] = u[j]
        middle = u[1] + ALPHA * (u[0] + u[2])
        down = (ALPHA * u[0], u[0] + BETA * middle)
        up = (u[3] + ALPHA * u[2], u[2] + BETA * middle)
        for k in range(2):
            outer5[f, k, rows, cols] = jnp.where(upper, up[k], down[k])
            inner5[f, k, rows, cols] = jnp.where(upper, down[k], up[k])
        return 0

    lax.fori_loop(0, 16, tile, 0)


def edges(limits, outer, inner, d1, d2, d3, d4, o1_in, o2_in, o3_in, o1, o2, o3, o4, sums, b1, b2, b3, b4, sem):
    upper, lowest, highest = where_am_i()
    det_lo, det_hi = response("lo")[1], response("hi")[1]
    raws, bufs, outs = (d1, d2, d3, d4), (b1, b2, b3, b4), (o1, o2, o3, o4)
    spans = [sorted({*range(EDGE_LO[l]), *range((32 >> l) - EDGE_HI[l], 32 >> l)}) for l in range(FAR)]
    sums[...] = jnp.zeros(sums.shape, jnp.float32)

    def tile(i, _):
        f, rows, cols = cell(i)
        limit = limits[f]
        below, above = arrived(outer, inner, f, rows, cols, upper, lowest, highest, 2 * FAR)
        for l in range(FAR):
            n, acc = 32 >> l, None
            for k, j in enumerate(spans[l]):
                row_lo = det_lo[l][j] if j < 6 else ()
                row_hi = det_hi[l][n - 1 - j] if n - 1 - j < 6 else ()
                v = corrected(raws[l][f, j, rows, cols], row_lo, below, row_hi, above)
                v = shrink(v, LOW**l * HIGH, limit)
                bufs[l][f, k, rows, cols] = v
                acc = v * v if acc is None else acc + v * v
            sums[f, l] += acc
        return 0

    lax.fori_loop(0, 16, tile, 0)
    copies = []
    for f in range(2):
        for l in range(FAR):
            n, lo = 32 >> l, EDGE_LO[l]
            pieces = [(0, lo, 0), (lo, len(spans[l]) - lo, n - EDGE_HI[l])] if l < 3 else [(0, n, 0)]
            for start, size, to in pieces:
                copy = pltpu.make_async_copy(
                    bufs[l].at[f, pl.ds(start, size)], outs[l].at[f, pl.ds(to, size)], sem.at[len(copies)]
                )
                copy.start()
                copies.append(copy)
    for copy in copies:
        copy.wait()


def fifth(limits, outer, inner, full, sums_a, sums_b, o5, o6, total, b5, b6, acc, sem):
    upper, lowest, highest = where_am_i()
    acc[...] = jnp.zeros(acc.shape, jnp.float32)

    def tile(i, _):
        f, rows, cols = cell(i)
        limit = limits[f]
        below, above = arrived(outer, inner, f, rows, cols, upper, lowest, highest, 2)

        def left(level):
            return tuple(jnp.where(lowest, e, v) for e, v in zip(low_end(level), below))

        def right(level):
            return tuple(jnp.where(highest, e, v) for e, v in zip(high_end(level), above))

        def keep_d(j, v):
            v = shrink(v, LOW**4 * HIGH, limit)
            b5[f, j, rows, cols] = v
            acc[f, 0] += v * v

        def keep_s(j, v):
            v = shrink(v, LOW**5, limit)
            b6[f, j, rows, cols] = v
            acc[f, 1] += v * v

        level = Level(2, left, right, keep_d, keep_s)
        for j in range(4):
            level.push(full[f, j, rows, cols])
        return 0

    lax.fori_loop(0, 16, tile, 0)
    copies = [pltpu.make_async_copy(b5, o5, sem.at[0]), pltpu.make_async_copy(b6, o6, sem.at[1])]
    for copy in copies:
        copy.start()
    lane = lax.broadcasted_iota(jnp.int32, (1, 128), 1)
    row = jnp.zeros((1, 128), jnp.float32)
    for f in range(2):
        for b in range(6):
            if b < 3:
                part = sums_a[f, b] + sums_b[f, b]
            elif b < 4:
                part = sums_b[f, b]
            else:
                part = acc[f, b - 4]
            row = row + jnp.where(lane == 6 * f + b, jnp.sum(part), 0.0)
    total[...] = row
    for copy in copies:
        copy.wait()


def local(fields, threshold):
    f32 = jnp.float32
    vmem, hbm, smem = (pl.BlockSpec(memory_space=m) for m in (pltpu.VMEM, pltpu.HBM, pltpu.SMEM))

    def arr(n):
        return jax.ShapeDtypeStruct((2, n, 32, 256), f32)

    def buf(n):
        return pltpu.VMEM((2, n, 32, 256), f32)

    def call(body, ins, outs, scratch, name, flops, mib, aliases=None):
        return pl.pallas_call(
            body,
            in_specs=ins,
            out_specs=[s for s, _ in outs],
            out_shape=[a for _, a in outs],
            scratch_shapes=scratch,
            input_output_aliases=aliases or {},
            compiler_params=pltpu.CompilerParams(vmem_limit_bytes=mib << 20),
            cost_estimate=pl.CostEstimate(flops=flops, bytes_accessed=1 << 20, transcendentals=0),
            name=name,
        )

    count = lax.axis_size("gz")
    across = [(i, (i + 1) % count if i % 2 else (i - 1) % count) for i in range(count)]
    within = [(i, i ^ 1) for i in range(count)]

    outer, inner, d1, d2, d3, d4, s4 = call(
        transform,
        [hbm],
        [(vmem, arr(8)), (vmem, arr(8)), (vmem, arr(32)), (vmem, arr(16)), (vmem, arr(8)), (vmem, arr(4)), (vmem, arr(4))],
        [buf(64), pltpu.SemaphoreType.DMA((8,))],
        "transform",
        20_000_000,
        8,
    )(fields)
    outer = lax.ppermute(outer, "gz", across)
    inner = lax.ppermute(inner, "gz", within)
    o1, o2, o3, sums_a = call(
        interiors,
        [smem, vmem, vmem, vmem],
        [(hbm, arr(32)), (hbm, arr(16)), (hbm, arr(8)), (vmem, jax.ShapeDtypeStruct((2, 3, 8, 128), f32))],
        [buf(32), buf(16), buf(8), pltpu.SemaphoreType.DMA((6,))],
        "interiors",
        2_000_000_000,
        8,
    )(threshold, d1, d2, d3)
    outer5, inner5, full = call(
        approximation,
        [vmem] * 3,
        [(vmem, arr(2)), (vmem, arr(2)), (vmem, arr(4))],
        [],
        "approximation",
        5_000_000,
        4,
    )(outer, inner, s4)
    outer5 = lax.ppermute(outer5, "gz", across)
    inner5 = lax.ppermute(inner5, "gz", within)
    o1, o2, o3, o4, sums_b = call(
        edges,
        [smem] + [vmem] * 6 + [hbm] * 3,
        [(hbm, arr(32)), (hbm, arr(16)), (hbm, arr(8)), (hbm, arr(4)), (vmem, jax.ShapeDtypeStruct((2, 4, 8, 128), f32))],
        [buf(3), buf(5), buf(6), buf(4), pltpu.SemaphoreType.DMA((14,))],
        "edges",
        1_000_000_000,
        6,
        {7: 0, 8: 1, 9: 2},
    )(threshold, outer, inner, d1, d2, d3, d4, o1, o2, o3)
    o5, o6, total = call(
        fifth,
        [smem] + [vmem] * 5,
        [(hbm, arr(2)), (hbm, arr(2)), (vmem, jax.ShapeDtypeStruct((1, 128), f32))],
        [buf(2), buf(2), pltpu.VMEM((2, 2, 8, 128), f32), pltpu.SemaphoreType.DMA((2,))],
        "fifth",
        5_000_000,
        4,
    )(threshold, outer5, inner5, full, sums_a, sums_b)

    devices = count * lax.axis_size("xy")
    parts = lax.all_to_all(jnp.broadcast_to(total[:, :12], (devices, 12)), ("gz", "xy"), 0, 0, tiled=True)
    cells = np.array([n * 32 * 256 * devices for n in (32, 16, 8, 4, 2, 2)] * 2, np.float32)
    energy = (jnp.sum(parts, axis=0) / cells).reshape(2, 6)
    return o1, o2, o3, o4, o5, o6, energy


def solution(mesh):
    split = P(None, "gz", "xy", None)
    return jax.shard_map(local, mesh=mesh, in_specs=(split, P()), out_specs=(split,) * 6 + (P(),), check_vma=False)
```

time: 125 us -> 54.2 us (0.43)
  the two profiles are of different devices: /device:TPU:56 before, /device:TPU:1 now
where the time goes in v1:
time: 54.2 us; the launch traced here: 54 us
  blocking collectives  20.5 us (38%)
  starting transfers between devices  16.3 us (30%)
  Pallas kernels  10.9 us (20%)
  local copies, waits for them, and re-layouts  2.91 us (5%)
  waiting for transfers between devices  2.38 us (4%)
  between operations  0.73 us (1%)
    all_to_all x1, blocking collectives, local(): lax.all_to_all(jnp.broadcast_to(total[:, :12], (devices, 12)), ('gz', 'xy...  20.5 us
    ppermute x1, starting transfers between devices, local(): inner5 = lax.ppermute(inner5, 'gz', within)  6.89 us
    ppermute x1, starting transfers between devices, local(): inner = lax.ppermute(inner, 'gz', within)  4.79 us
    pallas_call x1, Pallas kernels, local(): call(transform, [hbm], [(vmem, arr(8)), (vmem, arr(8)), (vmem, arr(32)),...  3.44 us
    ppermute x1, starting transfers between devices, local(): outer = lax.ppermute(outer, 'gz', across)  3.1 us
    pallas_call x1, Pallas kernels, local(): call(edges, [smem] + [vmem] * 6 + [hbm] * 3, [(hbm, arr(32)), (hbm, arr(1...  2.72 us
    ppermute x1, waiting for transfers between devices, local(): outer = lax.ppermute(outer, 'gz', across)  2.37 us
    pallas_call x1, Pallas kernels, local(): call(interiors, [smem, vmem, vmem, vmem], [(hbm, arr(32)), (hbm, arr(16))...  2.29 us
  transfers between devices with their start and end apart: 4, of which 1 were waited for; matrix products, arithmetic and copies ran while one was open for 0% of the time, Pallas kernels for 9%

profile of v1, /device:TPU:1, one launch (start us, length us, event | category | flops | bytes accessed | tf_op | source)
XLA Modules:
  0.0 54.0 jit_solution(6002659246040895923)
XLA Ops:
  0.6 0.0 copy-start
  0.6 2.2 %copy-done = f32[2,64,32,256]{3,2,1,0:T(8,128)S(1)} copy-done((f32[2,64,32,256]{3,2,1,0:T(8,128)S(1)}, f32[2,64,32,256]{3,2,1,0:T(8,128)}, u32[]{:S(2)}) %copy-start) | copy-done | bytes 4194328
  2.8 0.0 copy-start.1
  2.8 3.4 %transform.1 = (f32[2,8,32,256]{3,2,1,0:T(8,128)S(1)}, f32[2,8,32,256]{3,2,1,0:T(8,128)S(1)}, f32[2,32,32,256]{3,2,1,0:T(8,128)S(1)}, f32[2,16,32,256]{3,2,1,0:T...) custom-call(f32[2,64,32,256]{3,2,1,0:T(8,128)S(1)} %copy-done), custom_call_target="tpu_custom_call" | custom-call | flops 20000000 | bytes 1048576 | tf_op jit(solution)/shard_map/transform/pallas_call | solution.py:375
  6.3 3.1 %collective-permute-start = (f32[2,8,32,256]{3,2,1,0:T(8,128)S(1)}, f32[2,8,32,256]{3,2,1,0:T(8,128)S(1)}, u32[]{:S(2)}, u32[]{:S(2)}) collective-permute-start(f32[2,8,32,256]{3,2,1,0:T(8,128)S(1)} %get-tuple-element.29), channel_id=1, source_target_pairs={{0,248},{8,16},{16,8},{24,32},{32,24},{40,48},{48,40},{56,64},{64,... | collective-permute-start | bytes 1572872 | tf_op jit(solution)/shard_map/ppermute | solution.py:384
  9.4 4.8 %collective-permute-start.1 = (f32[2,8,32,256]{3,2,1,0:T(8,128)S(1)}, f32[2,8,32,256]{3,2,1,0:T(8,128)S(1)}, u32[]{:S(2)}, u32[]{:S(2)}) collective-permute-start(f32[2,8,32,256]{3,2,1,0:T(8,128)S(1)} %get-tuple-element.30), channel_id=1, source_target_pairs={{0,8},{8,0},{16,24},{24,16},{32,40},{40,32},{48,56},{56,48},{64,72... | collective-permute-start | bytes 1572872 | tf_op jit(solution)/shard_map/ppermute | solution.py:385
  14.2 2.4 %collective-permute-done.outer = f32[2,8,32,256]{3,2,1,0:T(8,128)S(1)} collective-permute-done((f32[2,8,32,256]{3,2,1,0:T(8,128)S(1)}, f32[2,8,32,256]{3,2,1,0:T(8,128)S(1)}, u32[]{:S(2)}, u32[]{:S(2)}) %collective-permute-start) | collective-permute-done | bytes 524320 | tf_op jit(solution)/shard_map/ppermute | solution.py:384
  16.5 0.0 collective-permute-done.1.inner
  16.5 0.6 %approximation.1 = (f32[2,2,32,256]{3,2,1,0:T(8,128)S(1)}, f32[2,2,32,256]{3,2,1,0:T(8,128)S(1)}, f32[2,4,32,256]{3,2,1,0:T(8,128)S(1)}) custom-call(f32[2,8,32,256]{3,2,1,0:T(8,128)S(1)} %collective-permute-done.outer, f32[2,8,32,256]{3,2,1,0:T(8,128)S(1)} %collective-permute-done.1.inner, f32[2,4,32,256]{3,2,1,0:T(8,128)S(1)} %get-tuple-element.42.s4), custom_call_target="tpu_custom_call" | custom-call | flops 5000000 | bytes 1048576 | tf_op jit(solution)/shard_map/approximation/pallas_call | solution.py:395
  17.2 1.5 %collective-permute-start.2 = (f32[2,2,32,256]{3,2,1,0:T(8,128)S(1)}, f32[2,2,32,256]{3,2,1,0:T(8,128)S(1)}, u32[]{:S(2)}, u32[]{:S(2)}) collective-permute-start(f32[2,2,32,256]{3,2,1,0:T(8,128)S(1)} %get-tuple-element.43), channel_id=1, source_target_pairs={{0,248},{8,16},{16,8},{24,32},{32,24},{40,48},{48,40},{56,64},{64,... | collective-permute-start | bytes 393224 | tf_op jit(solution)/shard_map/ppermute | solution.py:404
  18.7 6.9 %collective-permute-start.3 = (f32[2,2,32,256]{3,2,1,0:T(8,128)S(1)}, f32[2,2,32,256]{3,2,1,0:T(8,128)S(1)}, u32[]{:S(2)}, u32[]{:S(2)}) collective-permute-start(f32[2,2,32,256]{3,2,1,0:T(8,128)S(1)} %get-tuple-element.44), channel_id=1, source_target_pairs={{0,8},{8,0},{16,24},{24,16},{32,40},{40,32},{48,56},{56,48},{64,72... | collective-permute-start | bytes 393224 | tf_op jit(solution)/shard_map/ppermute | solution.py:405
  25.6 0.0 copy-done.1
  25.6 2.3 %interiors.1 = (f32[2,32,32,256]{3,2,1,0:T(8,128)}, f32[2,16,32,256]{3,2,1,0:T(8,128)}, f32[2,8,32,256]{3,2,1,0:T(8,128)}, f32[2,3,8,128]{3,2,1,0:T(8,128)S(1)}) custom-call(f32[2]{0:T(128)S(1)} %copy-done.1, f32[2,32,32,256]{3,2,1,0:T(8,128)S(1)} %get-tuple-element.31.d1, f32[2,16,32,256]{3,2,1,0:T(8,128)S(1)} %get-tuple-element.32.d2, ...), custom_call_target="tpu_custom_call" | custom-call | flops 2000000000 | bytes 1048576 | tf_op jit(solution)/shard_map/interiors/pallas_call | solution.py:386
  27.9 0.0 copy-start.2
  27.9 2.7 %edges.1 = (f32[2,32,32,256]{3,2,1,0:T(8,128)}, f32[2,16,32,256]{3,2,1,0:T(8,128)}, f32[2,8,32,256]{3,2,1,0:T(8,128)}, f32[2,4,32,256]{3,2,1,0:T(8,128)}, f32[2,4,8,128]{3,2,1,0:T(8,128)S(1)}) custom-call(f32[2]{0:T(128)S(1)} %copy-done.1, ...), custom_call_target="tpu_custom_call", output_to_operand_aliasing={{0}: (7, {}), {1}: (8, {}), {2}: (9, {})} | custom-call | flops 1000000000 | bytes 1048576 | tf_op jit(solution)/shard_map/edges/pallas_call | solution.py:406
  30.6 0.0 collective-permute-done.2.outer
  30.6 0.0 collective-permute-done.3.inner
  30.7 1.9 %fifth.1 = (f32[2,2,32,256]{3,2,1,0:T(8,128)}, f32[2,2,32,256]{3,2,1,0:T(8,128)}, f32[1,128]{1,0:T(1,128)S(1)}) custom-call(f32[2]{0:T(128)S(1)} %copy-done.1, f32[2,2,32,256]{3,2,1,0:T(8,128)S(1)} %collective-permute-done.2.outer, f32[2,2,32,256]{3,2,1,0:T(8,128)S(1)} %collective-permute-done.3.inner, f32[2,4,32,256]{3,2,1,0:T(8,128)S(1)} %get-tuple-element.45.full, ...), custom_call_target="tpu_custom_call" | custom-call | flops 5000000 | bytes 1048576 | tf_op jit(solution)/shard_map/fifth/pallas_call | solution.py:416
  32.5 0.1 broadcast_in_dim.2
  32.6 20.5 %all_to_all.6 = f32[256,1,12]{2,1,0:T(1,128)S(1)} all-to-all(f32[256,1,12]{2,1,0:T(1,128)S(1)} %broadcast_in_dim.2), channel_id=1, replica_groups=mesh['gz'=32,'xy'=8] {'gz','xy'}, dimensions={0} | all-to-all | bytes 24576 | tf_op jit(solution)/shard_map/all_to_all | solution.py:427
  53.1 0.3 reduce_sum.9
  53.4 0.0 copy-done.2
  53.4 0.6 %reshape.23 = f32[2,6]{1,0:T(2,128)} reshape(f32[12]{0:T(128)S(1)} %multiply) | data formatting | bytes 96 | tf_op jit(solution)/shard_map/reshape | solution.py:429
  (2 shorter events, 0.0 us)
Async XLA Ops:
  0.6 2.2 %copy-start = (f32[2,64,32,256]{3,2,1,0:T(8,128)S(1)}, f32[2,64,32,256]{3,2,1,0:T(8,128)}, u32[]{:S(2)}) copy-start(f32[2,64,32,256]{3,2,1,0:T(8,128)} %x_hbm.1) | copy-start | bytes 12582916
  2.8 22.8 %copy-start.1 = (f32[2]{0:T(128)S(1)}, f32[2]{0:T(128)}, u32[]{:S(2)}) copy-start(f32[2]{0:T(128)} %limits.5) | copy-start | bytes 28
  6.3 10.3 %collective-permute-start = (f32[2,8,32,256]{3,2,1,0:T(8,128)S(1)}, f32[2,8,32,256]{3,2,1,0:T(8,128)S(1)}, u32[]{:S(2)}, u32[]{:S(2)}) collective-permute-start(f32[2,8,32,256]{3,2,1,0:T(8,128)S(1)} %get-tuple-element.29), channel_id=1, source_target_pairs={{0,248},{8,16},{16,8},{24,32},{32,24},{40,48},{48,40},{56,64},{64,... | collective-permute-start | bytes 1572872 | tf_op jit(solution)/shard_map/ppermute | solution.py:384
  9.4 7.2 %collective-permute-start.1 = (f32[2,8,32,256]{3,2,1,0:T(8,128)S(1)}, f32[2,8,32,256]{3,2,1,0:T(8,128)S(1)}, u32[]{:S(2)}, u32[]{:S(2)}) collective-permute-start(f32[2,8,32,256]{3,2,1,0:T(8,128)S(1)} %get-tuple-element.30), channel_id=1, source_target_pairs={{0,8},{8,0},{16,24},{24,16},{32,40},{40,32},{48,56},{56,48},{64,72... | collective-permute-start | bytes 1572872 | tf_op jit(solution)/shard_map/ppermute | solution.py:385
  17.2 13.5 %collective-permute-start.2 = (f32[2,2,32,256]{3,2,1,0:T(8,128)S(1)}, f32[2,2,32,256]{3,2,1,0:T(8,128)S(1)}, u32[]{:S(2)}, u32[]{:S(2)}) collective-permute-start(f32[2,2,32,256]{3,2,1,0:T(8,128)S(1)} %get-tuple-element.43), channel_id=1, source_target_pairs={{0,248},{8,16},{16,8},{24,32},{32,24},{40,48},{48,40},{56,64},{64,... | collective-permute-start | bytes 393224 | tf_op jit(solution)/shard_map/ppermute | solution.py:404
  18.7 11.9 %collective-permute-start.3 = (f32[2,2,32,256]{3,2,1,0:T(8,128)S(1)}, f32[2,2,32,256]{3,2,1,0:T(8,128)S(1)}, u32[]{:S(2)}, u32[]{:S(2)}) collective-permute-start(f32[2,2,32,256]{3,2,1,0:T(8,128)S(1)} %get-tuple-element.44), channel_id=1, source_target_pairs={{0,8},{8,0},{16,24},{24,16},{32,40},{40,32},{48,56},{56,48},{64,72... | collective-permute-start | bytes 393224 | tf_op jit(solution)/shard_map/ppermute | solution.py:405
  27.9 25.5 %copy-start.2 = (f32[12]{0:T(128)S(1)}, f32[12]{0:T(128)}, u32[]{:S(2)}) copy-start(f32[12]{0:T(128)} %constant.5) | copy-start | bytes 148

commit v2 on v1

v2 whole, which is shorter than its diff:
```python
import functools

import jax
import jax.numpy as jnp
import numpy as np
from jax import lax
from jax.experimental import pallas as pl
from jax.experimental.pallas import tpu as pltpu
from jax.sharding import PartitionSpec as P

ALPHA = -1.586134342059924
BETA = -0.052980118572961
GAMMA = 0.882911075530934
DELTA = 0.443506852043971
KAPPA = 1.230174104914001
SQRT_TWO = 1.4142135623730951
LOW = SQRT_TWO / KAPPA
HIGH = KAPPA / SQRT_TWO
LEVELS = 5
FAR = 8
ALL = 2 * LEVELS
EDGE_LO = (1, 2, 3)
EDGE_HI = (2, 3, 3)
SPANS = [sorted({*range(lo), *range((32 >> l) - hi, 32 >> l)}) for l, (lo, hi) in enumerate(zip(EDGE_LO, EDGE_HI))]
SPANS += [[0, 1, 2, 3]]


class Level:
    def __init__(self, n, left, right, emit_d, emit_s):
        self.n, self.left, self.right, self.emit_d, self.emit_s = n, left, right, emit_d, emit_s
        self.s, self.d, self.d1, self.s2, self.d3 = [], [], [], [], []

    def push(self, x):
        if len(self.s) == len(self.d):
            self.s.append(x)
            i = len(self.s) - 2
            if i >= 0:
                self.add(self.d[i] + ALPHA * (self.s[i] + self.s[i + 1]))
        else:
            self.d.append(x)
            if len(self.d) == self.n:
                self.finish()

    def add(self, v):
        self.d1.append(v)
        i = len(self.d1) - 1
        if i == 0:
            self.p = ALPHA * self.s[0]
            self.c = self.s[0] + BETA * v
            return
        if i == 1:
            a, b = self.left(self)
            below = a + self.p
            self.s2.append(self.c + BETA * below)
            self.d3m = below + GAMMA * ((b + BETA * below) + self.s2[0])
        if i == self.n - 1:
            self.s2.append(self.b + BETA * v)
        else:
            self.s2.append(self.s[i] + BETA * (self.d1[i - 1] + v))
        self.third(i - 1, self.s2[i])

    def third(self, j, above):
        self.d3.append(self.d1[j] + GAMMA * (self.s2[j] + above))
        self.emit_d(j, self.d3[j])
        before = self.d3[j - 1] if j else self.d3m
        self.emit_s(j, self.s2[j] + DELTA * (before + self.d3[j]))

    def finish(self):
        n = self.n
        self.a = self.d[n - 1] + ALPHA * self.s[n - 1]
        self.b = self.s[n - 1] + BETA * self.d1[n - 2]
        p, c = self.right(self)
        v = self.a + p
        self.add(v)
        self.third(n - 1, c + BETA * v)


def low_end(level):
    return level.d[0] + ALPHA * level.s[1], level.s[1] + BETA * level.d1[1]


def high_end(level):
    return ALPHA * level.s[-1], level.b


@functools.cache
def response(side, length=1024):
    zero, unit = np.zeros(2 * LEVELS), np.eye(2 * LEVELS)
    found, u = [], [zero] * length
    for l in range(LEVELS):
        n = len(u) // 2
        state, none = (unit[2 * l], unit[2 * l + 1]), (zero, zero)
        d, s = [None] * n, [None] * n
        level = Level(
            n,
            lambda _: state if side == "lo" else none,
            lambda _: state if side == "hi" else none,
            d.__setitem__,
            s.__setitem__,
        )
        for x in u:
            level.push(x)
        u = s
        down, up = (level.p, level.c), (level.a, level.b)
        found.append((down, up, d, s) if side == "lo" else (up, down, d[::-1], s[::-1]))
    return found


TRANSFORM_MIB = 47
BACK, ON, DETAIL, APPROX = range(4)


def combine(row, states):
    total = None
    for k, x in zip(row, states):
        if k != 0.0:
            term = float(k) * x
            total = term if total is None else total + term
    return total


def where_am_i():
    z = lax.axis_index("gz")
    return lax.rem(z, 2) == 1, z == 0, z == lax.axis_size("gz") - 1


def cell(i):
    return i // 8, pl.ds(pl.multiple_of(lax.rem(i // 2, 4) * 8, 8), 8), pl.ds(pl.multiple_of(lax.rem(i, 2) * 128, 128), 128)


def transform(x_hbm, outer, outer5, inner, d1, d2, d3, d4, d5, s5, x_vmem, sem):
    upper, lowest, highest = where_am_i()

    def fetch(j):
        rows = pl.ds(pl.multiple_of(lax.rem(j, 4) * 8, 8), 8)
        at = (j // 4, slice(None), rows)
        return pltpu.make_async_copy(x_hbm.at[at], x_vmem.at[at], sem.at[j])

    for j in range(8):
        fetch(j).start()
    from_above, from_below = response("hi"), response("lo")
    bands = (d1, d2, d3, d4, d5)

    def tile(i, _):
        @pl.when(lax.rem(i, 2) == 0)
        def _():
            fetch(i // 2).wait()

        f, rows, cols = cell(i)
        down, up, levels = [], [], []

        def left(l):
            def state(level):
                down.extend((level.p, level.c))
                end = low_end(level)
                if l == 0:
                    return tuple(jnp.where(lowest, e, 0.0) for e in end)
                return tuple(jnp.where(lowest, e, combine(r, down)) for e, r in zip(end, from_above[l][BACK]))

            return state

        def right(l):
            def state(level):
                up.extend((level.a, level.b))
                end = high_end(level)
                if l == 0:
                    return tuple(jnp.where(highest, e, 0.0) for e in end)
                return tuple(jnp.where(highest, e, combine(r, up)) for e, r in zip(end, from_below[l][BACK]))

            return state

        def keep(l):
            def store(j, v):
                bands[l][f, j, rows, cols] = v

            return store

        def pass_on(l):
            def store(j, v):
                if l == LEVELS - 1:
                    s5[f, j, rows, cols] = v
                else:
                    levels[l + 1].push(v)

            return store

        for l in range(LEVELS):
            levels.append(Level(32 >> l, left(l), right(l), keep(l), pass_on(l)))
        for z in range(64):
            levels[0].push(x_vmem[f, z, rows, cols])
        for k in range(ALL):
            out = jnp.where(upper, up[k], down[k])
            if k < FAR:
                outer[f, k, rows, cols] = out
            else:
                outer5[f, k - FAR, rows, cols] = out
            inner[f, k, rows, cols] = jnp.where(upper, down[k], up[k])
        return 0

    lax.fori_loop(0, 16, tile, 0)


def shrink(v, scale, limit):
    v = v * scale
    return v - jnp.clip(v, -limit, limit)


def corrected(v, *parts):
    for row, states in parts:
        term = combine(row, states)
        if term is not None:
            v = term if v is None else v + term
    return v


def through(states, upper):
    lo, hi = response("lo", 64)[4][ON], response("hi", 64)[4][ON]
    sums = []
    for k in range(2):
        row = [jnp.where(upper, float(x), float(y)) for x, y in zip(lo[k], hi[k])]
        total = row[0] * states[0]
        for x, state in list(zip(row, states))[1:]:
            total = total + x * state
        sums.append(total)
    return sums


def hand_on(own5, inner, out5):
    upper, _, _ = where_am_i()

    def tile(i, _):
        f, rows, cols = cell(i)
        extra = through([inner[f, k, rows, cols] for k in range(FAR)], upper)
        for k in range(2):
            out5[f, k, rows, cols] = own5[f, k, rows, cols] + extra[k]
        return 0

    lax.fori_loop(0, 16, tile, 0)


def hand_in(outer, after, out5):
    upper, lowest, highest = where_am_i()
    end = jnp.logical_or(lowest, highest)

    def tile(i, _):
        f, rows, cols = cell(i)
        extra = through([outer[f, k, rows, cols] for k in range(FAR)], jnp.logical_not(upper))
        for k in range(2):
            out5[f, k, rows, cols] = jnp.where(end, 0.0, extra[k])
        return 0

    lax.fori_loop(0, 16, tile, 0)


def interiors(limits, d1, d2, d3, after, o1, o2, o3, sums, b1, b2, b3, sem):
    copies = []
    for f in range(2):
        limit = limits[f]
        for l, (raw, buf, out) in enumerate(((d1, b1, o1), (d2, b2, o2), (d3, b3, o3))):
            n = 32 >> l
            lo, hi = EDGE_LO[l], n - EDGE_HI[l]

            def layer(z, acc, raw=raw, buf=buf, l=l):
                v = shrink(raw[f, z], LOW**l * HIGH, limit)
                buf[f, z] = v
                return acc + v * v

            acc = lax.fori_loop(lo, hi, layer, jnp.zeros((32, 256), jnp.float32), unroll=True)
            acc = acc.reshape(4, 8, 256).sum(axis=0)
            sums[f, l] = acc[:, :128] + acc[:, 128:]
            at = (f, pl.ds(lo, hi - lo))
            copy = pltpu.make_async_copy(buf.at[at], out.at[at], sem.at[3 * f + l])
            copy.start()
            copies.append(copy)
    for copy in copies:
        copy.wait()


def arrived(outer, inner, f, rows, cols, upper, lowest, highest, width):
    below, above = [], []
    for k in range(width):
        o, i = outer[f, k, rows, cols], inner[f, k, rows, cols]
        below.append(jnp.where(lowest, 0.0, jnp.where(upper, i, o)))
        above.append(jnp.where(highest, 0.0, jnp.where(upper, o, i)))
    return below, above


def edges(limits, outer, inner, d1, d2, d3, d4, d5, s5, after, b1, b2, b3, b4, base, ends, sums):
    upper, lowest, highest = where_am_i()
    lo, hi = response("lo"), response("hi")
    pass_up = response("lo", 64)[4][ON]
    raws, bufs = (d1, d2, d3, d4), (b1, b2, b3, b4)
    sums[...] = jnp.zeros(sums.shape, jnp.float32)

    def tile(i, _):
        f, rows, cols = cell(i)
        limit = limits[f]
        below, above = arrived(outer, inner, f, rows, cols, upper, lowest, highest, FAR)
        for j in range(2):
            base[f, j, rows, cols] = corrected(
                d5[f, j, rows, cols], (lo[4][DETAIL][j][:FAR], below), (hi[4][DETAIL][1 - j][:FAR], above)
            )
            base[f, 2 + j, rows, cols] = corrected(
                s5[f, j, rows, cols], (lo[4][APPROX][j][:FAR], below), (hi[4][APPROX][1 - j][:FAR], above)
            )
            ends[f, j, rows, cols] = jnp.zeros((8, 128), jnp.float32)

        @pl.when(lowest)
        def _():
            u = [combine(hi[3][APPROX][3 - j], above) for j in range(4)]
            ends[f, 0, rows, cols] = u[1] + ALPHA * u[2]
            ends[f, 1, rows, cols] = u[2] + BETA * ((u[3] + ALPHA * u[2]) + inner[f, FAR, rows, cols])

        @pl.when(highest)
        def _():
            ends[f, 0, rows, cols] = ALPHA * combine(lo[3][APPROX][2], below)
            ends[f, 1, rows, cols] = combine(pass_up[1], below)

        for l in range(4):
            n, acc = 32 >> l, None
            for k, j in enumerate(SPANS[l]):
                row_lo = lo[l][DETAIL][j] if j < 6 else ()
                row_hi = hi[l][DETAIL][n - 1 - j] if n - 1 - j < 6 else ()
                v = corrected(raws[l][f, j, rows, cols], (row_lo, below), (row_hi, above))
                v = shrink(v, LOW**l * HIGH, limit)
                bufs[l][f, k, rows, cols] = v
                acc = v * v if acc is None else acc + v * v
            sums[f, l] += acc
        return 0

    lax.fori_loop(0, 16, tile, 0)


def fifth(limits, outer5, inner, relayed, base, ends, sums_a, sums_b, b5, b6, total, acc):
    upper, lowest, highest = where_am_i()
    lo, hi = response("lo")[4], response("hi")[4]
    acc[...] = jnp.zeros(acc.shape, jnp.float32)

    def tile(i, _):
        f, rows, cols = cell(i)
        limit = limits[f]
        below, above = [], []
        for k in range(2):
            o = outer5[f, k, rows, cols]
            n = inner[f, FAR + k, rows, cols] + relayed[f, k, rows, cols]
            e = ends[f, k, rows, cols]
            below.append(jnp.where(lowest, e, jnp.where(upper, n, o)))
            above.append(jnp.where(highest, e, jnp.where(upper, o, n)))
        for j in range(2):
            d = corrected(base[f, j, rows, cols], (lo[DETAIL][j][FAR:], below), (hi[DETAIL][1 - j][FAR:], above))
            d = shrink(d, LOW**4 * HIGH, limit)
            b5[f, j, rows, cols] = d
            s = corrected(base[f, 2 + j, rows, cols], (lo[APPROX][j][FAR:], below), (hi[APPROX][1 - j][FAR:], above))
            s = shrink(s, LOW**5, limit)
            b6[f, j, rows, cols] = s
            acc[f, 0] += d * d
            acc[f, 1] += s * s
        return 0

    lax.fori_loop(0, 16, tile, 0)
    lane = lax.broadcasted_iota(jnp.int32, (1, 128), 1)
    row = jnp.zeros((1, 128), jnp.float32)
    for f in range(2):
        for b in range(6):
            if b < 3:
                part = sums_a[f, b] + sums_b[f, b]
            elif b < 4:
                part = sums_b[f, b]
            else:
                part = acc[f, b - 4]
            row = row + jnp.where(lane == 6 * f + b, jnp.sum(part), 0.0)
    total[...] = row


def finish(cells, parts, b1, b2, b3, b4, b5, b6, o1_in, o2_in, o3_in, o1, o2, o3, o4, o5, o6, energy, sem):
    copies = []
    for f in range(2):
        for l, (buf, out) in enumerate(((b1, o1), (b2, o2), (b3, o3))):
            lo, hi, n = EDGE_LO[l], EDGE_HI[l], 32 >> l
            for start, size, to in ((0, lo, 0), (lo, hi, n - hi)):
                copies.append((buf.at[f, pl.ds(start, size)], out.at[f, pl.ds(to, size)]))
    copies += [(b4, o4), (b5, o5), (b6, o6)]
    copies = [pltpu.make_async_copy(a, b, sem.at[k]) for k, (a, b) in enumerate(copies)]
    for copy in copies:
        copy.start()
    row = jnp.sum(parts[...], axis=0) * (1.0 / cells[...])
    energy[0:1, :] = row[:, 0:6]
    energy[1:2, :] = row[:, 6:12]
    for copy in copies:
        copy.wait()


def local(fields, threshold):
    f32 = jnp.float32
    vmem, hbm, smem = (pl.BlockSpec(memory_space=m) for m in (pltpu.VMEM, pltpu.HBM, pltpu.SMEM))

    def arr(n):
        return jax.ShapeDtypeStruct((2, n, 32, 256), f32)

    def tiles(n):
        return jax.ShapeDtypeStruct((2, n, 8, 128), f32)

    def buf(n):
        return pltpu.VMEM((2, n, 32, 256), f32)

    def call(body, ins, outs, scratch, flops, mib, aliases=None):
        return pl.pallas_call(
            body,
            in_specs=ins,
            out_specs=[s for s, _ in outs],
            out_shape=[a for _, a in outs],
            scratch_shapes=scratch,
            input_output_aliases=aliases or {},
            compiler_params=pltpu.CompilerParams(vmem_limit_bytes=mib << 20),
            cost_estimate=pl.CostEstimate(flops=flops, bytes_accessed=1 << 20, transcendentals=0),
            name=body.__name__,
        )

    count = lax.axis_size("gz")
    across = [(i, i if i in (0, count - 1) else i + 1 if i % 2 else i - 1) for i in range(count)]
    within = [(i, i ^ 1) for i in range(count)]

    outer, own5, inner, d1, d2, d3, d4, d5, s5 = call(
        transform,
        [hbm],
        [(vmem, arr(n)) for n in (FAR, 2, ALL, 32, 16, 8, 4, 2, 2)],
        [buf(64), pltpu.SemaphoreType.DMA((8,))],
        20_000_000,
        TRANSFORM_MIB,
    )(fields)
    outer = lax.ppermute(outer, "gz", across)
    inner = lax.ppermute(inner, "gz", within)
    (own5,) = call(hand_on, [vmem] * 2, [(vmem, arr(2))], [], 5_000_000, 4)(own5, inner)
    outer5 = lax.ppermute(own5, "gz", across)
    o1, o2, o3, sums_a = call(
        interiors,
        [smem] + [vmem] * 4,
        [(hbm, arr(32)), (hbm, arr(16)), (hbm, arr(8)), (vmem, tiles(3))],
        [buf(32), buf(16), buf(8), pltpu.SemaphoreType.DMA((6,))],
        2_000_000_000,
        8,
    )(threshold, d1, d2, d3, own5)
    (relayed,) = call(hand_in, [vmem] * 2, [(vmem, arr(2))], [], 5_000_000, 4)(outer, sums_a)
    received = lax.ppermute(relayed, "gz", within)
    b1, b2, b3, b4, base, ends, sums_b = call(
        edges,
        [smem] + [vmem] * 9,
        [(vmem, arr(n)) for n in (3, 5, 6, 4, 4, 2)] + [(vmem, tiles(4))],
        [],
        1_000_000_000,
        4,
    )(threshold, outer, inner, d1, d2, d3, d4, d5, s5, relayed)
    b5, b6, total = call(
        fifth,
        [smem] + [vmem] * 7,
        [(vmem, arr(2)), (vmem, arr(2)), (vmem, jax.ShapeDtypeStruct((1, 128), f32))],
        [pltpu.VMEM((2, 2, 8, 128), f32)],
        5_000_000,
        4,
    )(threshold, outer5, inner, received, base, ends, sums_a, sums_b)

    devices = count * lax.axis_size("xy")
    parts = lax.all_to_all(jnp.broadcast_to(total, (devices, 1, 128)), ("gz", "xy"), 0, 0, tiled=True)
    cells = np.zeros((1, 128), np.float32) + 1.0
    cells[0, :12] = [n * 32 * 256 * devices for n in (32, 16, 8, 4, 2, 2)] * 2
    o1, o2, o3, o4, o5, o6, energy = call(
        finish,
        [vmem] * 8 + [hbm] * 3,
        [(hbm, arr(n)) for n in (32, 16, 8, 4, 2, 2)] + [(vmem, jax.ShapeDtypeStruct((2, 6), f32))],
        [pltpu.SemaphoreType.DMA((15,))],
        5_000_000,
        4,
        {8: 0, 9: 1, 10: 2},
    )(cells, parts, b1, b2, b3, b4, b5, b6, o1, o2, o3)
    return o1, o2, o3, o4, o5, o6, energy


def solution(mesh):
    split = P(None, "gz", "xy", None)
    return jax.shard_map(local, mesh=mesh, in_specs=(split, P()), out_specs=(split,) * 6 + (P(),), check_vma=False)
```

time: 54.2 us -> 50.6 us (0.934)
  starting transfers between devices: 16.3 us -> 8.93 us
  blocking collectives: 20.5 us -> 26.6 us
  local copies, waits for them, and re-layouts: 2.91 us -> 0.08 us
  Pallas kernels: 10.9 us -> 12 us
    all_to_all x1, blocking collectives: 20.5 us -> 26.6 us  [local(): lax.all_to_all(jnp.broadcast_to(total, (devices, 1, 128)), ('gz', 'xy'),...]
    ppermute x2, starting transfers between devices: 8.43 us -> 3.73 us  [the longest x1 3.64 us: local(): outer5 = lax.ppermute(own5, 'gz', across)]
    unnamed x6 -> x4, local copies, waits for them, and re-layouts: 2.19 us -> 0.01 us
    ppermute x1, starting transfers between devices: 4.79 us -> 3.29 us  [local(): inner = lax.ppermute(inner, 'gz', within)]
    ppermute x1, starting transfers between devices: 3.1 us -> 1.91 us  [local(): outer = lax.ppermute(outer, 'gz', across)]
    pallas_call x5 -> x7, Pallas kernels: 10.9 us -> 12 us  [the longest x1 3.69 us: local(): call(transform, [hbm], [(vmem, arr(n)) for n in (FAR, 2, ALL, 32, 16, 8,...]
    reshape x1 -> x0, local copies, waits for them, and re-layouts: 0.64 us -> none  [local(): energy = (jnp.sum(parts, axis=0) / cells).reshape(2, 6)]
  transfers between devices with their start and end apart: 4 -> 4, of which waited for: 1 -> 1; matrix products, arithmetic and copies ran while one was open for 0% -> 0% of each run, Pallas kernels for 9% -> 10%
where the time goes in v2:
time: 50.6 us; the launch traced here: 50.5 us
  blocking collectives  26.6 us (53%)
  Pallas kernels  12 us (24%)
  starting transfers between devices  8.93 us (18%)
  waiting for transfers between devices  2.14 us (4%)
  between operations  0.75 us (1%)
    all_to_all x1, blocking collectives, local(): lax.all_to_all(jnp.broadcast_to(total, (devices, 1, 128)), ('gz', 'xy'),...  26.6 us
    pallas_call x1, Pallas kernels, local(): call(transform, [hbm], [(vmem, arr(n)) for n in (FAR, 2, ALL, 32, 16, 8,...  3.69 us
    ppermute x1, starting transfers between devices, local(): outer5 = lax.ppermute(own5, 'gz', across)  3.64 us
    ppermute x1, starting transfers between devices, local(): inner = lax.ppermute(inner, 'gz', within)  3.29 us
    pallas_call x1, Pallas kernels, local(): call(interiors, [smem] + [vmem] * 4, [(hbm, arr(32)), (hbm, arr(16)), (hb...  2.29 us
    ppermute x1, waiting for transfers between devices, local(): outer = lax.ppermute(outer, 'gz', across)  2.13 us
    pallas_call x1, Pallas kernels, local(): call(edges, [smem] + [vmem] * 9, [(vmem, arr(n)) for n in (3, 5, 6, 4, 4,...  2.06 us
    ppermute x1, starting transfers between devices, local(): outer = lax.ppermute(outer, 'gz', across)  1.91 us
  transfers between devices with their start and end apart: 4, of which 1 were waited for; matrix products, arithmetic and copies ran while one was open for 0% of the time, Pallas kernels for 10%

profile of v2, /device:TPU:1, one launch (start us, length us, event | category | flops | bytes accessed | tf_op | source)
XLA Modules:
  0.0 50.5 jit_solution(18188417139415145071)
XLA Ops:
  0.6 0.0 copy-start
  0.6 3.7 %transform.1 = (f32[2,8,32,256]{3,2,1,0:T(8,128)S(1)}, f32[2,2,32,256]{3,2,1,0:T(8,128)S(1)}, f32[2,10,32,256]{3,2,1,0:T(8,128)S(1)}, f32[2,32,32,256]{3,2,1,0:T...) custom-call(f32[2,64,32,256]{3,2,1,0:T(8,128)} %x_hbm.1), custom_call_target="tpu_custom_call" | custom-call | flops 20000000 | bytes 1048576 | tf_op jit(solution)/shard_map/transform/pallas_call | solution.py:423
  4.3 3.3 %collective-permute-start = (f32[2,10,32,256]{3,2,1,0:T(8,128)S(1)}, f32[2,10,32,256]{3,2,1,0:T(8,128)S(1)}, u32[]{:S(2)}, u32[]{:S(2)}) collective-permute-start(f32[2,10,32,256]{3,2,1,0:T(8,128)S(1)} %get-tuple-element.31), channel_id=1, source_target_pairs={{0,8},{8,0},{16,24},{24,16},{32,40},{40,32},{48,56},{56,48},{64,72... | collective-permute-start | bytes 1966088 | tf_op jit(solution)/shard_map/ppermute | solution.py:432
  7.6 1.9 %collective-permute-start.2 = (f32[2,8,32,256]{3,2,1,0:T(8,128)S(1)}, f32[2,8,32,256]{3,2,1,0:T(8,128)S(1)}, u32[]{:S(2)}, u32[]{:S(2)}) collective-permute-start(f32[2,8,32,256]{3,2,1,0:T(8,128)S(1)} %get-tuple-element.32), channel_id=1, source_target_pairs={{0,0},{8,16},{16,8},{24,32},{32,24},{40,48},{48,40},{56,64},{64,56... | collective-permute-start | bytes 1572872 | tf_op jit(solution)/shard_map/ppermute | solution.py:431
  9.5 0.0 collective-permute-done.inner
  9.6 0.5 hand_on.1.after
  10.0 3.6 %collective-permute-start.1 = (f32[2,2,32,256]{3,2,1,0:T(8,128)S(1)}, f32[2,2,32,256]{3,2,1,0:T(8,128)S(1)}, u32[]{:S(2)}, u32[]{:S(2)}) collective-permute-start(f32[2,2,32,256]{3,2,1,0:T(8,128)S(1)} %hand_on.1.after), channel_id=1, source_target_pairs={{0,0},{8,16},{16,8},{24,32},{32,24},{40,48},{48,40},{56,64},{64,56... | collective-permute-start | bytes 393224 | tf_op jit(solution)/shard_map/ppermute | solution.py:434
  13.7 0.0 copy-done
  13.7 2.3 %interiors.1 = (f32[2,32,32,256]{3,2,1,0:T(8,128)}, f32[2,16,32,256]{3,2,1,0:T(8,128)}, f32[2,8,32,256]{3,2,1,0:T(8,128)}, f32[2,3,8,128]{3,2,1,0:T(8,128)S(1)}) custom-call(f32[2]{0:T(128)S(1)} %copy-done, f32[2,32,32,256]{3,2,1,0:T(8,128)S(1)} %get-tuple-element.33.d1, f32[2,16,32,256]{3,2,1,0:T(8,128)S(1)} %get-tuple-element.34.d2, ...), custom_call_target="tpu_custom_call" | custom-call | flops 2000000000 | bytes 1048576 | tf_op jit(solution)/shard_map/interiors/pallas_call | solution.py:435
  16.0 2.1 %collective-permute-done.2.outer = f32[2,8,32,256]{3,2,1,0:T(8,128)S(1)} collective-permute-done((f32[2,8,32,256]{3,2,1,0:T(8,128)S(1)}, f32[2,8,32,256]{3,2,1,0:T(8,128)S(1)}, u32[]{:S(2)}, u32[]{:S(2)}) %collective-permute-start.2) | collective-permute-done | bytes 524320 | tf_op jit(solution)/shard_map/ppermute | solution.py:431
  18.1 0.5 hand_in.1.after
  18.6 0.1 collective-permute-start.3
  18.7 0.0 copy-start.1
  18.7 2.1 %edges.1 = (f32[2,3,32,256]{3,2,1,0:T(8,128)S(1)}, f32[2,5,32,256]{3,2,1,0:T(8,128)S(1)}, f32[2,6,32,256]{3,2,1,0:T(8,128)S(1)}, f32[2,4,32,256]{3,2,1,0:T(8,128...) custom-call(f32[2]{0:T(128)S(1)} %copy-done, ...), custom_call_target="tpu_custom_call" | custom-call | flops 1000000000 | bytes 1048576 | tf_op jit(solution)/shard_map/edges/pallas_call | solution.py:445
  20.8 0.0 collective-permute-done.1.outer5
  20.8 0.0 collective-permute-done.3.relayed
  20.8 1.2 %fifth.1 = (f32[2,2,32,256]{3,2,1,0:T(8,128)S(1)}, f32[2,2,32,256]{3,2,1,0:T(8,128)S(1)}, f32[1,128]{1,0:T(1,128)S(1)}) custom-call(f32[2]{0:T(128)S(1)} %copy-done, f32[2,2,32,256]{3,2,1,0:T(8,128)S(1)} %collective-permute-done.1.outer5, f32[2,10,32,256]{3,2,1,0:T(8,128)S(1)} %collective-permute-done.inner, ...), custom_call_target="tpu_custom_call" | custom-call | flops 5000000 | bytes 1048576 | tf_op jit(solution)/shard_map/fifth/pallas_call | solution.py:453
  22.0 0.1 broadcast_in_dim.3
  22.1 26.6 %all_to_all.5.parts = f32[256,1,128]{2,1,0:T(1,128)S(1)} all-to-all(f32[256,1,128]{2,1,0:T(1,128)S(1)} %broadcast_in_dim.3), channel_id=1, replica_groups=mesh['gz'=32,'xy'=8] {'gz','xy'}, dimensions={0} | all-to-all | bytes 262144 | tf_op jit(solution)/shard_map/all_to_all | solution.py:463
  48.7 0.0 copy-done.1
  48.7 1.8 %finish.1 = (f32[2,32,32,256]{3,2,1,0:T(8,128)}, f32[2,16,32,256]{3,2,1,0:T(8,128)}, f32[2,8,32,256]{3,2,1,0:T(8,128)}, f32[2,4,32,256]{3,2,1,0:T(8,128)}, f32[2...) custom-call(f32[1,128]{1,0:T(1,128)S(1)} %copy-done.1, ...), custom_call_target="tpu_custom_call", output_to_operand_aliasing={{0}: (8, {}), {1}: (9, {}), {2}: (10, {})} | custom-call | flops 5000000 | bytes 1048576 | tf_op jit(solution)/shard_map/finish/pallas_call | solution.py:466
Async XLA Ops:
  0.6 13.0 %copy-start = (f32[2]{0:T(128)S(1)}, f32[2]{0:T(128)}, u32[]{:S(2)}) copy-start(f32[2]{0:T(128)} %limits.5) | copy-start | bytes 28
  4.3 5.2 %collective-permute-start = (f32[2,10,32,256]{3,2,1,0:T(8,128)S(1)}, f32[2,10,32,256]{3,2,1,0:T(8,128)S(1)}, u32[]{:S(2)}, u32[]{:S(2)}) collective-permute-start(f32[2,10,32,256]{3,2,1,0:T(8,128)S(1)} %get-tuple-element.31), channel_id=1, source_target_pairs={{0,8},{8,0},{16,24},{24,16},{32,40},{40,32},{48,56},{56,48},{64,72... | collective-permute-start | bytes 1966088 | tf_op jit(solution)/shard_map/ppermute | solution.py:432
  7.6 10.5 %collective-permute-start.2 = (f32[2,8,32,256]{3,2,1,0:T(8,128)S(1)}, f32[2,8,32,256]{3,2,1,0:T(8,128)S(1)}, u32[]{:S(2)}, u32[]{:S(2)}) collective-permute-start(f32[2,8,32,256]{3,2,1,0:T(8,128)S(1)} %get-tuple-element.32), channel_id=1, source_target_pairs={{0,0},{8,16},{16,8},{24,32},{32,24},{40,48},{48,40},{56,64},{64,56... | collective-permute-start | bytes 1572872 | tf_op jit(solution)/shard_map/ppermute | solution.py:431
  10.0 10.7 %collective-permute-start.1 = (f32[2,2,32,256]{3,2,1,0:T(8,128)S(1)}, f32[2,2,32,256]{3,2,1,0:T(8,128)S(1)}, u32[]{:S(2)}, u32[]{:S(2)}) collective-permute-start(f32[2,2,32,256]{3,2,1,0:T(8,128)S(1)} %hand_on.1.after), channel_id=1, source_target_pairs={{0,0},{8,16},{16,8},{24,32},{32,24},{40,48},{48,40},{56,64},{64,56... | collective-permute-start | bytes 393224 | tf_op jit(solution)/shard_map/ppermute | solution.py:434
  18.6 2.2 %collective-permute-start.3 = (f32[2,2,32,256]{3,2,1,0:T(8,128)S(1)}, f32[2,2,32,256]{3,2,1,0:T(8,128)S(1)}, u32[]{:S(2)}, u32[]{:S(2)}) collective-permute-start(f32[2,2,32,256]{3,2,1,0:T(8,128)S(1)} %hand_in.1.after), channel_id=1, source_target_pairs={{0,8},{8,0},{16,24},{24,16},{32,40},{40,32},{48,56},{56,48},{64,72... | collective-permute-start | bytes 393224 | tf_op jit(solution)/shard_map/ppermute | solution.py:444
  18.7 30.0 %copy-start.1 = (f32[1,128]{1,0:T(1,128)S(1)}, f32[1,128]{1,0:T(1,128)}, u32[]{:S(2)}) copy-start(f32[1,128]{1,0:T(1,128)} %constant.2.clone.cells) | copy-start | bytes 1540

commit v3 on v2

--- a/solution.py
+++ b/solution.py
@@ -7,6 +7,7 @@
 from jax.experimental import pallas as pl
 from jax.experimental.pallas import tpu as pltpu
 from jax.sharding import PartitionSpec as P
+
 
 ALPHA = -1.586134342059924
 BETA = -0.052980118572961
@@ -21,8 +22,6 @@
 ALL = 2 * LEVELS
 EDGE_LO = (1, 2, 3)
 EDGE_HI = (2, 3, 3)
-SPANS = [sorted({*range(lo), *range((32 >> l) - hi, 32 >> l)}) for l, (lo, hi) in enumerate(zip(EDGE_LO, EDGE_HI))]
-SPANS += [[0, 1, 2, 3]]
 
 
 class Level:
@@ -124,8 +123,15 @@
     return lax.rem(z, 2) == 1, z == 0, z == lax.axis_size("gz") - 1
 
 
-def cell(i):
-    return i // 8, pl.ds(pl.multiple_of(lax.rem(i // 2, 4) * 8, 8), 8), pl.ds(pl.multiple_of(lax.rem(i, 2) * 128, 128), 128)
+def over_tiles(body, fields=(0, 1), unroll=2):
+    for f in fields:
+
+        def step(i, carry, f=f):
+            rows = pl.ds(pl.multiple_of((i // 2) * 8, 8), 8)
+            body(f, rows, pl.ds(pl.multiple_of(lax.rem(i, 2) * 128, 128), 128))
+            return carry
+
+        lax.fori_loop(0, 8, step, 0, unroll=unroll)
 
 
 def transform(x_hbm, outer, outer5, inner, d1, d2, d3, d4, d5, s5, x_vmem, sem):
@@ -138,15 +144,17 @@
 
     for j in range(8):
         fetch(j).start()
+    bands = (d1, d2, d3, d4, d5)
     from_above, from_below = response("hi"), response("lo")
-    bands = (d1, d2, d3, d4, d5)
-
-    def tile(i, _):
+
+    def tile(i, carry):
         @pl.when(lax.rem(i, 2) == 0)
         def _():
             fetch(i // 2).wait()
 
-        f, rows, cols = cell(i)
+        f = i // 8
+        rows = pl.ds(pl.multiple_of(lax.rem(i // 2, 4) * 8, 8), 8)
+        cols = pl.ds(pl.multiple_of(lax.rem(i, 2) * 128, 128), 128)
         down, up, levels = [], [], []
 
         def left(l):
@@ -195,7 +203,7 @@
             else:
                 outer5[f, k - FAR, rows, cols] = out
             inner[f, k, rows, cols] = jnp.where(upper, down[k], up[k])
-        return 0
+        return carry
 
     lax.fori_loop(0, 16, tile, 0)
 
@@ -228,116 +236,169 @@
 def hand_on(own5, inner, out5):
     upper, _, _ = where_am_i()
 
-    def tile(i, _):
-        f, rows, cols = cell(i)
+    def tile(f, rows, cols):
         extra = through([inner[f, k, rows, cols] for k in range(FAR)], upper)
         for k in range(2):
             out5[f, k, rows, cols] = own5[f, k, rows, cols] + extra[k]
-        return 0
-
-    lax.fori_loop(0, 16, tile, 0)
+
+    over_tiles(tile)
 
 
 def hand_in(outer, after, out5):
     upper, lowest, highest = where_am_i()
     end = jnp.logical_or(lowest, highest)
 
-    def tile(i, _):
-        f, rows, cols = cell(i)
+    def tile(f, rows, cols):
         extra = through([outer[f, k, rows, cols] for k in range(FAR)], jnp.logical_not(upper))
         for k in range(2):
             out5[f, k, rows, cols] = jnp.where(end, 0.0, extra[k])
-        return 0
-
-    lax.fori_loop(0, 16, tile, 0)
-
-
-def interiors(limits, d1, d2, d3, after, o1, o2, o3, sums, b1, b2, b3, sem):
+
+    over_tiles(tile)
+
+
+def add_parts(lo, hi, upper_side, states, v4, v5, v6, f, rows, cols, out4, out5, out6):
+    rows_of = hi if upper_side else lo
+    for src, dst, l, kind, n in ((v4, out4, 3, DETAIL, 4), (v5, out5, 4, DETAIL, 2), (v6, out6, 4, APPROX, 2)):
+        for j in range(n):
+            row = rows_of[l][kind][n - 1 - j if upper_side else j][:FAR]
+            dst[f, j, rows, cols] = corrected(src[f, j, rows, cols], (row, states))
+
+
+def side(upper_side, l):
+    return ((32 >> l) - EDGE_HI[l], EDGE_HI[l]) if upper_side else (0, EDGE_LO[l])
+
+
+def near(limits, d1, d2, d3, d4, d5, s5, inner, after, o1, o2, o3, n4, n5, n6, ends, sums, b1, b2, b3, acc, sem):
+    upper, lowest, highest = where_am_i()
+    lo, hi = response("lo"), response("hi")
+    pass_up = response("lo", 64)[4][ON]
+    triples = ((d1, b1, o1), (d2, b2, o2), (d3, b3, o3))
     copies = []
     for f in range(2):
         limit = limits[f]
-        for l, (raw, buf, out) in enumerate(((d1, b1, o1), (d2, b2, o2), (d3, b3, o3))):
-            n = 32 >> l
-            lo, hi = EDGE_LO[l], n - EDGE_HI[l]
-
-            def layer(z, acc, raw=raw, buf=buf, l=l):
+        for l, (raw, buf, out) in enumerate(triples):
+            first, last = EDGE_LO[l], (32 >> l) - EDGE_HI[l]
+
+            def layer(z, total, raw=raw, buf=buf, l=l):
                 v = shrink(raw[f, z], LOW**l * HIGH, limit)
                 buf[f, z] = v
-                return acc + v * v
-
-            acc = lax.fori_loop(lo, hi, layer, jnp.zeros((32, 256), jnp.float32), unroll=True)
-            acc = acc.reshape(4, 8, 256).sum(axis=0)
-            sums[f, l] = acc[:, :128] + acc[:, 128:]
-            at = (f, pl.ds(lo, hi - lo))
+                return total + v * v
+
+            total = lax.fori_loop(first, last, layer, jnp.zeros((32, 256), jnp.float32), unroll=True)
+            total = total.reshape(4, 8, 256).sum(axis=0)
+            acc[f, l] = total[:, :128] + total[:, 128:]
+            at = (f, pl.ds(first, last - first))
             copy = pltpu.make_async_copy(buf.at[at], out.at[at], sem.at[3 * f + l])
             copy.start()
             copies.append(copy)
-    for copy in copies:
-        copy.wait()
-
-
-def arrived(outer, inner, f, rows, cols, upper, lowest, highest, width):
-    below, above = [], []
-    for k in range(width):
-        o, i = outer[f, k, rows, cols], inner[f, k, rows, cols]
-        below.append(jnp.where(lowest, 0.0, jnp.where(upper, i, o)))
-        above.append(jnp.where(highest, 0.0, jnp.where(upper, o, i)))
-    return below, above
-
-
-def edges(limits, outer, inner, d1, d2, d3, d4, d5, s5, after, b1, b2, b3, b4, base, ends, sums):
-    upper, lowest, highest = where_am_i()
-    lo, hi = response("lo"), response("hi")
-    pass_up = response("lo", 64)[4][ON]
-    raws, bufs = (d1, d2, d3, d4), (b1, b2, b3, b4)
-    sums[...] = jnp.zeros(sums.shape, jnp.float32)
-
-    def tile(i, _):
-        f, rows, cols = cell(i)
-        limit = limits[f]
-        below, above = arrived(outer, inner, f, rows, cols, upper, lowest, highest, FAR)
-        for j in range(2):
-            base[f, j, rows, cols] = corrected(
-                d5[f, j, rows, cols], (lo[4][DETAIL][j][:FAR], below), (hi[4][DETAIL][1 - j][:FAR], above)
-            )
-            base[f, 2 + j, rows, cols] = corrected(
-                s5[f, j, rows, cols], (lo[4][APPROX][j][:FAR], below), (hi[4][APPROX][1 - j][:FAR], above)
-            )
-            ends[f, j, rows, cols] = jnp.zeros((8, 128), jnp.float32)
-
-        @pl.when(lowest)
-        def _():
+
+    def inner_side(upper_side):
+        def tile(f, rows, cols):
+            limit = limits[f]
+            states = [inner[f, k, rows, cols] for k in range(FAR)]
+            for l, (raw, buf, _) in enumerate(triples):
+                start, size = side(upper_side, l)
+                total = acc[f, l]
+                for j in range(start, start + size):
+                    row = hi[l][DETAIL][(32 >> l) - 1 - j] if upper_side else lo[l][DETAIL][j]
+                    v = shrink(corrected(raw[f, j, rows, cols], (row, states)), LOW**l * HIGH, limit)
+                    buf[f, j, rows, cols] = v
+                    total = total + v * v
+                acc[f, l] = total
+            add_parts(lo, hi, upper_side, states, d4, d5, s5, f, rows, cols, n4, n5, n6)
+
+        over_tiles(tile)
+        pieces = []
+        for f in range(2):
+            for l, (_, buf, out) in enumerate(triples):
+                at = (f, pl.ds(*side(upper_side, l)))
+                pieces.append(pltpu.make_async_copy(buf.at[at], out.at[at], sem.at[6 + 3 * f + l]))
+        for piece in pieces:
+            piece.start()
+        for piece in pieces:
+            piece.wait()
+
+    @pl.when(jnp.logical_not(jnp.logical_or(lowest, highest)))
+    def _():
+        ends[...] = jnp.zeros(ends.shape, jnp.float32)
+
+    @pl.when(lowest)
+    def _():
+        def tile(f, rows, cols):
+            above = [inner[f, k, rows, cols] for k in range(FAR)]
             u = [combine(hi[3][APPROX][3 - j], above) for j in range(4)]
             ends[f, 0, rows, cols] = u[1] + ALPHA * u[2]
             ends[f, 1, rows, cols] = u[2] + BETA * ((u[3] + ALPHA * u[2]) + inner[f, FAR, rows, cols])
 
-        @pl.when(highest)
-        def _():
+        over_tiles(tile)
+
+    @pl.when(highest)
+    def _():
+        def tile(f, rows, cols):
+            below = [inner[f, k, rows, cols] for k in range(FAR)]
             ends[f, 0, rows, cols] = ALPHA * combine(lo[3][APPROX][2], below)
             ends[f, 1, rows, cols] = combine(pass_up[1], below)
 
-        for l in range(4):
-            n, acc = 32 >> l, None
-            for k, j in enumerate(SPANS[l]):
-                row_lo = lo[l][DETAIL][j] if j < 6 else ()
-                row_hi = hi[l][DETAIL][n - 1 - j] if n - 1 - j < 6 else ()
-                v = corrected(raws[l][f, j, rows, cols], (row_lo, below), (row_hi, above))
-                v = shrink(v, LOW**l * HIGH, limit)
-                bufs[l][f, k, rows, cols] = v
-                acc = v * v if acc is None else acc + v * v
-            sums[f, l] += acc
-        return 0
-
-    lax.fori_loop(0, 16, tile, 0)
-
-
-def fifth(limits, outer5, inner, relayed, base, ends, sums_a, sums_b, b5, b6, total, acc):
+        over_tiles(tile)
+
+    @pl.when(upper)
+    def _():
+        inner_side(False)
+
+    @pl.when(jnp.logical_not(upper))
+    def _():
+        inner_side(True)
+
+    sums[...] = acc[...]
+    for copy in copies:
+        copy.wait()
+
+
+def edges(limits, outer, d1, d2, d3, n4, n5, n6, after, b1, b2, b3, b4, m5, m6, sums):
+    upper, lowest, highest = where_am_i()
+    end = jnp.logical_or(lowest, highest)
+    lo, hi = response("lo"), response("hi")
+    sums[...] = jnp.zeros(sums.shape, jnp.float32)
+
+    def outer_side(upper_side):
+        def tile(f, rows, cols):
+            limit = limits[f]
+            states = [jnp.where(end, 0.0, outer[f, k, rows, cols]) for k in range(FAR)]
+            for l, (raw, buf) in enumerate(((d1, b1), (d2, b2), (d3, b3))):
+                start, size = side(upper_side, l)
+                total = sums[f, l]
+                for k in range(size):
+                    j = start + k
+                    row = hi[l][DETAIL][(32 >> l) - 1 - j] if upper_side else lo[l][DETAIL][j]
+                    v = shrink(corrected(raw[f, j, rows, cols], (row, states)), LOW**l * HIGH, limit)
+                    buf[f, k, rows, cols] = v
+                    total = total + v * v
+                sums[f, l] = total
+            add_parts(lo, hi, upper_side, states, n4, n5, n6, f, rows, cols, b4, m5, m6)
+            total = sums[f, 3]
+            for j in range(4):
+                v = shrink(b4[f, j, rows, cols], LOW**3 * HIGH, limit)
+                b4[f, j, rows, cols] = v
+                total = total + v * v
+            sums[f, 3] = total
+
+        over_tiles(tile)
+
+    @pl.when(upper)
+    def _():
+        outer_side(True)
+
+    @pl.when(jnp.logical_not(upper))
+    def _():
+        outer_side(False)
+
+
+def fifth(limits, outer5, inner, relayed, m5, m6, ends, sums_a, sums_b, b5, b6, total, acc):
     upper, lowest, highest = where_am_i()
     lo, hi = response("lo")[4], response("hi")[4]
     acc[...] = jnp.zeros(acc.shape, jnp.float32)
 
-    def tile(i, _):
-        f, rows, cols = cell(i)
+    def tile(f, rows, cols):
         limit = limits[f]
         below, above = [], []
         for k in range(2):
@@ -347,17 +408,16 @@
             below.append(jnp.where(lowest, e, jnp.where(upper, n, o)))
             above.append(jnp.where(highest, e, jnp.where(upper, o, n)))
         for j in range(2):
-            d = corrected(base[f, j, rows, cols], (lo[DETAIL][j][FAR:], below), (hi[DETAIL][1 - j][FAR:], above))
+            d = corrected(m5[f, j, rows, cols], (lo[DETAIL][j][FAR:], below), (hi[DETAIL][1 - j][FAR:], above))
             d = shrink(d, LOW**4 * HIGH, limit)
             b5[f, j, rows, cols] = d
-            s = corrected(base[f, 2 + j, rows, cols], (lo[APPROX][j][FAR:], below), (hi[APPROX][1 - j][FAR:], above))
+            s = corrected(m6[f, j, rows, cols], (lo[APPROX][j][FAR:], below), (hi[APPROX][1 - j][FAR:], above))
             s = shrink(s, LOW**5, limit)
             b6[f, j, rows, cols] = s
             acc[f, 0] += d * d
             acc[f, 1] += s * s
-        return 0
-
-    lax.fori_loop(0, 16, tile, 0)
+
+    over_tiles(tile)
     lane = lax.broadcasted_iota(jnp.int32, (1, 128), 1)
     row = jnp.zeros((1, 128), jnp.float32)
     for f in range(2):
@@ -372,22 +432,47 @@
     total[...] = row
 
 
-def finish(cells, parts, b1, b2, b3, b4, b5, b6, o1_in, o2_in, o3_in, o1, o2, o3, o4, o5, o6, energy, sem):
-    copies = []
-    for f in range(2):
-        for l, (buf, out) in enumerate(((b1, o1), (b2, o2), (b3, o3))):
-            lo, hi, n = EDGE_LO[l], EDGE_HI[l], 32 >> l
-            for start, size, to in ((0, lo, 0), (lo, hi, n - hi)):
-                copies.append((buf.at[f, pl.ds(start, size)], out.at[f, pl.ds(to, size)]))
-    copies += [(b4, o4), (b5, o5), (b6, o6)]
-    copies = [pltpu.make_async_copy(a, b, sem.at[k]) for k, (a, b) in enumerate(copies)]
+def finish(cells, parts, b1, b2, b3, b4, b5, b6, o1_in, o2_in, o3_in, o1, o2, o3, o4, o5, o6, energy, row_vmem, sem):
+    upper, _, _ = where_am_i()
+    copies = [pltpu.make_async_copy(a, b, sem.at[k]) for k, (a, b) in enumerate(((b4, o4), (b5, o5), (b6, o6)))]
     for copy in copies:
         copy.start()
+
+    def outer_side(upper_side):
+        for f in range(2):
+            for l, (buf, out) in enumerate(((b1, o1), (b2, o2), (b3, o3))):
+                start, size = side(upper_side, l)
+                yield pltpu.make_async_copy(
+                    buf.at[f, pl.ds(0, size)], out.at[f, pl.ds(start, size)], sem.at[4 + 3 * f + l]
+                )
+
+    @pl.when(upper)
+    def _():
+        for copy in outer_side(True):
+            copy.start()
+
+    @pl.when(jnp.logical_not(upper))
+    def _():
+        for copy in outer_side(False):
+            copy.start()
+
     row = jnp.sum(parts[...], axis=0) * (1.0 / cells[...])
-    energy[0:1, :] = row[:, 0:6]
-    energy[1:2, :] = row[:, 6:12]
+    row_vmem[0:1, :] = row[:, 0:6]
+    row_vmem[1:2, :] = row[:, 6:12]
+    copies.append(pltpu.make_async_copy(row_vmem, energy, sem.at[3]))
+    copies[-1].start()
     for copy in copies:
         copy.wait()
+
+    @pl.when(upper)
+    def _():
+        for copy in outer_side(True):
+            copy.wait()
+
+    @pl.when(jnp.logical_not(upper))
+    def _():
+        for copy in outer_side(False):
+            copy.wait()
 
 
 def local(fields, threshold):
@@ -413,11 +498,10 @@
             input_output_aliases=aliases or {},
             compiler_params=pltpu.CompilerParams(vmem_limit_bytes=mib << 20),
             cost_estimate=pl.CostEstimate(flops=flops, bytes_accessed=1 << 20, transcendentals=0),
-            name=body.__name__,
         )
 
     count = lax.axis_size("gz")
-    across = [(i, i if i in (0, count - 1) else i + 1 if i % 2 else i - 1) for i in range(count)]
+    across = [(i, (i + 1) % count if i % 2 else (i - 1) % count) for i in range(count)]
     within = [(i, i ^ 1) for i in range(count)]
 
     outer, own5, inner, d1, d2, d3, d4, d5, s5 = call(
@@ -432,32 +516,32 @@
     inner = lax.ppermute(inner, "gz", within)
     (own5,) = call(hand_on, [vmem] * 2, [(vmem, arr(2))], [], 5_000_000, 4)(own5, inner)
     outer5 = lax.ppermute(own5, "gz", across)
-    o1, o2, o3, sums_a = call(
-        interiors,
-        [smem] + [vmem] * 4,
-        [(hbm, arr(32)), (hbm, arr(16)), (hbm, arr(8)), (vmem, tiles(3))],
-        [buf(32), buf(16), buf(8), pltpu.SemaphoreType.DMA((6,))],
+    o1, o2, o3, n4, n5, n6, ends, sums_a = call(
+        near,
+        [smem] + [vmem] * 8,
+        [(hbm, arr(32)), (hbm, arr(16)), (hbm, arr(8))] + [(vmem, arr(n)) for n in (4, 2, 2, 2)] + [(vmem, tiles(3))],
+        [buf(32), buf(16), buf(8), pltpu.VMEM((2, 3, 8, 128), f32), pltpu.SemaphoreType.DMA((12,))],
         2_000_000_000,
         8,
-    )(threshold, d1, d2, d3, own5)
+    )(threshold, d1, d2, d3, d4, d5, s5, inner, own5)
     (relayed,) = call(hand_in, [vmem] * 2, [(vmem, arr(2))], [], 5_000_000, 4)(outer, sums_a)
     received = lax.ppermute(relayed, "gz", within)
-    b1, b2, b3, b4, base, ends, sums_b = call(
+    b1, b2, b3, b4, m5, m6, sums_b = call(
         edges,
-        [smem] + [vmem] * 9,
-        [(vmem, arr(n)) for n in (3, 5, 6, 4, 4, 2)] + [(vmem, tiles(4))],
+        [smem] + [vmem] * 8,
+        [(vmem, arr(n)) for n in (2, 3, 3, 4, 2, 2)] + [(vmem, tiles(4))],
         [],
         1_000_000_000,
         4,
-    )(threshold, outer, inner, d1, d2, d3, d4, d5, s5, relayed)
+    )(threshold, outer, d1, d2, d3, n4, n5, n6, relayed)
     b5, b6, total = call(
         fifth,
-        [smem] + [vmem] * 7,
+        [smem] + [vmem] * 8,
         [(vmem, arr(2)), (vmem, arr(2)), (vmem, jax.ShapeDtypeStruct((1, 128), f32))],
         [pltpu.VMEM((2, 2, 8, 128), f32)],
         5_000_000,
         4,
-    )(threshold, outer5, inner, received, base, ends, sums_a, sums_b)
+    )(threshold, outer5, inner, received, m5, m6, ends, sums_a, sums_b)
 
     devices = count * lax.axis_size("xy")
     parts = lax.all_to_all(jnp.broadcast_to(total, (devices, 1, 128)), ("gz", "xy"), 0, 0, tiled=True)
@@ -466,8 +550,8 @@
     o1, o2, o3, o4, o5, o6, energy = call(
         finish,
         [vmem] * 8 + [hbm] * 3,
-        [(hbm, arr(n)) for n in (32, 16, 8, 4, 2, 2)] + [(vmem, jax.ShapeDtypeStruct((2, 6), f32))],
-        [pltpu.SemaphoreType.DMA((15,))],
+        [(hbm, arr(n)) for n in (32, 16, 8, 4, 2, 2)] + [(hbm, jax.ShapeDtypeStruct((2, 6), f32))],
+        [pltpu.VMEM((2, 6), f32), pltpu.SemaphoreType.DMA((10,))],
         5_000_000,
         4,
         {8: 0, 9: 1, 10: 2},
@@ -477,4 +561,9 @@
 
 def solution(mesh):
     split = P(None, "gz", "xy", None)
-    return jax.shard_map(local, mesh=mesh, in_specs=(split, P()), out_specs=(split,) * 6 + (P(),), check_vma=False)
+
+    def step(fields, threshold):
+        return local(fields, threshold)
+
+    step = jax.shard_map(step, mesh=mesh, in_specs=(split, P()), out_specs=(split,) * 6 + (P(),), check_vma=False)
+    return step

time: 50.6 us -> 46.7 us (0.923)
  waiting for transfers between devices: 2.14 us -> 5.89 us
  blocking collectives: 26.6 us -> 23.2 us
  Pallas kernels: 12 us -> 9.82 us
  starting transfers between devices: 8.93 us -> 6.89 us
    all_to_all x1, blocking collectives: 26.6 us -> 23.2 us  [local(): lax.all_to_all(jnp.broadcast_to(total, (devices, 1, 128)), ('gz', 'xy'),...]
    ppermute x1, starting transfers between devices: 3.64 us -> 0.28 us  [local(): outer5 = lax.ppermute(own5, 'gz', across)]
    ppermute x1, starting transfers between devices: 0.09 us -> 3.32 us  [local(): received = lax.ppermute(relayed, 'gz', within)]
    ppermute x1, waiting for transfers between devices: 2.13 us -> 4.16 us  [local(): outer = lax.ppermute(outer, 'gz', across)]
    ppermute x1, starting transfers between devices: 1.91 us -> 0.01 us  [local(): outer = lax.ppermute(outer, 'gz', across)]
    ppermute x1, waiting for transfers between devices: 0.01 us -> 1.72 us  [local(): inner = lax.ppermute(inner, 'gz', within)]
    pallas_call x3, Pallas kernels: 5.58 us -> 4.61 us  [the longest x1 2.48 us: local(): call(near, [smem] + [vmem] * 8, [(hbm, arr(32)), (hbm, arr(16)), (hbm, ar...]
    pallas_call x1, Pallas kernels: 1.78 us -> 1.05 us  [local(): call(finish, [vmem] * 8 + [hbm] * 3, [(hbm, arr(n)) for n in (32, 16, 8,...]
  transfers between devices with their start and end apart: 4 -> 4, of which waited for: 1 -> 2; matrix products, arithmetic and copies ran while one was open for 0% -> 0% of each run, Pallas kernels for 10% -> 9%
where the time goes in v3:
time: 46.7 us; the launch traced here: 46.6 us
  blocking collectives  23.2 us (50%)
  Pallas kernels  9.82 us (21%)
  starting transfers between devices  6.89 us (15%)
  waiting for transfers between devices  5.89 us (13%)
  between operations  0.72 us (2%)
    all_to_all x1, blocking collectives, local(): lax.all_to_all(jnp.broadcast_to(total, (devices, 1, 128)), ('gz', 'xy'),...  23.2 us
    ppermute x1, waiting for transfers between devices, local(): outer = lax.ppermute(outer, 'gz', across)  4.16 us
    pallas_call x1, Pallas kernels, local(): call(transform, [hbm], [(vmem, arr(n)) for n in (FAR, 2, ALL, 32, 16, 8,...  3.69 us
    ppermute x1, starting transfers between devices, local(): received = lax.ppermute(relayed, 'gz', within)  3.32 us
    ppermute x1, starting transfers between devices, local(): inner = lax.ppermute(inner, 'gz', within)  3.29 us
    pallas_call x1, Pallas kernels, local(): call(near, [smem] + [vmem] * 8, [(hbm, arr(32)), (hbm, arr(16)), (hbm, ar...  2.48 us
    ppermute x1, waiting for transfers between devices, local(): inner = lax.ppermute(inner, 'gz', within)  1.72 us
    pallas_call x1, Pallas kernels, local(): call(edges, [smem] + [vmem] * 8, [(vmem, arr(n)) for n in (2, 3, 3, 4, 2,...  1.15 us
  transfers between devices with their start and end apart: 4, of which 2 were waited for; matrix products, arithmetic and copies ran while one was open for 0% of the time, Pallas kernels for 9%

profile of v3, /device:TPU:1, one launch (start us, length us, event | category | flops | bytes accessed | tf_op | source)
XLA Modules:
  0.0 46.6 jit_solution(381440483126809735)
XLA Ops:
  0.6 0.0 copy-start
  0.6 3.7 %shard_map.90 = (f32[2,8,32,256]{3,2,1,0:T(8,128)S(1)}, f32[2,2,32,256]{3,2,1,0:T(8,128)S(1)}, f32[2,10,32,256]{3,2,1,0:T(8,128)S(1)}, f32[2,32,32,256]{3,2,1,0:...) custom-call(f32[2,64,32,256]{3,2,1,0:T(8,128)} %x_hbm.1), custom_call_target="tpu_custom_call" | custom-call | flops 20000000 | bytes 1048576 | tf_op jit(solution)/shard_map/pallas_call | solution.py:507
  4.3 3.3 %collective-permute-start = (f32[2,10,32,256]{3,2,1,0:T(8,128)S(1)}, f32[2,10,32,256]{3,2,1,0:T(8,128)S(1)}, u32[]{:S(2)}, u32[]{:S(2)}) collective-permute-start(f32[2,10,32,256]{3,2,1,0:T(8,128)S(1)} %get-tuple-element.35), channel_id=1, source_target_pairs={{0,8},{8,0},{16,24},{24,16},{32,40},{40,32},{48,56},{56,48},{64,72... | collective-permute-start | bytes 1966088 | tf_op jit(solution)/shard_map/ppermute | solution.py:516
  7.6 0.0 collective-permute-start.2
  7.6 1.7 %collective-permute-done.inner = f32[2,10,32,256]{3,2,1,0:T(8,128)S(1)} collective-permute-done((f32[2,10,32,256]{3,2,1,0:T(8,128)S(1)}, f32[2,10,32,256]{3,2,1,0:T(8,128)S(1)}, u32[]{:S(2)}, u32[]{:S(2)}) %collective-permute-start) | collective-permute-done | bytes 655392 | tf_op jit(solution)/shard_map/ppermute | solution.py:516
  9.4 0.2 shard_map.91.after
  9.6 0.3 collective-permute-start.1
  9.9 0.0 copy-done
  9.9 2.5 %shard_map.92 = (f32[2,32,32,256]{3,2,1,0:T(8,128)}, f32[2,16,32,256]{3,2,1,0:T(8,128)}, f32[2,8,32,256]{3,2,1,0:T(8,128)}, f32[2,4,32,256]{3,2,1,0:T(8,128)S(1)...) custom-call(f32[2]{0:T(128)S(1)} %copy-done, ...), custom_call_target="tpu_custom_call" | custom-call | flops 2000000000 | bytes 1048576 | tf_op jit(solution)/shard_map/pallas_call | solution.py:519
  12.4 4.2 %collective-permute-done.2.outer = f32[2,8,32,256]{3,2,1,0:T(8,128)S(1)} collective-permute-done((f32[2,8,32,256]{3,2,1,0:T(8,128)S(1)}, f32[2,8,32,256]{3,2,1,0:T(8,128)S(1)}, u32[]{:S(2)}, u32[]{:S(2)}) %collective-permute-start.2) | collective-permute-done | bytes 524320 | tf_op jit(solution)/shard_map/ppermute | solution.py:515
  16.5 0.2 shard_map.93.after
  16.8 3.3 %collective-permute-start.3 = (f32[2,2,32,256]{3,2,1,0:T(8,128)S(1)}, f32[2,2,32,256]{3,2,1,0:T(8,128)S(1)}, u32[]{:S(2)}, u32[]{:S(2)}) collective-permute-start(f32[2,2,32,256]{3,2,1,0:T(8,128)S(1)} %shard_map.93.after), channel_id=1, source_target_pairs={{0,8},{8,0},{16,24},{24,16},{32,40},{40,32},{48,56},{56,48},{64,72... | collective-permute-start | bytes 393224 | tf_op jit(solution)/shard_map/ppermute | solution.py:528
  20.1 0.0 copy-start.1
  20.1 1.2 %shard_map.94 = (f32[2,2,32,256]{3,2,1,0:T(8,128)S(1)}, f32[2,3,32,256]{3,2,1,0:T(8,128)S(1)}, f32[2,3,32,256]{3,2,1,0:T(8,128)S(1)}, f32[2,4,32,256]{3,2,1,0:T(...) custom-call(f32[2]{0:T(128)S(1)} %copy-done, ...), custom_call_target="tpu_custom_call" | custom-call | flops 1000000000 | bytes 1048576 | tf_op jit(solution)/shard_map/pallas_call | solution.py:529
  21.3 0.0 collective-permute-done.1.outer5
  21.3 0.0 collective-permute-done.3.relayed
  21.3 1.0 %shard_map.95 = (f32[2,2,32,256]{3,2,1,0:T(8,128)S(1)}, f32[2,2,32,256]{3,2,1,0:T(8,128)S(1)}, f32[1,128]{1,0:T(1,128)S(1)}) custom-call(f32[2]{0:T(128)S(1)} %copy-done, f32[2,2,32,256]{3,2,1,0:T(8,128)S(1)} %collective-permute-done.1.outer5, f32[2,10,32,256]{3,2,1,0:T(8,128)S(1)} %collective-permute-done.inner, ...), custom_call_target="tpu_custom_call" | custom-call | flops 5000000 | bytes 1048576 | tf_op jit(solution)/shard_map/pallas_call | solution.py:537
  22.3 0.1 broadcast_in_dim.3
  22.3 23.2 %all_to_all.5.parts = f32[256,1,128]{2,1,0:T(1,128)S(1)} all-to-all(f32[256,1,128]{2,1,0:T(1,128)S(1)} %broadcast_in_dim.3), channel_id=1, replica_groups=mesh['gz'=32,'xy'=8] {'gz','xy'}, dimensions={0} | all-to-all | bytes 262144 | tf_op jit(solution)/shard_map/all_to_all | solution.py:547
  45.6 0.0 copy-done.1
  45.6 1.0 %shard_map.96 = (f32[2,32,32,256]{3,2,1,0:T(8,128)}, f32[2,16,32,256]{3,2,1,0:T(8,128)}, f32[2,8,32,256]{3,2,1,0:T(8,128)}, f32[2,4,32,256]{3,2,1,0:T(8,128)}, f...) custom-call(f32[1,128]{1,0:T(1,128)S(1)} %copy-done.1, ...), custom_call_target="tpu_custom_call", output_to_operand_aliasing={{0}: (8, {}), {1}: (9, {}), {2}: (10, {})} | custom-call | flops 5000000 | bytes 1048576 | tf_op jit(solution)/shard_map/pallas_call | solution.py:550
Async XLA Ops:
  0.6 9.2 %copy-start = (f32[2]{0:T(128)S(1)}, f32[2]{0:T(128)}, u32[]{:S(2)}) copy-start(f32[2]{0:T(128)} %limits.5) | copy-start | bytes 28
  4.3 5.0 %collective-permute-start = (f32[2,10,32,256]{3,2,1,0:T(8,128)S(1)}, f32[2,10,32,256]{3,2,1,0:T(8,128)S(1)}, u32[]{:S(2)}, u32[]{:S(2)}) collective-permute-start(f32[2,10,32,256]{3,2,1,0:T(8,128)S(1)} %get-tuple-element.35), channel_id=1, source_target_pairs={{0,8},{8,0},{16,24},{24,16},{32,40},{40,32},{48,56},{56,48},{64,72... | collective-permute-start | bytes 1966088 | tf_op jit(solution)/shard_map/ppermute | solution.py:516
  7.6 8.9 %collective-permute-start.2 = (f32[2,8,32,256]{3,2,1,0:T(8,128)S(1)}, f32[2,8,32,256]{3,2,1,0:T(8,128)S(1)}, u32[]{:S(2)}, u32[]{:S(2)}) collective-permute-start(f32[2,8,32,256]{3,2,1,0:T(8,128)S(1)} %get-tuple-element.36), channel_id=1, source_target_pairs={{0,248},{8,16},{16,8},{24,32},{32,24},{40,48},{48,40},{56,64},{64,... | collective-permute-start | bytes 1572872 | tf_op jit(solution)/shard_map/ppermute | solution.py:515
  9.6 11.7 %collective-permute-start.1 = (f32[2,2,32,256]{3,2,1,0:T(8,128)S(1)}, f32[2,2,32,256]{3,2,1,0:T(8,128)S(1)}, u32[]{:S(2)}, u32[]{:S(2)}) collective-permute-start(f32[2,2,32,256]{3,2,1,0:T(8,128)S(1)} %shard_map.91.after), channel_id=1, source_target_pairs={{0,248},{8,16},{16,8},{24,32},{32,24},{40,48},{48,40},{56,64},{64,... | collective-permute-start | bytes 393224 | tf_op jit(solution)/shard_map/ppermute | solution.py:518
  16.8 4.5 %collective-permute-start.3 = (f32[2,2,32,256]{3,2,1,0:T(8,128)S(1)}, f32[2,2,32,256]{3,2,1,0:T(8,128)S(1)}, u32[]{:S(2)}, u32[]{:S(2)}) collective-permute-start(f32[2,2,32,256]{3,2,1,0:T(8,128)S(1)} %shard_map.93.after), channel_id=1, source_target_pairs={{0,8},{8,0},{16,24},{24,16},{32,40},{40,32},{48,56},{56,48},{64,72... | collective-permute-start | bytes 393224 | tf_op jit(solution)/shard_map/ppermute | solution.py:528
  20.1 25.5 %copy-start.1 = (f32[1,128]{1,0:T(1,128)S(1)}, f32[1,128]{1,0:T(1,128)}, u32[]{:S(2)}) copy-start(f32[1,128]{1,0:T(1,128)} %constant.2.clone.cells) | copy-start | bytes 1540

commit v4 on v3

--- a/solution.py
+++ b/solution.py
@@ -105,7 +105,7 @@
     return found
 
 
-TRANSFORM_MIB = 47
+TRANSFORM_MIB = 46
 BACK, ON, DETAIL, APPROX = range(4)
 
 
@@ -123,37 +123,55 @@
     return lax.rem(z, 2) == 1, z == 0, z == lax.axis_size("gz") - 1
 
 
-def over_tiles(body, fields=(0, 1), unroll=2):
+def over_tiles(body, fields=(0, 1)):
     for f in fields:
-
-        def step(i, carry, f=f):
-            rows = pl.ds(pl.multiple_of((i // 2) * 8, 8), 8)
-            body(f, rows, pl.ds(pl.multiple_of(lax.rem(i, 2) * 128, 128), 128))
-            return carry
-
-        lax.fori_loop(0, 8, step, 0, unroll=unroll)
-
-
-def transform(x_hbm, outer, outer5, inner, d1, d2, d3, d4, d5, s5, x_vmem, sem):
+        for rows in range(0, 32, 8):
+            for cols in range(0, 256, 128):
+                body(f, pl.ds(rows, 8), pl.ds(cols, 128))
+
+
+class Sums:
+    def __init__(self):
+        self.parts = {}
+
+    def add(self, key, v):
+        self.parts[key] = self.parts[key] + v * v if key in self.parts else v * v
+
+
+def first_half(x_hbm, outer, own5, passed, inner, d1, d2, d3, d4, d5, s5, x_next, x_vmem, sem):
+    copies = []
+    for j in range(4):
+        rows = pl.ds(8 * j, 8)
+        copies.append(pltpu.make_async_copy(x_hbm.at[0, :, rows], x_vmem.at[:, rows], sem.at[j]))
+    copies.append(pltpu.make_async_copy(x_hbm.at[1], x_next, sem.at[4]))
+    for copy in copies:
+        copy.start()
+
+    def fetched(j):
+        rows = pl.ds(pl.multiple_of(8 * j, 8), 8)
+        pltpu.make_async_copy(x_hbm.at[0, :, rows], x_vmem.at[:, rows], sem.at[j]).wait()
+
+    transform(x_vmem, outer, own5, passed, inner, (d1, d2, d3, d4, d5), s5, 0, fetched)
+    copies[4].wait()
+
+
+def second_half(*refs):
+    outer, own5, passed, inner, d1, d2, d3, d4, d5, s5 = refs[-10:]
+    transform(refs[0], outer, own5, passed, inner, (d1, d2, d3, d4, d5), s5, 1, None)
+
+
+def transform(x, outer, outer5, passed, inner, bands, s5, f, fetched):
     upper, lowest, highest = where_am_i()
-
-    def fetch(j):
-        rows = pl.ds(pl.multiple_of(lax.rem(j, 4) * 8, 8), 8)
-        at = (j // 4, slice(None), rows)
-        return pltpu.make_async_copy(x_hbm.at[at], x_vmem.at[at], sem.at[j])
-
-    for j in range(8):
-        fetch(j).start()
-    bands = (d1, d2, d3, d4, d5)
     from_above, from_below = response("hi"), response("lo")
 
     def tile(i, carry):
-        @pl.when(lax.rem(i, 2) == 0)
-        def _():
-            fetch(i // 2).wait()
-
-        f = i // 8
-        rows = pl.ds(pl.multiple_of(lax.rem(i // 2, 4) * 8, 8), 8)
+        if fetched is not None:
+
+            @pl.when(lax.rem(i, 2) == 0)
+            def _():
+                fetched(i // 2)
+
+        rows = pl.ds(pl.multiple_of((i // 2) * 8, 8), 8)
         cols = pl.ds(pl.multiple_of(lax.rem(i, 2) * 128, 128), 128)
         down, up, levels = [], [], []
 
@@ -195,17 +213,21 @@
         for l in range(LEVELS):
             levels.append(Level(32 >> l, left(l), right(l), keep(l), pass_on(l)))
         for z in range(64):
-            levels[0].push(x_vmem[f, z, rows, cols])
+            levels[0].push(x[z, rows, cols])
         for k in range(ALL):
             out = jnp.where(upper, up[k], down[k])
             if k < FAR:
-                outer[f, k, rows, cols] = out
+                outer[k, rows, cols] = out
             else:
                 outer5[f, k - FAR, rows, cols] = out
-            inner[f, k, rows, cols] = jnp.where(upper, down[k], up[k])
+        inwards = [jnp.where(upper, y, x) for x, y in zip(up, down)]
+        for k in range(ALL):
+            inner[f, k, rows, cols] = inwards[k]
+        for k, v in enumerate(through(inwards[:FAR], jnp.logical_not(upper))):
+            passed[f, k, rows, cols] = v
         return carry
 
-    lax.fori_loop(0, 16, tile, 0)
+    lax.fori_loop(0, 8, tile, 0)
 
 
 def shrink(v, scale, limit):
@@ -233,86 +255,94 @@
     return sums
 
 
-def hand_on(own5, inner, out5):
-    upper, _, _ = where_am_i()
-
-    def tile(f, rows, cols):
-        extra = through([inner[f, k, rows, cols] for k in range(FAR)], upper)
-        for k in range(2):
-            out5[f, k, rows, cols] = own5[f, k, rows, cols] + extra[k]
-
-    over_tiles(tile)
-
-
-def hand_in(outer, after, out5):
+def hand_on(own5, passed, out5):
+    out5[...] = own5[...] + passed[...]
+
+
+def hand_in(outer_a, outer_b, after, out5):
     upper, lowest, highest = where_am_i()
     end = jnp.logical_or(lowest, highest)
 
     def tile(f, rows, cols):
-        extra = through([outer[f, k, rows, cols] for k in range(FAR)], jnp.logical_not(upper))
+        extra = through([(outer_a, outer_b)[f][k, rows, cols] for k in range(FAR)], jnp.logical_not(upper))
         for k in range(2):
             out5[f, k, rows, cols] = jnp.where(end, 0.0, extra[k])
 
     over_tiles(tile)
 
 
-def add_parts(lo, hi, upper_side, states, v4, v5, v6, f, rows, cols, out4, out5, out6):
-    rows_of = hi if upper_side else lo
-    for src, dst, l, kind, n in ((v4, out4, 3, DETAIL, 4), (v5, out5, 4, DETAIL, 2), (v6, out6, 4, APPROX, 2)):
+def add_parts(lo, hi, upper_side, states, v4, v5, v6, f, rows, cols):
+    rows_of, sums = (hi if upper_side else lo), {}
+    for i, (src, l, kind, n) in enumerate(((v4, 3, DETAIL, 4), (v5, 4, DETAIL, 2), (v6, 4, APPROX, 2))):
         for j in range(n):
             row = rows_of[l][kind][n - 1 - j if upper_side else j][:FAR]
-            dst[f, j, rows, cols] = corrected(src[f, j, rows, cols], (row, states))
+            sums[i, j] = corrected(src[f, j, rows, cols], (row, states))
+    return sums
 
 
 def side(upper_side, l):
     return ((32 >> l) - EDGE_HI[l], EDGE_HI[l]) if upper_side else (0, EDGE_LO[l])
 
 
-def near(limits, d1, d2, d3, d4, d5, s5, inner, after, o1, o2, o3, n4, n5, n6, ends, sums, b1, b2, b3, acc, sem):
-    upper, lowest, highest = where_am_i()
-    lo, hi = response("lo"), response("hi")
-    pass_up = response("lo", 64)[4][ON]
-    triples = ((d1, b1, o1), (d2, b2, o2), (d3, b3, o3))
-    copies = []
+def interiors(limits, d1, d2, d3, b1, b2, b3, sums):
     for f in range(2):
         limit = limits[f]
-        for l, (raw, buf, out) in enumerate(triples):
-            first, last = EDGE_LO[l], (32 >> l) - EDGE_HI[l]
+        for l, (raw, buf) in enumerate(((d1, b1), (d2, b2), (d3, b3))):
 
             def layer(z, total, raw=raw, buf=buf, l=l):
                 v = shrink(raw[f, z], LOW**l * HIGH, limit)
                 buf[f, z] = v
                 return total + v * v
 
-            total = lax.fori_loop(first, last, layer, jnp.zeros((32, 256), jnp.float32), unroll=True)
+            zero = jnp.zeros((32, 256), jnp.float32)
+            total = lax.fori_loop(EDGE_LO[l], (32 >> l) - EDGE_HI[l], layer, zero, unroll=True)
             total = total.reshape(4, 8, 256).sum(axis=0)
-            acc[f, l] = total[:, :128] + total[:, 128:]
+            sums[f, l] = total[:, :128] + total[:, 128:]
+
+
+def near(limits, d1, d2, d3, d4, d5, s5, inner, after, c1, c2, c3, acc, o1, o2, o3, n4, n5, n6, ends, sums, e1, e2, e3, sem):
+    upper, lowest, highest = where_am_i()
+    lo, hi = response("lo"), response("hi")
+    pass_up = response("lo", 64)[4][ON]
+    triples = ((d1, e1, o1), (d2, e2, o2), (d3, e3, o3))
+    copies = []
+    for f in range(2):
+        for l, (buf, out) in enumerate(((c1, o1), (c2, o2), (c3, o3))):
+            first, last = EDGE_LO[l], (32 >> l) - EDGE_HI[l]
             at = (f, pl.ds(first, last - first))
-            copy = pltpu.make_async_copy(buf.at[at], out.at[at], sem.at[3 * f + l])
-            copy.start()
-            copies.append(copy)
+            copies.append(pltpu.make_async_copy(buf.at[at], out.at[at], sem.at[3 * f + l]))
+    for copy in copies:
+        copy.start()
 
     def inner_side(upper_side):
+        found = Sums()
+
         def tile(f, rows, cols):
             limit = limits[f]
             states = [inner[f, k, rows, cols] for k in range(FAR)]
             for l, (raw, buf, _) in enumerate(triples):
                 start, size = side(upper_side, l)
-                total = acc[f, l]
-                for j in range(start, start + size):
+                for k in range(size):
+                    j = start + k
                     row = hi[l][DETAIL][(32 >> l) - 1 - j] if upper_side else lo[l][DETAIL][j]
                     v = shrink(corrected(raw[f, j, rows, cols], (row, states)), LOW**l * HIGH, limit)
-                    buf[f, j, rows, cols] = v
-                    total = total + v * v
-                acc[f, l] = total
-            add_parts(lo, hi, upper_side, states, d4, d5, s5, f, rows, cols, n4, n5, n6)
+                    buf[f, k, rows, cols] = v
+                    found.add((f, l), v)
+            for (l, j), v in add_parts(lo, hi, upper_side, states, d4, d5, s5, f, rows, cols).items():
+                (n4, n5, n6)[l][f, j, rows, cols] = v
 
         over_tiles(tile)
+        for (f, l), part in found.parts.items():
+            sums[f, l] = acc[f, l] + part
         pieces = []
         for f in range(2):
             for l, (_, buf, out) in enumerate(triples):
-                at = (f, pl.ds(*side(upper_side, l)))
-                pieces.append(pltpu.make_async_copy(buf.at[at], out.at[at], sem.at[6 + 3 * f + l]))
+                start, size = side(upper_side, l)
+                pieces.append(
+                    pltpu.make_async_copy(
+                        buf.at[f, pl.ds(0, size)], out.at[f, pl.ds(start, size)], sem.at[6 + 3 * f + l]
+                    )
+                )
         for piece in pieces:
             piece.start()
         for piece in pieces:
@@ -349,40 +379,38 @@
     def _():
         inner_side(True)
 
-    sums[...] = acc[...]
     for copy in copies:
         copy.wait()
 
 
-def edges(limits, outer, d1, d2, d3, n4, n5, n6, after, b1, b2, b3, b4, m5, m6, sums):
+def edges(limits, outer_a, outer_b, d1, d2, d3, n4, n5, n6, after, b1, b2, b3, b4, m5, m6, sums):
     upper, lowest, highest = where_am_i()
     end = jnp.logical_or(lowest, highest)
     lo, hi = response("lo"), response("hi")
-    sums[...] = jnp.zeros(sums.shape, jnp.float32)
 
     def outer_side(upper_side):
+        found = Sums()
+
         def tile(f, rows, cols):
             limit = limits[f]
-            states = [jnp.where(end, 0.0, outer[f, k, rows, cols]) for k in range(FAR)]
+            states = [jnp.where(end, 0.0, (outer_a, outer_b)[f][k, rows, cols]) for k in range(FAR)]
             for l, (raw, buf) in enumerate(((d1, b1), (d2, b2), (d3, b3))):
                 start, size = side(upper_side, l)
-                total = sums[f, l]
                 for k in range(size):
                     j = start + k
                     row = hi[l][DETAIL][(32 >> l) - 1 - j] if upper_side else lo[l][DETAIL][j]
                     v = shrink(corrected(raw[f, j, rows, cols], (row, states)), LOW**l * HIGH, limit)
                     buf[f, k, rows, cols] = v
-                    total = total + v * v
-                sums[f, l] = total
-            add_parts(lo, hi, upper_side, states, n4, n5, n6, f, rows, cols, b4, m5, m6)
-            total = sums[f, 3]
-            for j in range(4):
-                v = shrink(b4[f, j, rows, cols], LOW**3 * HIGH, limit)
-                b4[f, j, rows, cols] = v
-                total = total + v * v
-            sums[f, 3] = total
+                    found.add((f, l), v)
+            for (i, j), v in add_parts(lo, hi, upper_side, states, n4, n5, n6, f, rows, cols).items():
+                if i == 0:
+                    v = shrink(v, LOW**3 * HIGH, limit)
+                    found.add((f, 3), v)
+                (b4, m5, m6)[i][f, j, rows, cols] = v
 
         over_tiles(tile)
+        for (f, l), part in found.parts.items():
+            sums[f, l] = part
 
     @pl.when(upper)
     def _():
@@ -393,10 +421,10 @@
         outer_side(False)
 
 
-def fifth(limits, outer5, inner, relayed, m5, m6, ends, sums_a, sums_b, b5, b6, total, acc):
+def fifth(limits, outer5, inner, relayed, m5, m6, ends, sums_a, sums_b, b5, b6, total):
     upper, lowest, highest = where_am_i()
     lo, hi = response("lo")[4], response("hi")[4]
-    acc[...] = jnp.zeros(acc.shape, jnp.float32)
+    found = Sums()
 
     def tile(f, rows, cols):
         limit = limits[f]
@@ -414,8 +442,8 @@
             s = corrected(m6[f, j, rows, cols], (lo[APPROX][j][FAR:], below), (hi[APPROX][1 - j][FAR:], above))
             s = shrink(s, LOW**5, limit)
             b6[f, j, rows, cols] = s
-            acc[f, 0] += d * d
-            acc[f, 1] += s * s
+            found.add((f, 0), d)
+            found.add((f, 1), s)
 
     over_tiles(tile)
     lane = lax.broadcasted_iota(jnp.int32, (1, 128), 1)
@@ -427,7 +455,7 @@
             elif b < 4:
                 part = sums_b[f, b]
             else:
-                part = acc[f, b - 4]
+                part = found.parts[f, b - 4]
             row = row + jnp.where(lane == 6 * f + b, jnp.sum(part), 0.0)
     total[...] = row
 
@@ -504,41 +532,56 @@
     across = [(i, (i + 1) % count if i % 2 else (i - 1) % count) for i in range(count)]
     within = [(i, i ^ 1) for i in range(count)]
 
-    outer, own5, inner, d1, d2, d3, d4, d5, s5 = call(
-        transform,
+    states = jax.ShapeDtypeStruct((FAR, 32, 256), f32)
+    kept = [(vmem, arr(n)) for n in (2, 2, ALL, 32, 16, 8, 4, 2, 2)]
+    outer_a, *half, x_next = call(
+        first_half,
         [hbm],
-        [(vmem, arr(n)) for n in (FAR, 2, ALL, 32, 16, 8, 4, 2, 2)],
-        [buf(64), pltpu.SemaphoreType.DMA((8,))],
+        [(vmem, states), *kept, (vmem, jax.ShapeDtypeStruct((64, 32, 256), f32))],
+        [pltpu.VMEM((64, 32, 256), f32), pltpu.SemaphoreType.DMA((5,))],
         20_000_000,
         TRANSFORM_MIB,
     )(fields)
-    outer = lax.ppermute(outer, "gz", across)
+    outer_a = lax.ppermute(outer_a, "gz", across)
+    outer_b, own5, passed, inner, d1, d2, d3, d4, d5, s5 = call(
+        second_half, [vmem] * 10, [(vmem, states), *kept], [], 20_000_000, 4, {1 + k: 1 + k for k in range(9)}
+    )(x_next, *half)
+    passed = lax.ppermute(passed, "gz", within)
+    outer_b = lax.ppermute(outer_b, "gz", across)
+    (own5,) = call(hand_on, [vmem] * 2, [(vmem, arr(2))], [], 5_000_000, 4)(own5, passed)
+    outer5 = lax.ppermute(own5, "gz", across)
     inner = lax.ppermute(inner, "gz", within)
-    (own5,) = call(hand_on, [vmem] * 2, [(vmem, arr(2))], [], 5_000_000, 4)(own5, inner)
-    outer5 = lax.ppermute(own5, "gz", across)
+    c1, c2, c3, sums_c = call(
+        interiors,
+        [smem] + [vmem] * 3,
+        [(vmem, arr(n)) for n in (32, 16, 8)] + [(vmem, tiles(3))],
+        [],
+        20_000_000,
+        4,
+    )(threshold, d1, d2, d3)
     o1, o2, o3, n4, n5, n6, ends, sums_a = call(
         near,
-        [smem] + [vmem] * 8,
+        [smem] + [vmem] * 12,
         [(hbm, arr(32)), (hbm, arr(16)), (hbm, arr(8))] + [(vmem, arr(n)) for n in (4, 2, 2, 2)] + [(vmem, tiles(3))],
-        [buf(32), buf(16), buf(8), pltpu.VMEM((2, 3, 8, 128), f32), pltpu.SemaphoreType.DMA((12,))],
+        [buf(3), buf(3), buf(3), pltpu.SemaphoreType.DMA((12,))],
         2_000_000_000,
         8,
-    )(threshold, d1, d2, d3, d4, d5, s5, inner, own5)
-    (relayed,) = call(hand_in, [vmem] * 2, [(vmem, arr(2))], [], 5_000_000, 4)(outer, sums_a)
+    )(threshold, d1, d2, d3, d4, d5, s5, inner, own5, c1, c2, c3, sums_c)
+    (relayed,) = call(hand_in, [vmem] * 3, [(vmem, arr(2))], [], 5_000_000, 4)(outer_a, outer_b, sums_a)
     received = lax.ppermute(relayed, "gz", within)
     b1, b2, b3, b4, m5, m6, sums_b = call(
         edges,
-        [smem] + [vmem] * 8,
+        [smem] + [vmem] * 9,
         [(vmem, arr(n)) for n in (2, 3, 3, 4, 2, 2)] + [(vmem, tiles(4))],
         [],
         1_000_000_000,
         4,
-    )(threshold, outer, d1, d2, d3, n4, n5, n6, relayed)
+    )(threshold, outer_a, outer_b, d1, d2, d3, n4, n5, n6, relayed)
     b5, b6, total = call(
         fifth,
         [smem] + [vmem] * 8,
         [(vmem, arr(2)), (vmem, arr(2)), (vmem, jax.ShapeDtypeStruct((1, 128), f32))],
-        [pltpu.VMEM((2, 2, 8, 128), f32)],
+        [],
         5_000_000,
         4,
     )(threshold, outer5, inner, received, m5, m6, ends, sums_a, sums_b)

time: 46.7 us -> 46.8 us (level)
  starting transfers between devices: 6.89 us -> 9.81 us
  waiting for transfers between devices: 5.89 us -> 3.44 us
  blocking collectives: 23.2 us -> 22.6 us
    ppermute x1 -> x3, starting transfers between devices: 0.01 us -> 1.85 us  [the longest x1 1.52 us: local(): outer_a = lax.ppermute(outer_a, 'gz', across)]
    ppermute x1, waiting for transfers between devices: 1.72 us -> 0.01 us  [local(): inner = lax.ppermute(inner, 'gz', within)]
    ppermute x1, starting transfers between devices: 3.32 us -> 4.37 us  [local(): received = lax.ppermute(relayed, 'gz', within)]
    ppermute x1 -> x3, waiting for transfers between devices: 4.16 us -> 3.43 us  [the longest x1 3.1 us: local(): outer_a = lax.ppermute(outer_a, 'gz', across)]
    all_to_all x1, blocking collectives: 23.2 us -> 22.6 us  [local(): lax.all_to_all(jnp.broadcast_to(total, (devices, 1, 128)), ('gz', 'xy'),...]
    pallas_call x5 -> x7, Pallas kernels: 7.8 us -> 8.1 us  [the longest x1 2.34 us: local(): call(first_half, [hbm], [(vmem, states), *kept, (vmem, jax.ShapeDtypeStru...]
  transfers between devices with their start and end apart: 4 -> 6, of which waited for: 2 -> 2; matrix products, arithmetic and copies ran while one was open for 0% -> 0% of each run, Pallas kernels for 9% -> 10%
where the time goes in v4:
time: 46.8 us; the launch traced here: 46.6 us
  blocking collectives  22.6 us (48%)
  Pallas kernels  9.97 us (21%)
  starting transfers between devices  9.81 us (21%)
  waiting for transfers between devices  3.44 us (7%)
  between operations  0.73 us (2%)
    all_to_all x1, blocking collectives, local(): lax.all_to_all(jnp.broadcast_to(total, (devices, 1, 128)), ('gz', 'xy'),...  22.6 us
    ppermute x1, starting transfers between devices, local(): received = lax.ppermute(relayed, 'gz', within)  4.37 us
    ppermute x1, starting transfers between devices, local(): inner = lax.ppermute(inner, 'gz', within)  3.29 us
    ppermute x1, waiting for transfers between devices, local(): outer_a = lax.ppermute(outer_a, 'gz', across)  3.1 us
    pallas_call x1, Pallas kernels, local(): call(first_half, [hbm], [(vmem, states), *kept, (vmem, jax.ShapeDtypeStru...  2.34 us
    pallas_call x1, Pallas kernels, local(): call(near, [smem] + [vmem] * 12, [(hbm, arr(32)), (hbm, arr(16)), (hbm, a...  2.3 us
    ppermute x1, starting transfers between devices, local(): outer_a = lax.ppermute(outer_a, 'gz', across)  1.52 us
    pallas_call x1, Pallas kernels, local(): call(second_half, [vmem] * 10, [(vmem, states), *kept], [], 20000000, 4,...  1.27 us
  transfers between devices with their start and end apart: 6, of which 2 were waited for; matrix products, arithmetic and copies ran while one was open for 0% of the time, Pallas kernels for 10%

profile of v4, /device:TPU:1, one launch (start us, length us, event | category | flops | bytes accessed | tf_op | source)
XLA Modules:
  0.0 46.6 jit_solution(4993574791838337208)
XLA Ops:
  0.6 2.3 %shard_map.90 = (f32[8,32,256]{2,1,0:T(8,128)S(1)}, f32[2,2,32,256]{3,2,1,0:T(8,128)S(1)}, f32[2,2,32,256]{3,2,1,0:T(8,128)S(1)}, f32[2,10,32,256]{3,2,1,0:T(8,1...) custom-call(f32[2,64,32,256]{3,2,1,0:T(8,128)} %x_hbm.1), custom_call_target="tpu_custom_call" | custom-call | flops 20000000 | bytes 1048576 | tf_op jit(solution)/shard_map/pallas_call | solution.py:537
  3.0 0.0 copy-start
  3.0 1.3 %shard_map.91 = (f32[8,32,256]{2,1,0:T(8,128)S(1)}, f32[2,2,32,256]{3,2,1,0:T(8,128)S(1)}, f32[2,2,32,256]{3,2,1,0:T(8,128)S(1)}, f32[2,10,32,256]{3,2,1,0:T(8,1...) custom-call(f32[64,32,256]{2,1,0:T(8,128)S(1)} %get-tuple-element.50, ...), custom_call_target="tpu_custom_call", output_to_operand_aliasing={{1}: (1, {}), {2}: (2, {}), {3}: (3, {}), {4}: (4, {}), {5}... | custom-call | flops 20000000 | bytes 1048576 | tf_op jit(solution)/shard_map/pallas_call | solution.py:546
  4.3 3.3 %collective-permute-start.2 = (f32[2,10,32,256]{3,2,1,0:T(8,128)S(1)}, f32[2,10,32,256]{3,2,1,0:T(8,128)S(1)}, u32[]{:S(2)}, u32[]{:S(2)}) collective-permute-start(f32[2,10,32,256]{3,2,1,0:T(8,128)S(1)} %get-tuple-element.62), channel_id=1, source_target_pairs={{0,8},{8,0},{16,24},{24,16},{32,40},{40,32},{48,56},{56,48},{64,72... | collective-permute-start | bytes 1966088 | tf_op jit(solution)/shard_map/ppermute | solution.py:553
  7.6 0.1 collective-permute-start
  7.7 0.2 collective-permute-start.4
  7.9 1.5 %collective-permute-start.3 = (f32[8,32,256]{2,1,0:T(8,128)S(1)}, f32[8,32,256]{2,1,0:T(8,128)S(1)}, u32[]{:S(2)}, u32[]{:S(2)}) collective-permute-start(f32[8,32,256]{2,1,0:T(8,128)S(1)} %get-tuple-element.63), channel_id=1, source_target_pairs={{0,248},{8,16},{16,8},{24,32},{32,24},{40,48},{48,40},{56,64},{64,... | collective-permute-start | bytes 786440 | tf_op jit(solution)/shard_map/ppermute | solution.py:545
  9.4 0.0 copy-done
  9.4 1.1 %shard_map.93 = (f32[2,32,32,256]{3,2,1,0:T(8,128)S(1)}, f32[2,16,32,256]{3,2,1,0:T(8,128)S(1)}, f32[2,8,32,256]{3,2,1,0:T(8,128)S(1)}, f32[2,3,8,128]{3,2,1,0:T(8,128)S(1)}) custom-call(f32[2]{0:T(128)S(1)} %copy-done, f32[2,32,32,256]{3,2,1,0:T(8,128)S(1)} %get-tuple-element.65.d1, f32[2,16,32,256]{3,2,1,0:T(8,128)S(1)} %get-tuple-element.66.d2, ...), custom_call_target="tpu_custom_call" | custom-call | flops 20000000 | bytes 1048576 | tf_op jit(solution)/shard_map/pallas_call | solution.py:554
  10.5 0.0 collective-permute-done.passed
  10.5 0.3 collective-permute-start.1
  10.8 0.0 collective-permute-done.2.inner
  10.8 2.3 %shard_map.94 = (f32[2,32,32,256]{3,2,1,0:T(8,128)}, f32[2,16,32,256]{3,2,1,0:T(8,128)}, f32[2,8,32,256]{3,2,1,0:T(8,128)}, f32[2,4,32,256]{3,2,1,0:T(8,128)S(1)...) custom-call(f32[2]{0:T(128)S(1)} %copy-done, ...), custom_call_target="tpu_custom_call" | custom-call | flops 2000000000 | bytes 1048576 | tf_op jit(solution)/shard_map/pallas_call | solution.py:562
  13.1 0.3 collective-permute-done.4.outer_b
  13.5 3.1 %collective-permute-done.3.outer_a = f32[8,32,256]{2,1,0:T(8,128)S(1)} collective-permute-done((f32[8,32,256]{2,1,0:T(8,128)S(1)}, f32[8,32,256]{2,1,0:T(8,128)S(1)}, u32[]{:S(2)}, u32[]{:S(2)}) %collective-permute-start.3) | collective-permute-done | bytes 262176 | tf_op jit(solution)/shard_map/ppermute | solution.py:545
  16.6 0.1 shard_map.95.after
  16.6 4.4 %collective-permute-start.5 = (f32[2,2,32,256]{3,2,1,0:T(8,128)S(1)}, f32[2,2,32,256]{3,2,1,0:T(8,128)S(1)}, u32[]{:S(2)}, u32[]{:S(2)}) collective-permute-start(f32[2,2,32,256]{3,2,1,0:T(8,128)S(1)} %shard_map.95.after), channel_id=1, source_target_pairs={{0,8},{8,0},{16,24},{24,16},{32,40},{40,32},{48,56},{56,48},{64,72... | collective-permute-start | bytes 393224 | tf_op jit(solution)/shard_map/ppermute | solution.py:571
  21.0 0.0 copy-start.1
  21.0 1.0 %shard_map.96 = (f32[2,2,32,256]{3,2,1,0:T(8,128)S(1)}, f32[2,3,32,256]{3,2,1,0:T(8,128)S(1)}, f32[2,3,32,256]{3,2,1,0:T(8,128)S(1)}, f32[2,4,32,256]{3,2,1,0:T(...) custom-call(f32[2]{0:T(128)S(1)} %copy-done, ...), custom_call_target="tpu_custom_call" | custom-call | flops 1000000000 | bytes 1048576 | tf_op jit(solution)/shard_map/pallas_call | solution.py:572
  22.1 0.0 collective-permute-done.1.outer5
  22.1 0.0 collective-permute-done.5.relayed
  22.1 0.8 %shard_map.97 = (f32[2,2,32,256]{3,2,1,0:T(8,128)S(1)}, f32[2,2,32,256]{3,2,1,0:T(8,128)S(1)}, f32[1,128]{1,0:T(1,128)S(1)}) custom-call(f32[2]{0:T(128)S(1)} %copy-done, f32[2,2,32,256]{3,2,1,0:T(8,128)S(1)} %collective-permute-done.1.outer5, f32[2,10,32,256]{3,2,1,0:T(8,128)S(1)} %collective-permute-done.2.inner, ...), custom_call_target="tpu_custom_call" | custom-call | flops 5000000 | bytes 1048576 | tf_op jit(solution)/shard_map/pallas_call | solution.py:580
  22.9 0.1 broadcast_in_dim.3
  23.0 22.6 %all_to_all.5.parts = f32[256,1,128]{2,1,0:T(1,128)S(1)} all-to-all(f32[256,1,128]{2,1,0:T(1,128)S(1)} %broadcast_in_dim.3), channel_id=1, replica_groups=mesh['gz'=32,'xy'=8] {'gz','xy'}, dimensions={0} | all-to-all | bytes 262144 | tf_op jit(solution)/shard_map/all_to_all | solution.py:590
  45.6 0.0 copy-done.1
  45.6 1.0 %shard_map.98 = (f32[2,32,32,256]{3,2,1,0:T(8,128)}, f32[2,16,32,256]{3,2,1,0:T(8,128)}, f32[2,8,32,256]{3,2,1,0:T(8,128)}, f32[2,4,32,256]{3,2,1,0:T(8,128)}, f...) custom-call(f32[1,128]{1,0:T(1,128)S(1)} %copy-done.1, ...), custom_call_target="tpu_custom_call", output_to_operand_aliasing={{0}: (8, {}), {1}: (9, {}), {2}: (10, {})} | custom-call | flops 5000000 | bytes 1048576 | tf_op jit(solution)/shard_map/pallas_call | solution.py:593
  (1 shorter events, 0.0 us)
Async XLA Ops:
  3.0 6.4 %copy-start = (f32[2]{0:T(128)S(1)}, f32[2]{0:T(128)}, u32[]{:S(2)}) copy-start(f32[2]{0:T(128)} %limits.7) | copy-start | bytes 28
  4.3 6.6 %collective-permute-start.2 = (f32[2,10,32,256]{3,2,1,0:T(8,128)S(1)}, f32[2,10,32,256]{3,2,1,0:T(8,128)S(1)}, u32[]{:S(2)}, u32[]{:S(2)}) collective-permute-start(f32[2,10,32,256]{3,2,1,0:T(8,128)S(1)} %get-tuple-element.62), channel_id=1, source_target_pairs={{0,8},{8,0},{16,24},{24,16},{32,40},{40,32},{48,56},{56,48},{64,72... | collective-permute-start | bytes 1966088 | tf_op jit(solution)/shard_map/ppermute | solution.py:553
  7.6 2.9 %collective-permute-start = (f32[2,2,32,256]{3,2,1,0:T(8,128)S(1)}, f32[2,2,32,256]{3,2,1,0:T(8,128)S(1)}, u32[]{:S(2)}, u32[]{:S(2)}) collective-permute-start(f32[2,2,32,256]{3,2,1,0:T(8,128)S(1)} %get-tuple-element.61), channel_id=1, source_target_pairs={{0,8},{8,0},{16,24},{24,16},{32,40},{40,32},{48,56},{56,48},{64,72... | collective-permute-start | bytes 393224 | tf_op jit(solution)/shard_map/ppermute | solution.py:549
  7.7 5.8 %collective-permute-start.4 = (f32[8,32,256]{2,1,0:T(8,128)S(1)}, f32[8,32,256]{2,1,0:T(8,128)S(1)}, u32[]{:S(2)}, u32[]{:S(2)}) collective-permute-start(f32[8,32,256]{2,1,0:T(8,128)S(1)} %get-tuple-element.64), channel_id=1, source_target_pairs={{0,248},{8,16},{16,8},{24,32},{32,24},{40,48},{48,40},{56,64},{64,... | collective-permute-start | bytes 786440 | tf_op jit(solution)/shard_map/ppermute | solution.py:550
  7.9 8.7 %collective-permute-start.3 = (f32[8,32,256]{2,1,0:T(8,128)S(1)}, f32[8,32,256]{2,1,0:T(8,128)S(1)}, u32[]{:S(2)}, u32[]{:S(2)}) collective-permute-start(f32[8,32,256]{2,1,0:T(8,128)S(1)} %get-tuple-element.63), channel_id=1, source_target_pairs={{0,248},{8,16},{16,8},{24,32},{32,24},{40,48},{48,40},{56,64},{64,... | collective-permute-start | bytes 786440 | tf_op jit(solution)/shard_map/ppermute | solution.py:545
  10.5 11.6 %collective-permute-start.1 = (f32[2,2,32,256]{3,2,1,0:T(8,128)S(1)}, f32[2,2,32,256]{3,2,1,0:T(8,128)S(1)}, u32[]{:S(2)}, u32[]{:S(2)}) collective-permute-start(f32[2,2,32,256]{3,2,1,0:T(8,128)S(1)} %shard_map.92.after), channel_id=1, source_target_pairs={{0,248},{8,16},{16,8},{24,32},{32,24},{40,48},{48,40},{56,64},{64,... | collective-permute-start | bytes 393224 | tf_op jit(solution)/shard_map/ppermute | solution.py:552
  16.6 5.4 %collective-permute-start.5 = (f32[2,2,32,256]{3,2,1,0:T(8,128)S(1)}, f32[2,2,32,256]{3,2,1,0:T(8,128)S(1)}, u32[]{:S(2)}, u32[]{:S(2)}) collective-permute-start(f32[2,2,32,256]{3,2,1,0:T(8,128)S(1)} %shard_map.95.after), channel_id=1, source_target_pairs={{0,8},{8,0},{16,24},{24,16},{32,40},{40,32},{48,56},{56,48},{64,72... | collective-permute-start | bytes 393224 | tf_op jit(solution)/shard_map/ppermute | solution.py:571
  21.0 24.6 %copy-start.1 = (f32[1,128]{1,0:T(1,128)S(1)}, f32[1,128]{1,0:T(1,128)}, u32[]{:S(2)}) copy-start(f32[1,128]{1,0:T(1,128)} %constant.2.clone.cells) | copy-start | bytes 1540

commit v5 on v4

--- a/solution.py
+++ b/solution.py
@@ -284,35 +284,45 @@
     return ((32 >> l) - EDGE_HI[l], EDGE_HI[l]) if upper_side else (0, EDGE_LO[l])
 
 
-def interiors(limits, d1, d2, d3, b1, b2, b3, sums):
+def interiors(limits, d1, d2, d3, o1, o2, o3, sums, limit_tiles, b1, b2, b3, sem):
+    copies = []
     for f in range(2):
-        limit = limits[f]
-        for l, (raw, buf) in enumerate(((d1, b1), (d2, b2), (d3, b3))):
-
-            def layer(z, total, raw=raw, buf=buf, l=l):
+        limit_tiles[f] = jnp.full((8, 128), limits[f], jnp.float32)
+    for l, (raw, buf, out) in enumerate(((d1, b1, o1), (d2, b2, o2), (d3, b3, o3))):
+        first, last = EDGE_LO[l], (32 >> l) - EDGE_HI[l]
+        for f in range(2):
+            limit = limits[f]
+
+            def layer(z, total, raw=raw, buf=buf, l=l, f=f, limit=limit):
                 v = shrink(raw[f, z], LOW**l * HIGH, limit)
                 buf[f, z] = v
                 return total + v * v
 
-            zero = jnp.zeros((32, 256), jnp.float32)
-            total = lax.fori_loop(EDGE_LO[l], (32 >> l) - EDGE_HI[l], layer, zero, unroll=True)
+            total = lax.fori_loop(first, last, layer, jnp.zeros((32, 256), jnp.float32), unroll=True)
+            at = (f, pl.ds(first, last - first))
+            copy = pltpu.make_async_copy(buf.at[at], out.at[at], sem.at[3 * f + l])
+            copy.start()
+            copies.append(copy)
             total = total.reshape(4, 8, 256).sum(axis=0)
             sums[f, l] = total[:, :128] + total[:, 128:]
-
-
-def near(limits, d1, d2, d3, d4, d5, s5, inner, after, c1, c2, c3, acc, o1, o2, o3, n4, n5, n6, ends, sums, e1, e2, e3, sem):
+    for copy in copies:
+        copy.wait()
+
+
+def pieces(pairs, upper_side, sem, base):
+    for f in range(2):
+        for l, (buf, out) in enumerate(pairs):
+            start, size = side(upper_side, l)
+            yield pltpu.make_async_copy(
+                buf.at[f, pl.ds(0, size)], out.at[f, pl.ds(start, size)], sem.at[base + 3 * f + l]
+            )
+
+
+def near(limits, d1, d2, d3, d4, d5, s5, inner, after, acc, e1, e2, e3, n4, n5, n6, ends, sums):
     upper, lowest, highest = where_am_i()
     lo, hi = response("lo"), response("hi")
     pass_up = response("lo", 64)[4][ON]
-    triples = ((d1, e1, o1), (d2, e2, o2), (d3, e3, o3))
-    copies = []
-    for f in range(2):
-        for l, (buf, out) in enumerate(((c1, o1), (c2, o2), (c3, o3))):
-            first, last = EDGE_LO[l], (32 >> l) - EDGE_HI[l]
-            at = (f, pl.ds(first, last - first))
-            copies.append(pltpu.make_async_copy(buf.at[at], out.at[at], sem.at[3 * f + l]))
-    for copy in copies:
-        copy.start()
+    triples = ((d1, e1), (d2, e2), (d3, e3))
 
     def inner_side(upper_side):
         found = Sums()
@@ -320,7 +330,7 @@
         def tile(f, rows, cols):
             limit = limits[f]
             states = [inner[f, k, rows, cols] for k in range(FAR)]
-            for l, (raw, buf, _) in enumerate(triples):
+            for l, (raw, buf) in enumerate(triples):
                 start, size = side(upper_side, l)
                 for k in range(size):
                     j = start + k
@@ -334,19 +344,6 @@
         over_tiles(tile)
         for (f, l), part in found.parts.items():
             sums[f, l] = acc[f, l] + part
-        pieces = []
-        for f in range(2):
-            for l, (_, buf, out) in enumerate(triples):
-                start, size = side(upper_side, l)
-                pieces.append(
-                    pltpu.make_async_copy(
-                        buf.at[f, pl.ds(0, size)], out.at[f, pl.ds(start, size)], sem.at[6 + 3 * f + l]
-                    )
-                )
-        for piece in pieces:
-            piece.start()
-        for piece in pieces:
-            piece.wait()
 
     @pl.when(jnp.logical_not(jnp.logical_or(lowest, highest)))
     def _():
@@ -379,17 +376,20 @@
     def _():
         inner_side(True)
 
-    for copy in copies:
-        copy.wait()
-
-
-def edges(limits, outer_a, outer_b, d1, d2, d3, n4, n5, n6, after, b1, b2, b3, b4, m5, m6, sums):
+
+def edges(
+    limits, outer_a, outer_b, d1, d2, d3, n4, n5, n6, after, e1, e2, e3, o1_in, o2_in, o3_in,
+    b1, b2, b3, b4, m5, m6, sums, o1, o2, o3, sem,
+):
     upper, lowest, highest = where_am_i()
     end = jnp.logical_or(lowest, highest)
     lo, hi = response("lo"), response("hi")
 
     def outer_side(upper_side):
         found = Sums()
+        copies = [*pieces(((e1, o1), (e2, o2), (e3, o3)), not upper_side, sem, 0)]
+        for copy in copies:
+            copy.start()
 
         def tile(f, rows, cols):
             limit = limits[f]
@@ -411,6 +411,8 @@
         over_tiles(tile)
         for (f, l), part in found.parts.items():
             sums[f, l] = part
+        for copy in copies:
+            copy.wait()
 
     @pl.when(upper)
     def _():
@@ -419,6 +421,10 @@
     @pl.when(jnp.logical_not(upper))
     def _():
         outer_side(False)
+
+
+def total_of(part):
+    return jnp.sum(jnp.sum(part, axis=0, keepdims=True), axis=1, keepdims=True)
 
 
 def fifth(limits, outer5, inner, relayed, m5, m6, ends, sums_a, sums_b, b5, b6, total):
@@ -456,7 +462,7 @@
                 part = sums_b[f, b]
             else:
                 part = found.parts[f, b - 4]
-            row = row + jnp.where(lane == 6 * f + b, jnp.sum(part), 0.0)
+            row = row + jnp.where(lane == 6 * f + b, total_of(part), 0.0)
     total[...] = row
 
 
@@ -467,12 +473,7 @@
         copy.start()
 
     def outer_side(upper_side):
-        for f in range(2):
-            for l, (buf, out) in enumerate(((b1, o1), (b2, o2), (b3, o3))):
-                start, size = side(upper_side, l)
-                yield pltpu.make_async_copy(
-                    buf.at[f, pl.ds(0, size)], out.at[f, pl.ds(start, size)], sem.at[4 + 3 * f + l]
-                )
+        return pieces(((b1, o1), (b2, o2), (b3, o3)), upper_side, sem, 4)
 
     @pl.when(upper)
     def _():
@@ -551,40 +552,41 @@
     (own5,) = call(hand_on, [vmem] * 2, [(vmem, arr(2))], [], 5_000_000, 4)(own5, passed)
     outer5 = lax.ppermute(own5, "gz", across)
     inner = lax.ppermute(inner, "gz", within)
-    c1, c2, c3, sums_c = call(
+    o1, o2, o3, sums_c, limits = call(
         interiors,
         [smem] + [vmem] * 3,
-        [(vmem, arr(n)) for n in (32, 16, 8)] + [(vmem, tiles(3))],
+        [(hbm, arr(n)) for n in (32, 16, 8)] + [(vmem, tiles(3)), (vmem, jax.ShapeDtypeStruct((2, 8, 128), f32))],
+        [buf(32), buf(16), buf(8), pltpu.SemaphoreType.DMA((6,))],
+        20_000_000,
+        8,
+    )(threshold, d1, d2, d3)
+    e1, e2, e3, n4, n5, n6, ends, sums_a = call(
+        near,
+        [vmem] * 10,
+        [(vmem, arr(n)) for n in (3, 3, 3, 4, 2, 2, 2)] + [(vmem, tiles(3))],
         [],
-        20_000_000,
+        2_000_000_000,
         4,
-    )(threshold, d1, d2, d3)
-    o1, o2, o3, n4, n5, n6, ends, sums_a = call(
-        near,
-        [smem] + [vmem] * 12,
-        [(hbm, arr(32)), (hbm, arr(16)), (hbm, arr(8))] + [(vmem, arr(n)) for n in (4, 2, 2, 2)] + [(vmem, tiles(3))],
-        [buf(3), buf(3), buf(3), pltpu.SemaphoreType.DMA((12,))],
-        2_000_000_000,
-        8,
-    )(threshold, d1, d2, d3, d4, d5, s5, inner, own5, c1, c2, c3, sums_c)
+    )(limits, d1, d2, d3, d4, d5, s5, inner, own5, sums_c)
     (relayed,) = call(hand_in, [vmem] * 3, [(vmem, arr(2))], [], 5_000_000, 4)(outer_a, outer_b, sums_a)
     received = lax.ppermute(relayed, "gz", within)
-    b1, b2, b3, b4, m5, m6, sums_b = call(
+    b1, b2, b3, b4, m5, m6, sums_b, o1, o2, o3 = call(
         edges,
-        [smem] + [vmem] * 9,
-        [(vmem, arr(n)) for n in (2, 3, 3, 4, 2, 2)] + [(vmem, tiles(4))],
-        [],
+        [vmem] * 13 + [hbm] * 3,
+        [(vmem, arr(n)) for n in (2, 3, 3, 4, 2, 2)] + [(vmem, tiles(4))] + [(hbm, arr(n)) for n in (32, 16, 8)],
+        [pltpu.SemaphoreType.DMA((6,))],
         1_000_000_000,
         4,
-    )(threshold, outer_a, outer_b, d1, d2, d3, n4, n5, n6, relayed)
+        {13: 7, 14: 8, 15: 9},
+    )(limits, outer_a, outer_b, d1, d2, d3, n4, n5, n6, relayed, e1, e2, e3, o1, o2, o3)
     b5, b6, total = call(
         fifth,
-        [smem] + [vmem] * 8,
+        [vmem] * 9,
         [(vmem, arr(2)), (vmem, arr(2)), (vmem, jax.ShapeDtypeStruct((1, 128), f32))],
         [],
         5_000_000,
         4,
-    )(threshold, outer5, inner, received, m5, m6, ends, sums_a, sums_b)
+    )(limits, outer5, inner, received, m5, m6, ends, sums_a, sums_b)
 
     devices = count * lax.axis_size("xy")
     parts = lax.all_to_all(jnp.broadcast_to(total, (devices, 1, 128)), ("gz", "xy"), 0, 0, tiled=True)

time: 46.8 us -> 46.1 us (0.985)
  Pallas kernels: 9.97 us -> 8.44 us
  waiting for transfers between devices: 3.44 us -> 4.3 us
    pallas_call x4, Pallas kernels: 5.21 us -> 3.68 us  [the longest x1 2.29 us: local(): call(interiors, [smem] + [vmem] * 3, [(hbm, arr(n)) for n in (32, 16, 8)]...]
    ppermute x1, waiting for transfers between devices: 0.33 us -> 1.01 us  [local(): outer_b = lax.ppermute(outer_b, 'gz', across)]
  transfers between devices with their start and end apart: 6 -> 6, of which waited for: 2 -> 3; matrix products, arithmetic and copies ran while one was open for 0% -> 0% of each run, Pallas kernels for 10% -> 8%
where the time goes in v5:
time: 46.1 us; the launch traced here: 46 us
  blocking collectives  22.7 us (49%)
  starting transfers between devices  9.81 us (21%)
  Pallas kernels  8.44 us (18%)
  waiting for transfers between devices  4.3 us (9%)
  between operations  0.71 us (2%)
    all_to_all x1, blocking collectives, local(): lax.all_to_all(jnp.broadcast_to(total, (devices, 1, 128)), ('gz', 'xy'),...  22.7 us
    ppermute x1, starting transfers between devices, local(): received = lax.ppermute(relayed, 'gz', within)  4.37 us
    ppermute x1, starting transfers between devices, local(): inner = lax.ppermute(inner, 'gz', within)  3.29 us
    ppermute x1, waiting for transfers between devices, local(): outer_a = lax.ppermute(outer_a, 'gz', across)  3.1 us
    pallas_call x1, Pallas kernels, local(): call(first_half, [hbm], [(vmem, states), *kept, (vmem, jax.ShapeDtypeStru...  2.34 us
    pallas_call x1, Pallas kernels, local(): call(interiors, [smem] + [vmem] * 3, [(hbm, arr(n)) for n in (32, 16, 8)]...  2.29 us
    ppermute x1, starting transfers between devices, local(): outer_a = lax.ppermute(outer_a, 'gz', across)  1.52 us
    pallas_call x1, Pallas kernels, local(): call(second_half, [vmem] * 10, [(vmem, states), *kept], [], 20000000, 4,...  1.27 us
  transfers between devices with their start and end apart: 6, of which 3 were waited for; matrix products, arithmetic and copies ran while one was open for 0% of the time, Pallas kernels for 8%

profile of v5, /device:TPU:1, one launch (start us, length us, event | category | flops | bytes accessed | tf_op | source)
XLA Modules:
  0.0 46.0 jit_solution(12338191386669171623)
XLA Ops:
  0.6 2.3 %shard_map.90 = (f32[8,32,256]{2,1,0:T(8,128)S(1)}, f32[2,2,32,256]{3,2,1,0:T(8,128)S(1)}, f32[2,2,32,256]{3,2,1,0:T(8,128)S(1)}, f32[2,10,32,256]{3,2,1,0:T(8,1...) custom-call(f32[2,64,32,256]{3,2,1,0:T(8,128)} %x_hbm.1), custom_call_target="tpu_custom_call" | custom-call | flops 20000000 | bytes 1048576 | tf_op jit(solution)/shard_map/pallas_call | solution.py:538
  3.0 0.0 copy-start.1
  3.0 1.3 %shard_map.91 = (f32[8,32,256]{2,1,0:T(8,128)S(1)}, f32[2,2,32,256]{3,2,1,0:T(8,128)S(1)}, f32[2,2,32,256]{3,2,1,0:T(8,128)S(1)}, f32[2,10,32,256]{3,2,1,0:T(8,1...) custom-call(f32[64,32,256]{2,1,0:T(8,128)S(1)} %get-tuple-element.54, ...), custom_call_target="tpu_custom_call", output_to_operand_aliasing={{1}: (1, {}), {2}: (2, {}), {3}: (3, {}), {4}: (4, {}), {5}... | custom-call | flops 20000000 | bytes 1048576 | tf_op jit(solution)/shard_map/pallas_call | solution.py:547
  4.3 3.3 %collective-permute-start.2 = (f32[2,10,32,256]{3,2,1,0:T(8,128)S(1)}, f32[2,10,32,256]{3,2,1,0:T(8,128)S(1)}, u32[]{:S(2)}, u32[]{:S(2)}) collective-permute-start(f32[2,10,32,256]{3,2,1,0:T(8,128)S(1)} %get-tuple-element.70), channel_id=1, source_target_pairs={{0,8},{8,0},{16,24},{24,16},{32,40},{40,32},{48,56},{56,48},{64,72... | collective-permute-start | bytes 1966088 | tf_op jit(solution)/shard_map/ppermute | solution.py:554
  7.6 0.1 collective-permute-start
  7.7 0.2 collective-permute-start.4
  7.9 1.5 %collective-permute-start.3 = (f32[8,32,256]{2,1,0:T(8,128)S(1)}, f32[8,32,256]{2,1,0:T(8,128)S(1)}, u32[]{:S(2)}, u32[]{:S(2)}) collective-permute-start(f32[8,32,256]{2,1,0:T(8,128)S(1)} %get-tuple-element.71), channel_id=1, source_target_pairs={{0,248},{8,16},{16,8},{24,32},{32,24},{40,48},{48,40},{56,64},{64,... | collective-permute-start | bytes 786440 | tf_op jit(solution)/shard_map/ppermute | solution.py:546
  9.4 0.0 copy-done.1
  9.4 2.3 %shard_map.92 = (f32[2,32,32,256]{3,2,1,0:T(8,128)}, f32[2,16,32,256]{3,2,1,0:T(8,128)}, f32[2,8,32,256]{3,2,1,0:T(8,128)}, f32[2,3,8,128]{3,2,1,0:T(8,128)S(1)}, f32[2,8,128]{2,1,0:T(8,128)S(1)}) custom-call(f32[2]{0:T(128)S(1)} %copy-done.1, f32[2,32,32,256]{3,2,1,0:T(8,128)S(1)} %get-tuple-element.64.d1, f32[2,16,32,256]{3,2,1,0:T(8,128)S(1)} %get-tuple-element.65.d2, ...), custom_call_target="tpu_custom_call" | custom-call | flops 20000000 | bytes 1048576 | tf_op jit(solution)/shard_map/pallas_call | solution.py:555
  11.7 0.0 collective-permute-done.passed
  11.7 0.3 collective-permute-start.1
  12.1 0.0 collective-permute-done.2.inner
  12.1 0.4 shard_map.94
  12.4 1.0 %collective-permute-done.4.outer_b = f32[8,32,256]{2,1,0:T(8,128)S(1)} collective-permute-done((f32[8,32,256]{2,1,0:T(8,128)S(1)}, f32[8,32,256]{2,1,0:T(8,128)S(1)}, u32[]{:S(2)}, u32[]{:S(2)}) %collective-permute-start.4) | collective-permute-done | bytes 262176 | tf_op jit(solution)/shard_map/ppermute | solution.py:551
  13.5 3.1 %collective-permute-done.3.outer_a = f32[8,32,256]{2,1,0:T(8,128)S(1)} collective-permute-done((f32[8,32,256]{2,1,0:T(8,128)S(1)}, f32[8,32,256]{2,1,0:T(8,128)S(1)}, u32[]{:S(2)}, u32[]{:S(2)}) %collective-permute-start.3) | collective-permute-done | bytes 262176 | tf_op jit(solution)/shard_map/ppermute | solution.py:546
  16.6 0.1 shard_map.95.after
  16.6 4.4 %collective-permute-start.5 = (f32[2,2,32,256]{3,2,1,0:T(8,128)S(1)}, f32[2,2,32,256]{3,2,1,0:T(8,128)S(1)}, u32[]{:S(2)}, u32[]{:S(2)}) collective-permute-start(f32[2,2,32,256]{3,2,1,0:T(8,128)S(1)} %shard_map.95.after), channel_id=1, source_target_pairs={{0,8},{8,0},{16,24},{24,16},{32,40},{40,32},{48,56},{56,48},{64,72... | collective-permute-start | bytes 393224 | tf_op jit(solution)/shard_map/ppermute | solution.py:572
  21.0 0.0 copy-start
  21.0 0.8 %shard_map.96 = (f32[2,2,32,256]{3,2,1,0:T(8,128)S(1)}, f32[2,3,32,256]{3,2,1,0:T(8,128)S(1)}, f32[2,3,32,256]{3,2,1,0:T(8,128)S(1)}, f32[2,4,32,256]{3,2,1,0:T(...) custom-call(f32[2,8,128]{2,1,0:T(8,128)S(1)} %get-tuple-element.67.l, ...), custom_call_target="tpu_custom_call", output_to_operand_aliasing={{7}: (13, {}), {8}: (14, {}), {9}: (15, {})} | custom-call | flops 1000000000 | bytes 1048576 | tf_op jit(solution)/shard_map/pallas_call | solution.py:573
  21.8 0.0 collective-permute-done.1.outer5
  21.8 0.2 collective-permute-done.5.relayed
  22.0 0.2 shard_map.97
  22.2 0.1 broadcast_in_dim.3
  22.3 22.7 %all_to_all.5.parts = f32[256,1,128]{2,1,0:T(1,128)S(1)} all-to-all(f32[256,1,128]{2,1,0:T(1,128)S(1)} %broadcast_in_dim.3), channel_id=1, replica_groups=mesh['gz'=32,'xy'=8] {'gz','xy'}, dimensions={0} | all-to-all | bytes 262144 | tf_op jit(solution)/shard_map/all_to_all | solution.py:592
  45.0 0.0 copy-done
  45.0 1.0 %shard_map.98 = (f32[2,32,32,256]{3,2,1,0:T(8,128)}, f32[2,16,32,256]{3,2,1,0:T(8,128)}, f32[2,8,32,256]{3,2,1,0:T(8,128)}, f32[2,4,32,256]{3,2,1,0:T(8,128)}, f...) custom-call(f32[1,128]{1,0:T(1,128)S(1)} %copy-done, ...), custom_call_target="tpu_custom_call", output_to_operand_aliasing={{0}: (8, {}), {1}: (9, {}), {2}: (10, {})} | custom-call | flops 5000000 | bytes 1048576 | tf_op jit(solution)/shard_map/pallas_call | solution.py:595
  (1 shorter events, 0.0 us)
Async XLA Ops:
  3.0 6.4 %copy-start.1 = (f32[2]{0:T(128)S(1)}, f32[2]{0:T(128)}, u32[]{:S(2)}) copy-start(f32[2]{0:T(128)} %limits.1) | copy-start | bytes 28
  4.3 7.8 %collective-permute-start.2 = (f32[2,10,32,256]{3,2,1,0:T(8,128)S(1)}, f32[2,10,32,256]{3,2,1,0:T(8,128)S(1)}, u32[]{:S(2)}, u32[]{:S(2)}) collective-permute-start(f32[2,10,32,256]{3,2,1,0:T(8,128)S(1)} %get-tuple-element.70), channel_id=1, source_target_pairs={{0,8},{8,0},{16,24},{24,16},{32,40},{40,32},{48,56},{56,48},{64,72... | collective-permute-start | bytes 1966088 | tf_op jit(solution)/shard_map/ppermute | solution.py:554
  7.6 4.1 %collective-permute-start = (f32[2,2,32,256]{3,2,1,0:T(8,128)S(1)}, f32[2,2,32,256]{3,2,1,0:T(8,128)S(1)}, u32[]{:S(2)}, u32[]{:S(2)}) collective-permute-start(f32[2,2,32,256]{3,2,1,0:T(8,128)S(1)} %get-tuple-element.69), channel_id=1, source_target_pairs={{0,8},{8,0},{16,24},{24,16},{32,40},{40,32},{48,56},{56,48},{64,72... | collective-permute-start | bytes 393224 | tf_op jit(solution)/shard_map/ppermute | solution.py:550
  7.7 5.8 %collective-permute-start.4 = (f32[8,32,256]{2,1,0:T(8,128)S(1)}, f32[8,32,256]{2,1,0:T(8,128)S(1)}, u32[]{:S(2)}, u32[]{:S(2)}) collective-permute-start(f32[8,32,256]{2,1,0:T(8,128)S(1)} %get-tuple-element.72), channel_id=1, source_target_pairs={{0,248},{8,16},{16,8},{24,32},{32,24},{40,48},{48,40},{56,64},{64,... | collective-permute-start | bytes 786440 | tf_op jit(solution)/shard_map/ppermute | solution.py:551
  7.9 8.7 %collective-permute-start.3 = (f32[8,32,256]{2,1,0:T(8,128)S(1)}, f32[8,32,256]{2,1,0:T(8,128)S(1)}, u32[]{:S(2)}, u32[]{:S(2)}) collective-permute-start(f32[8,32,256]{2,1,0:T(8,128)S(1)} %get-tuple-element.71), channel_id=1, source_target_pairs={{0,248},{8,16},{16,8},{24,32},{32,24},{40,48},{48,40},{56,64},{64,... | collective-permute-start | bytes 786440 | tf_op jit(solution)/shard_map/ppermute | solution.py:546
  11.7 10.1 %collective-permute-start.1 = (f32[2,2,32,256]{3,2,1,0:T(8,128)S(1)}, f32[2,2,32,256]{3,2,1,0:T(8,128)S(1)}, u32[]{:S(2)}, u32[]{:S(2)}) collective-permute-start(f32[2,2,32,256]{3,2,1,0:T(8,128)S(1)} %shard_map.93.after), channel_id=1, source_target_pairs={{0,248},{8,16},{16,8},{24,32},{32,24},{40,48},{48,40},{56,64},{64,... | collective-permute-start | bytes 393224 | tf_op jit(solution)/shard_map/ppermute | solution.py:553
  16.6 5.4 %collective-permute-start.5 = (f32[2,2,32,256]{3,2,1,0:T(8,128)S(1)}, f32[2,2,32,256]{3,2,1,0:T(8,128)S(1)}, u32[]{:S(2)}, u32[]{:S(2)}) collective-permute-start(f32[2,2,32,256]{3,2,1,0:T(8,128)S(1)} %shard_map.95.after), channel_id=1, source_target_pairs={{0,8},{8,0},{16,24},{24,16},{32,40},{40,32},{48,56},{56,48},{64,72... | collective-permute-start | bytes 393224 | tf_op jit(solution)/shard_map/ppermute | solution.py:572
  21.0 24.0 %copy-start = (f32[1,128]{1,0:T(1,128)S(1)}, f32[1,128]{1,0:T(1,128)}, u32[]{:S(2)}) copy-start(f32[1,128]{1,0:T(1,128)} %constant.2.clone.cells) | copy-start | bytes 1540

commit v6 on v5

--- a/solution.py
+++ b/solution.py
@@ -379,7 +379,7 @@
 
 def edges(
     limits, outer_a, outer_b, d1, d2, d3, n4, n5, n6, after, e1, e2, e3, o1_in, o2_in, o3_in,
-    b1, b2, b3, b4, m5, m6, sums, o1, o2, o3, sem,
+    m5, m6, sums, o1, o2, o3, o4, b1, b2, b3, b4, sem,
 ):
     upper, lowest, highest = where_am_i()
     end = jnp.logical_or(lowest, highest)
@@ -408,7 +408,13 @@
                     found.add((f, 3), v)
                 (b4, m5, m6)[i][f, j, rows, cols] = v
 
-        over_tiles(tile)
+        own = [*pieces(((b1, o1), (b2, o2), (b3, o3)), upper_side, sem, 6)]
+        for f in range(2):
+            over_tiles(tile, (f,))
+            done = own[3 * f : 3 * f + 3] + [pltpu.make_async_copy(b4.at[f], o4.at[f], sem.at[12 + f])]
+            for copy in done:
+                copy.start()
+            copies += done
         for (f, l), part in found.parts.items():
             sums[f, l] = part
         for copy in copies:
@@ -466,42 +472,20 @@
     total[...] = row
 
 
-def finish(cells, parts, b1, b2, b3, b4, b5, b6, o1_in, o2_in, o3_in, o1, o2, o3, o4, o5, o6, energy, row_vmem, sem):
-    upper, _, _ = where_am_i()
-    copies = [pltpu.make_async_copy(a, b, sem.at[k]) for k, (a, b) in enumerate(((b4, o4), (b5, o5), (b6, o6)))]
+def finish(cells, parts, b5, b6, o5, o6, energy, row_vmem, sem):
+    copies = [pltpu.make_async_copy(a, b, sem.at[k]) for k, (a, b) in enumerate(((b5, o5), (b6, o6)))]
     for copy in copies:
         copy.start()
-
-    def outer_side(upper_side):
-        return pieces(((b1, o1), (b2, o2), (b3, o3)), upper_side, sem, 4)
-
-    @pl.when(upper)
-    def _():
-        for copy in outer_side(True):
-            copy.start()
-
-    @pl.when(jnp.logical_not(upper))
-    def _():
-        for copy in outer_side(False):
-            copy.start()
-
-    row = jnp.sum(parts[...], axis=0) * (1.0 / cells[...])
+    some = [jnp.sum(parts[k : k + 32], axis=0) for k in range(0, parts.shape[0], 32)]
+    while len(some) > 1:
+        some = [a + b for a, b in zip(some[::2], some[1::2])]
+    row = some[0] * (1.0 / cells[...])
     row_vmem[0:1, :] = row[:, 0:6]
     row_vmem[1:2, :] = row[:, 6:12]
-    copies.append(pltpu.make_async_copy(row_vmem, energy, sem.at[3]))
+    copies.append(pltpu.make_async_copy(row_vmem, energy, sem.at[2]))
     copies[-1].start()
     for copy in copies:
         copy.wait()
-
-    @pl.when(upper)
-    def _():
-        for copy in outer_side(True):
-            copy.wait()
-
-    @pl.when(jnp.logical_not(upper))
-    def _():
-        for copy in outer_side(False):
-            copy.wait()
 
 
 def local(fields, threshold):
@@ -570,14 +554,14 @@
     )(limits, d1, d2, d3, d4, d5, s5, inner, own5, sums_c)
     (relayed,) = call(hand_in, [vmem] * 3, [(vmem, arr(2))], [], 5_000_000, 4)(outer_a, outer_b, sums_a)
     received = lax.ppermute(relayed, "gz", within)
-    b1, b2, b3, b4, m5, m6, sums_b, o1, o2, o3 = call(
+    m5, m6, sums_b, o1, o2, o3, o4 = call(
         edges,
         [vmem] * 13 + [hbm] * 3,
-        [(vmem, arr(n)) for n in (2, 3, 3, 4, 2, 2)] + [(vmem, tiles(4))] + [(hbm, arr(n)) for n in (32, 16, 8)],
-        [pltpu.SemaphoreType.DMA((6,))],
+        [(vmem, arr(2)), (vmem, arr(2)), (vmem, tiles(4))] + [(hbm, arr(n)) for n in (32, 16, 8, 4)],
+        [buf(2), buf(3), buf(3), buf(4), pltpu.SemaphoreType.DMA((14,))],
         1_000_000_000,
         4,
-        {13: 7, 14: 8, 15: 9},
+        {13: 3, 14: 4, 15: 5},
     )(limits, outer_a, outer_b, d1, d2, d3, n4, n5, n6, relayed, e1, e2, e3, o1, o2, o3)
     b5, b6, total = call(
         fifth,
@@ -592,15 +576,14 @@
     parts = lax.all_to_all(jnp.broadcast_to(total, (devices, 1, 128)), ("gz", "xy"), 0, 0, tiled=True)
     cells = np.zeros((1, 128), np.float32) + 1.0
     cells[0, :12] = [n * 32 * 256 * devices for n in (32, 16, 8, 4, 2, 2)] * 2
-    o1, o2, o3, o4, o5, o6, energy = call(
+    o5, o6, energy = call(
         finish,
-        [vmem] * 8 + [hbm] * 3,
-        [(hbm, arr(n)) for n in (32, 16, 8, 4, 2, 2)] + [(hbm, jax.ShapeDtypeStruct((2, 6), f32))],
-        [pltpu.VMEM((2, 6), f32), pltpu.SemaphoreType.DMA((10,))],
+        [vmem] * 4,
+        [(hbm, arr(2)), (hbm, arr(2)), (hbm, jax.ShapeDtypeStruct((2, 6), f32))],
+        [pltpu.VMEM((2, 6), f32), pltpu.SemaphoreType.DMA((3,))],
         5_000_000,
         4,
-        {8: 0, 9: 1, 10: 2},
-    )(cells, parts, b1, b2, b3, b4, b5, b6, o1, o2, o3)
+    )(cells, parts, b5, b6)
     return o1, o2, o3, o4, o5, o6, energy
 
 

time: 46.1 us -> 45.9 us (level)
  transfers between devices with their start and end apart: 6 -> 6, of which waited for: 3 -> 2; matrix products, arithmetic and copies ran while one was open for 0% -> 0% of each run, Pallas kernels for 8% -> 9%
where the time goes in v6:
time: 45.9 us; the launch traced here: 45.8 us
  blocking collectives  22.5 us (49%)
  starting transfers between devices  9.81 us (21%)
  Pallas kernels  8.51 us (19%)
  waiting for transfers between devices  4.12 us (9%)
  between operations  0.72 us (2%)
    all_to_all x1, blocking collectives, local(): lax.all_to_all(jnp.broadcast_to(total, (devices, 1, 128)), ('gz', 'xy'),...  22.5 us
    ppermute x1, starting transfers between devices, local(): received = lax.ppermute(relayed, 'gz', within)  4.37 us
    ppermute x1, starting transfers between devices, local(): inner = lax.ppermute(inner, 'gz', within)  3.29 us
    ppermute x1, waiting for transfers between devices, local(): outer_a = lax.ppermute(outer_a, 'gz', across)  3.1 us
    pallas_call x1, Pallas kernels, local(): call(first_half, [hbm], [(vmem, states), *kept, (vmem, jax.ShapeDtypeStru...  2.34 us
    pallas_call x1, Pallas kernels, local(): call(interiors, [smem] + [vmem] * 3, [(hbm, arr(n)) for n in (32, 16, 8)]...  2.29 us
    ppermute x1, starting transfers between devices, local(): outer_a = lax.ppermute(outer_a, 'gz', across)  1.52 us
    pallas_call x1, Pallas kernels, local(): call(second_half, [vmem] * 10, [(vmem, states), *kept], [], 20000000, 4,...  1.27 us
  transfers between devices with their start and end apart: 6, of which 2 were waited for; matrix products, arithmetic and copies ran while one was open for 0% of the time, Pallas kernels for 9%

profile of v6, /device:TPU:1, one launch (start us, length us, event | category | flops | bytes accessed | tf_op | source)
XLA Modules:
  0.0 45.8 jit_solution(2639481762626125277)
XLA Ops:
  0.6 2.3 %shard_map.90 = (f32[8,32,256]{2,1,0:T(8,128)S(1)}, f32[2,2,32,256]{3,2,1,0:T(8,128)S(1)}, f32[2,2,32,256]{3,2,1,0:T(8,128)S(1)}, f32[2,10,32,256]{3,2,1,0:T(8,1...) custom-call(f32[2,64,32,256]{3,2,1,0:T(8,128)} %x_hbm.1), custom_call_target="tpu_custom_call" | custom-call | flops 20000000 | bytes 1048576 | tf_op jit(solution)/shard_map/pallas_call | solution.py:522
  3.0 0.0 copy-start.1
  3.0 1.3 %shard_map.91 = (f32[8,32,256]{2,1,0:T(8,128)S(1)}, f32[2,2,32,256]{3,2,1,0:T(8,128)S(1)}, f32[2,2,32,256]{3,2,1,0:T(8,128)S(1)}, f32[2,10,32,256]{3,2,1,0:T(8,1...) custom-call(f32[64,32,256]{2,1,0:T(8,128)S(1)} %get-tuple-element.54, ...), custom_call_target="tpu_custom_call", output_to_operand_aliasing={{1}: (1, {}), {2}: (2, {}), {3}: (3, {}), {4}: (4, {}), {5}... | custom-call | flops 20000000 | bytes 1048576 | tf_op jit(solution)/shard_map/pallas_call | solution.py:531
  4.3 3.3 %collective-permute-start.2 = (f32[2,10,32,256]{3,2,1,0:T(8,128)S(1)}, f32[2,10,32,256]{3,2,1,0:T(8,128)S(1)}, u32[]{:S(2)}, u32[]{:S(2)}) collective-permute-start(f32[2,10,32,256]{3,2,1,0:T(8,128)S(1)} %get-tuple-element.73), channel_id=1, source_target_pairs={{0,8},{8,0},{16,24},{24,16},{32,40},{40,32},{48,56},{56,48},{64,72... | collective-permute-start | bytes 1966088 | tf_op jit(solution)/shard_map/ppermute | solution.py:538
  7.6 0.1 collective-permute-start.3
  7.7 0.2 collective-permute-start.1
  7.9 1.5 %collective-permute-start = (f32[8,32,256]{2,1,0:T(8,128)S(1)}, f32[8,32,256]{2,1,0:T(8,128)S(1)}, u32[]{:S(2)}, u32[]{:S(2)}) collective-permute-start(f32[8,32,256]{2,1,0:T(8,128)S(1)} %get-tuple-element.68), channel_id=1, source_target_pairs={{0,248},{8,16},{16,8},{24,32},{32,24},{40,48},{48,40},{56,64},{64,... | collective-permute-start | bytes 786440 | tf_op jit(solution)/shard_map/ppermute | solution.py:530
  9.4 0.0 copy-done.1
  9.4 2.3 %shard_map.92 = (f32[2,32,32,256]{3,2,1,0:T(8,128)}, f32[2,16,32,256]{3,2,1,0:T(8,128)}, f32[2,8,32,256]{3,2,1,0:T(8,128)}, f32[2,3,8,128]{3,2,1,0:T(8,128)S(1)}, f32[2,8,128]{2,1,0:T(8,128)S(1)}) custom-call(f32[2]{0:T(128)S(1)} %copy-done.1, f32[2,32,32,256]{3,2,1,0:T(8,128)S(1)} %get-tuple-element.64.d1, f32[2,16,32,256]{3,2,1,0:T(8,128)S(1)} %get-tuple-element.65.d2, ...), custom_call_target="tpu_custom_call" | custom-call | flops 20000000 | bytes 1048576 | tf_op jit(solution)/shard_map/pallas_call | solution.py:539
  11.7 0.0 collective-permute-done.3.passed
  11.7 0.3 collective-permute-start.4
  12.1 0.0 collective-permute-done.2.inner
  12.1 0.4 shard_map.94
  12.4 1.0 %collective-permute-done.1.outer_b = f32[8,32,256]{2,1,0:T(8,128)S(1)} collective-permute-done((f32[8,32,256]{2,1,0:T(8,128)S(1)}, f32[8,32,256]{2,1,0:T(8,128)S(1)}, u32[]{:S(2)}, u32[]{:S(2)}) %collective-permute-start.1) | collective-permute-done | bytes 262176 | tf_op jit(solution)/shard_map/ppermute | solution.py:535
  13.5 3.1 %collective-permute-done.outer_a = f32[8,32,256]{2,1,0:T(8,128)S(1)} collective-permute-done((f32[8,32,256]{2,1,0:T(8,128)S(1)}, f32[8,32,256]{2,1,0:T(8,128)S(1)}, u32[]{:S(2)}, u32[]{:S(2)}) %collective-permute-start) | collective-permute-done | bytes 262176 | tf_op jit(solution)/shard_map/ppermute | solution.py:530
  16.6 0.1 shard_map.95.after
  16.6 4.4 %collective-permute-start.5 = (f32[2,2,32,256]{3,2,1,0:T(8,128)S(1)}, f32[2,2,32,256]{3,2,1,0:T(8,128)S(1)}, u32[]{:S(2)}, u32[]{:S(2)}) collective-permute-start(f32[2,2,32,256]{3,2,1,0:T(8,128)S(1)} %shard_map.95.after), channel_id=1, source_target_pairs={{0,8},{8,0},{16,24},{24,16},{32,40},{40,32},{48,56},{56,48},{64,72... | collective-permute-start | bytes 393224 | tf_op jit(solution)/shard_map/ppermute | solution.py:556
  21.0 0.0 copy-start
  21.0 1.1 %shard_map.96 = (f32[2,2,32,256]{3,2,1,0:T(8,128)S(1)}, f32[2,2,32,256]{3,2,1,0:T(8,128)S(1)}, f32[2,4,8,128]{3,2,1,0:T(8,128)S(1)}, f32[2,32,32,256]{3,2,1,0:T(...) custom-call(f32[2,8,128]{2,1,0:T(8,128)S(1)} %get-tuple-element.67.l, ...), custom_call_target="tpu_custom_call", output_to_operand_aliasing={{3}: (13, {}), {4}: (14, {}), {5}: (15, {})} | custom-call | flops 1000000000 | bytes 1048576 | tf_op jit(solution)/shard_map/pallas_call | solution.py:557
  22.1 0.0 collective-permute-done.4.outer5
  22.2 0.0 collective-permute-done.5.relayed
  22.2 0.2 shard_map.97
  22.4 0.1 broadcast_in_dim.3
  22.5 22.5 %all_to_all.5.parts = f32[256,1,128]{2,1,0:T(1,128)S(1)} all-to-all(f32[256,1,128]{2,1,0:T(1,128)S(1)} %broadcast_in_dim.3), channel_id=1, replica_groups=mesh['gz'=32,'xy'=8] {'gz','xy'}, dimensions={0} | all-to-all | bytes 262144 | tf_op jit(solution)/shard_map/all_to_all | solution.py:576
  45.0 0.0 copy-done
  45.0 0.8 %shard_map.98 = (f32[2,2,32,256]{3,2,1,0:T(8,128)}, f32[2,2,32,256]{3,2,1,0:T(8,128)}, f32[2,6]{1,0:T(2,128)}) custom-call(f32[1,128]{1,0:T(1,128)S(1)} %copy-done, f32[256,1,128]{2,1,0:T(1,128)S(1)} %all_to_all.5.parts, f32[2,2,32,256]{3,2,1,0:T(8,128)S(1)} %get-tuple-element.96.b5, f32[2,2,32,256]{3,2,1,0:T(8,128)S(1)} %get-tuple-element.97.b6), custom_call_target="tpu_custom_call" | custom-call | flops 5000000 | bytes 1048576 | tf_op jit(solution)/shard_map/pallas_call | solution.py:579
  (1 shorter events, 0.0 us)
Async XLA Ops:
  3.0 6.4 %copy-start.1 = (f32[2]{0:T(128)S(1)}, f32[2]{0:T(128)}, u32[]{:S(2)}) copy-start(f32[2]{0:T(128)} %limits.1) | copy-start | bytes 28
  4.3 7.8 %collective-permute-start.2 = (f32[2,10,32,256]{3,2,1,0:T(8,128)S(1)}, f32[2,10,32,256]{3,2,1,0:T(8,128)S(1)}, u32[]{:S(2)}, u32[]{:S(2)}) collective-permute-start(f32[2,10,32,256]{3,2,1,0:T(8,128)S(1)} %get-tuple-element.73), channel_id=1, source_target_pairs={{0,8},{8,0},{16,24},{24,16},{32,40},{40,32},{48,56},{56,48},{64,72... | collective-permute-start | bytes 1966088 | tf_op jit(solution)/shard_map/ppermute | solution.py:538
  7.6 4.1 %collective-permute-start.3 = (f32[2,2,32,256]{3,2,1,0:T(8,128)S(1)}, f32[2,2,32,256]{3,2,1,0:T(8,128)S(1)}, u32[]{:S(2)}, u32[]{:S(2)}) collective-permute-start(f32[2,2,32,256]{3,2,1,0:T(8,128)S(1)} %get-tuple-element.75), channel_id=1, source_target_pairs={{0,8},{8,0},{16,24},{24,16},{32,40},{40,32},{48,56},{56,48},{64,72... | collective-permute-start | bytes 393224 | tf_op jit(solution)/shard_map/ppermute | solution.py:534
  7.7 5.8 %collective-permute-start.1 = (f32[8,32,256]{2,1,0:T(8,128)S(1)}, f32[8,32,256]{2,1,0:T(8,128)S(1)}, u32[]{:S(2)}, u32[]{:S(2)}) collective-permute-start(f32[8,32,256]{2,1,0:T(8,128)S(1)} %get-tuple-element.69), channel_id=1, source_target_pairs={{0,248},{8,16},{16,8},{24,32},{32,24},{40,48},{48,40},{56,64},{64,... | collective-permute-start | bytes 786440 | tf_op jit(solution)/shard_map/ppermute | solution.py:535
  7.9 8.7 %collective-permute-start = (f32[8,32,256]{2,1,0:T(8,128)S(1)}, f32[8,32,256]{2,1,0:T(8,128)S(1)}, u32[]{:S(2)}, u32[]{:S(2)}) collective-permute-start(f32[8,32,256]{2,1,0:T(8,128)S(1)} %get-tuple-element.68), channel_id=1, source_target_pairs={{0,248},{8,16},{16,8},{24,32},{32,24},{40,48},{48,40},{56,64},{64,... | collective-permute-start | bytes 786440 | tf_op jit(solution)/shard_map/ppermute | solution.py:530
  11.7 10.4 %collective-permute-start.4 = (f32[2,2,32,256]{3,2,1,0:T(8,128)S(1)}, f32[2,2,32,256]{3,2,1,0:T(8,128)S(1)}, u32[]{:S(2)}, u32[]{:S(2)}) collective-permute-start(f32[2,2,32,256]{3,2,1,0:T(8,128)S(1)} %shard_map.93.after), channel_id=1, source_target_pairs={{0,248},{8,16},{16,8},{24,32},{32,24},{40,48},{48,40},{56,64},{64,... | collective-permute-start | bytes 393224 | tf_op jit(solution)/shard_map/ppermute | solution.py:537
  16.6 5.5 %collective-permute-start.5 = (f32[2,2,32,256]{3,2,1,0:T(8,128)S(1)}, f32[2,2,32,256]{3,2,1,0:T(8,128)S(1)}, u32[]{:S(2)}, u32[]{:S(2)}) collective-permute-start(f32[2,2,32,256]{3,2,1,0:T(8,128)S(1)} %shard_map.95.after), channel_id=1, source_target_pairs={{0,8},{8,0},{16,24},{24,16},{32,40},{40,32},{48,56},{56,48},{64,72... | collective-permute-start | bytes 393224 | tf_op jit(solution)/shard_map/ppermute | solution.py:556
  21.0 24.0 %copy-start = (f32[1,128]{1,0:T(1,128)S(1)}, f32[1,128]{1,0:T(1,128)}, u32[]{:S(2)}) copy-start(f32[1,128]{1,0:T(1,128)} %constant.2.clone.cells) | copy-start | bytes 1540
